TPU v7x, 32 devices: a whole 2x2x4 slice. The times are simulated.
32 devices in a mesh: slab: 8 (over y, x, core), trace: 4 (over z).
Axes of the slice: x: 2, y: 2, z: 4, core: 2. Of those that a mesh axis runs over, the one named last changes fastest.
Arguments:
- transmission: bfloat16 [8, 2048, 2048], P('slab', None, 'trace'), may hold values from -0.125 to 0.125
- reflection: bfloat16 [8, 2048, 2048], P('slab', None, 'trace'), may hold values from -0.0625 to 0.0625
- response: bfloat16 [8, 2048, 2048], P('slab', None, 'trace'), may hold values from -0.125 to 0.125
- sources: bfloat16 [8, 8, 32, 2048], P('slab', None, None, 'trace'), may hold values from -6 to 6
- placement: int32 [8, 32], replicated, may hold values from 0 to 7
Outputs:
- field_trace: bfloat16 [8, 8, 32, 2048], P('slab', None, None, 'trace')
All inputs are finite; a program needn't handle non-finite values.
Results may differ from a plain program's by a relative error of at most 0.018.
Values may be sent and summed in bfloat16 or wider, within the bound.
No kernel may reach another device: no remote copies, remote signals or barrier semaphores. Data moves between devices by JAX's collectives and lax.ppermute only.
A program may use at most 64 MiB of HBM per device.

v0:
```python
import functools

import jax
import jax.numpy as jnp
from jax import lax
from jax.experimental import pallas as pl
from jax.experimental.pallas import tpu as pltpu
from jax.sharding import PartitionSpec as P


AXES = ("slab", "trace")
CHUNKS = 2


class Places:
    def __init__(self, slab_count, trace_count):
        self.columns = slab_count // 2
        self.width = trace_count
        self.holders = (trace_count // 2 - 1, trace_count // 2)
        self.extra = trace_count // 2 - 1

    def at(self, column, core, z):
        return (2 * column + core) * self.width + z

    def everyone(self):
        return [(c, k, z) for c in range(self.columns) for k in (0, 1) for z in range(self.width)]

    def working(self, stage):
        return ((stage, 0), (self.columns - 1 - stage, 1))

    def partner_map(self):
        return {self.at(c, k, z): self.at(c, 1 - k, z) for c, k, z in self.everyone()}

    def across_cores(self):
        return list(self.partner_map().items())

    def swap(self, stage):
        moves = self.partner_map()
        (ca, ka), (cb, kb) = self.working(stage)
        low, high = self.holders
        for z, other in ((low, high), (high, low)):
            for c, k in ((ca, ka), (cb, kb)):
                moves[self.at(c, k, z)] = self.at(c, k, other)
            if ca != cb:
                moves[self.at(ca, 1 - ka, z)] = self.at(cb, 1 - kb, z)
                moves[self.at(cb, 1 - kb, z)] = self.at(ca, 1 - ka, z)
        return list(moves.items())

    def swap_all(self):
        moves = self.partner_map()
        low, high = self.holders
        for c in range(self.columns):
            for k in (0, 1):
                moves[self.at(c, k, low)] = self.at(c, k, high)
                moves[self.at(c, k, high)] = self.at(c, k, low)
        return list(moves.items())

    def hop(self, stage, crossed):
        moves = self.partner_map()
        low, high = self.holders
        for z, other in ((low, high), (high, low)):
            for (before, k), (after, _) in zip(self.working(stage - 1), self.working(stage)):
                moves[self.at(before, k, z)] = self.at(after, k, other if crossed else z)
                if 2 * stage != self.columns:
                    moves[self.at(after, 1 - k, z)] = self.at(before, 1 - k, z)
        return list(moves.items())

    def ends(self, hop):
        low, high = self.holders
        return ((low - hop, low), (high + hop, high))

    def exchange_end(self, hop):
        moves = []
        for c in range(self.columns):
            for k in (0, 1):
                for end, holder in self.ends(hop):
                    moves += [(self.at(c, k, end), self.at(c, k, holder)), (self.at(c, k, holder), self.at(c, k, end))]
        return moves

    def inward(self, hop):
        return [
            (self.at(c, k, end), self.at(c, k, holder))
            for c in range(self.columns) for k in (0, 1) for end, holder in self.ends(hop)
        ]

    def first_sender(self, column):
        if column < self.columns // 2:
            return 1 if column == 0 else 0
        return 1 - self.first_sender(self.columns - 1 - column)

    def inward_crossed(self, hop, early):
        moves = []
        for c in range(self.columns):
            k = self.first_sender(c) if early else 1 - self.first_sender(c)
            for end, holder in self.ends(hop):
                moves.append((self.at(c, k, end), self.at(c, 1 - k, holder)))
        return moves


def move(values, pairs):
    return lax.ppermute(values, AXES, pairs)


def after(values, earlier):
    return lax.optimization_barrier((values, earlier))[0]


def joined(pieces):
    return pieces if len(pieces) < 2 else [jnp.concatenate(pieces, 1)]


def dot32(rows, matrix):
    return jnp.dot(rows, matrix, preferred_element_type=jnp.float32)


def apply_kernel(width, own_ref, other_ref, near_ref, far_ref, add_ref, out_ref, near_tiles, far_tiles, sems):
    depth = near_ref.shape[0] // width
    half = width // 2
    lower = lax.axis_index("trace") < half
    down = [half - 1 - i for i in range(half)]
    up = [half + i for i in range(half)]
    blocks = [jnp.where(lower, x, y) for x, y in zip(down + up, up + down)]
    copies = []
    for t, block in enumerate(blocks):
        rows = pl.ds(pl.multiple_of(block * depth, depth), depth)
        pair = (
            pltpu.make_async_copy(near_ref.at[rows, :], near_tiles.at[t], sems.at[0, t]),
            pltpu.make_async_copy(far_ref.at[rows, :], far_tiles.at[t], sems.at[1, t]),
        )
        for copy in pair:
            copy.start()
        copies.append(pair)
    near = far = 0.0
    for t, pair in enumerate(copies):
        source = own_ref if t < half else other_ref
        rows = source[:, (t % half) * depth:(t % half + 1) * depth]
        for copy in pair:
            copy.wait()
        near += jnp.dot(rows, near_tiles[t], preferred_element_type=jnp.float32)
        far += jnp.dot(rows, far_tiles[t], preferred_element_type=jnp.float32)
    cut = near_ref.shape[1]
    out_ref[:, :cut] = (near + add_ref[:, :cut]).astype(out_ref.dtype)
    out_ref[:, cut:] = (far + add_ref[:, cut:]).astype(out_ref.dtype)


def applied(own, other, pieces, addend):
    near, far = pieces
    width = lax.axis_size("trace")
    rows, columns = addend.shape
    depth = near.shape[0] // width
    vmem = pl.BlockSpec(memory_space=pltpu.VMEM)
    hbm = pl.BlockSpec(memory_space=pltpu.HBM)
    return pl.pallas_call(
        functools.partial(apply_kernel, width),
        out_shape=jax.ShapeDtypeStruct((rows, columns), jnp.bfloat16),
        in_specs=[vmem, vmem, hbm, hbm, vmem],
        out_specs=vmem,
        scratch_shapes=[
            pltpu.VMEM((width, depth, near.shape[1]), near.dtype),
            pltpu.VMEM((width, depth, far.shape[1]), far.dtype),
            pltpu.SemaphoreType.DMA((2, width)),
        ],
        compiler_params=pltpu.CompilerParams(vmem_limit_bytes=16 * 1024 * 1024),
        cost_estimate=pl.CostEstimate(
            flops=2 * rows * columns * near.shape[0], bytes_accessed=2 * columns * near.shape[0], transcendentals=0
        ),
    )(own, other, near, far, addend)


def in_turn(rows, pieces, addends, last):
    results = []
    for (own, other), addend in zip(rows, addends):
        last = applied(after(own, last), other, pieces, addend)
        results.append(last)
    return results


def shards(transmission, reflection, response, sources, placement):
    own_sources = sources[0]
    tick_count, batch_count, trace_width = own_sources.shape
    total_rows = tick_count * batch_count
    slab_index = lax.axis_index("slab")
    z = lax.axis_index("trace")
    trace_count = lax.axis_size("trace")
    places = Places(lax.axis_size("slab"), trace_count)
    core = slab_index % 2
    column = slab_index // 2
    my_stage = jnp.where(core == 0, column, places.columns - 1 - column)
    hops = range(1, places.extra + 1)

    distance = jnp.abs(slab_index - placement).astype(jnp.float32)
    weighting = 1.0 / (1.0 + distance)
    weighted = (own_sources.astype(jnp.float32) * weighting[:, :, None]).astype(jnp.bfloat16)
    flat = weighted.reshape(total_rows, trace_width)

    gathered = [flat]
    for k in range(1, trace_count):
        gathered.append(lax.ppermute(flat, "trace", [(i, (i + k) % trace_count) for i in range(trace_count)]))
    respond = response[0]
    driven = jnp.zeros((total_rows, trace_width), jnp.float32)
    for k, rows in enumerate(gathered):
        block = lax.rem(z - k + trace_count, trace_count)
        driven = driven + dot32(rows, lax.dynamic_slice_in_dim(respond, block * trace_width, trace_width, 0))

    transfer = transmission[0]
    reflect = reflection[0]
    second_own = move(transfer, places.across_cores())
    second_early = joined([move(transfer, places.inward_crossed(hop, True)) for hop in hops])

    driven_sent = driven.astype(jnp.bfloat16)
    first_driven = jnp.concatenate(
        [driven_sent] + [move(driven_sent, places.exchange_end(hop)) for hop in hops], 1
    )
    late_source = after(transfer, first_driven)
    second_late = joined([move(late_source, places.inward_crossed(hop, False)) for hop in hops])

    step = total_rows // CHUNKS

    def split(values):
        return [values[i * step:(i + 1) * step] for i in range(CHUNKS)]

    firsts, seconds = [], []

    def chosen(stages, part):
        result = stages[0][part]
        for stage in range(1, places.columns):
            result = jnp.where(my_stage == stage, stages[stage][part], result)
        return result

    first_parts = split(first_driven)
    second_parts = split(move(first_driven, places.across_cores()))
    traces = first_parts
    for stage in range(places.columns):
        early = places.first_sender(stage) == 0
        second_pieces = [second_own] + (second_late if early else second_early)
        if stage:
            first_pieces = [transfer] + (first_early if early else first_late)
            arrived = []
            for part in traces:
                crossed = move(part, places.hop(stage, True))
                arrived.append((move(part, places.hop(stage, False)), crossed))
            traces = in_turn(arrived, first_pieces, first_parts, traces[-1])
        firsts.append(traces)
        others = []
        for part in traces:
            others.append(move(part, places.swap(stage)))
        traces = in_turn(list(zip(traces, others)), second_pieces, second_parts, traces[-1])
        seconds.append(traces)
        if stage == 0:
            first_early = [move(after(piece, traces[-1]), places.across_cores()) for piece in second_early]
        if stage == min(1, places.columns - 1):
            first_late = [move(after(piece, traces[-1]), places.across_cores()) for piece in second_late]
            reflect_source = after(reflect, traces[-1])
            reflect_rest = joined([move(reflect_source, places.inward(hop)) for hop in hops])

    outs = []
    for part in range(CHUNKS):
        mine = chosen(firsts, part).astype(jnp.float32)
        opposite = move(chosen(seconds, part), places.across_cores()).astype(jnp.float32)
        contrast = jnp.where(core == 0, mine - opposite, opposite - mine).astype(jnp.bfloat16)
        other = move(contrast, places.swap_all())
        combined = applied(contrast, other, [reflect] + reflect_rest, mine + opposite)
        own = combined[:, :trace_width]
        for hop in hops:
            piece = move(combined[:, hop * trace_width:(hop + 1) * trace_width], places.exchange_end(hop))
            own = jnp.where((z == places.ends(hop)[0][0]) | (z == places.ends(hop)[1][0]), piece, own)
        outs.append(own)
    return jnp.concatenate(outs, 0).reshape(1, tick_count, batch_count, trace_width)


def solution(mesh):
    placed = (
        P("slab", None, "trace"),
        P("slab", None, "trace"),
        P("slab", None, "trace"),
        P("slab", None, None, "trace"),
        P(),
    )

    return jax.shard_map(
        shards,
        mesh=mesh,
        in_specs=placed,
        out_specs=P("slab", None, None, "trace"),
        check_vma=False,
    )
```

profile of v0, /device:TPU:0, one launch (start us, length us, event | category | flops | bytes accessed | tf_op | source)
XLA Modules:
  0.0 182.5 jit_solution(12054988003648932728)
XLA Ops:
  0.0 0.8 add_divide_fusion
  0.9 1.8 fusion.10
  2.7 3.1 %collective-permute-start = (bf16[256,512]{1,0:T(8,128)(2,1)}, bf16[256,512]{1,0:T(8,128)(2,1)}, u32[]{:S(2)}, u32[]{:S(2)}) collective-permute-start(bf16[256,512]{1,0:T(8,128)(2,1)} %fusion.10), channel_id=1, source_target_pairs={{0,1},{1,2},{2,3},{3,0},{4,5},{5,6},{6,7},{7,4},{8,9},{9,10},{10,1... | collective-permute-start | bytes 786440 | tf_op jit(solution)/shard_map/ppermute | solution.py:198
  5.7 2.0 %collective-permute-start.2 = (bf16[256,512]{1,0:T(8,128)(2,1)}, bf16[256,512]{1,0:T(8,128)(2,1)S(1)}, u32[]{:S(2)}, u32[]{:S(2)}) collective-permute-start(bf16[256,512]{1,0:T(8,128)(2,1)} %fusion.10), channel_id=1, source_target_pairs={{0,3},{1,0},{2,1},{3,2},{4,7},{5,4},{6,5},{7,6},{8,11},{9,8},{10,9... | collective-permute-start | bytes 786440 | tf_op jit(solution)/shard_map/ppermute | solution.py:198
  7.8 1.0 collective-permute-start.1
  8.8 2.0 %collective-permute-start.6 = (bf16[2048,512]{1,0:T(8,128)(2,1)}, bf16[2048,512]{1,0:T(8,128)(2,1)}, u32[]{:S(2)}, u32[]{:S(2)}) collective-permute-start(bf16[2048,512]{1,0:T(8,128)(2,1)} %bitcast.25), channel_id=1, source_target_pairs={{4,1},{7,2},{8,13},{11,14},{20,17},{23,18},{24,29},{27,30}} | collective-permute-start | bytes 6291464 | tf_op jit(solution)/shard_map/ppermute | solution.py:101
  10.8 1.1 multiply_convert_fusion
  11.9 0.3 fusion.11
  12.2 7.1 %collective-permute-done.2 = bf16[256,512]{1,0:T(8,128)(2,1)S(1)} collective-permute-done((bf16[256,512]{1,0:T(8,128)(2,1)}, bf16[256,512]{1,0:T(8,128)(2,1)S(1)}, u32[]{:S(2)}, u32[]{:S(2)}) %collective-permute-start.2) | collective-permute-done | bytes 262176 | tf_op jit(solution)/shard_map/ppermute | solution.py:198
  19.3 0.3 fusion.6
  19.7 1.3 convolution_add_fusion.1
  20.9 10.2 %collective-permute-done.1 = bf16[256,512]{1,0:T(8,128)(2,1)S(1)} collective-permute-done((bf16[256,512]{1,0:T(8,128)(2,1)}, bf16[256,512]{1,0:T(8,128)(2,1)S(1)}, u32[]{:S(2)}, u32[]{:S(2)}) %collective-permute-start.1) | collective-permute-done | bytes 262176 | tf_op jit(solution)/shard_map/ppermute | solution.py:198
  31.1 0.3 fusion.1
  31.5 8.2 %collective-permute-done.3 = bf16[256,512]{1,0:T(8,128)(2,1)S(1)} collective-permute-done((bf16[256,512]{1,0:T(8,128)(2,1)S(1)}, bf16[256,512]{1,0:T(8,128)(2,1)S(1)}, u32[]{:S(2)}, u32[]{:S(2)}) %collective-permute-start.3) | collective-permute-done | bytes 262176 | tf_op jit(solution)/shard_map/ppermute | solution.py:101
  39.8 11.3 %collective-permute-start.7 = (bf16[256,1024]{1,0:T(8,128)(2,1)S(1)}, bf16[256,1024]{1,0:T(8,128)(2,1)S(1)}, u32[]{:S(2)}, u32[]{:S(2)}) collective-permute-start(bf16[256,1024]{1,0:T(8,128)(2,1)S(1)} %pad_maximum_fusion), channel_id=1, source_target_pairs={{0,4},{1,5},{2,6},{3,7},{4,0},{5,1},{6,2},{7,3},{8,12},{9,13},{10,... | collective-permute-start | bytes 1572872 | tf_op jit(solution)/shard_map/ppermute | solution.py:101
  51.3 0.5 collective-permute-start.9
  51.8 0.9 collective-permute-done.7
  52.7 0.3 collective-permute-done.4.other_ref
  53.1 2.5 %shard_map.55 = bf16[128,1024]{1,0:T(8,128)(2,1)S(1)} custom-call(bf16[128,1024]{1,0:T(8,128)(2,1)S(1)} %get-tuple-element.47.add_ref, bf16[128,1024]{1,0:T(8,128)(2,1)S(1)} %collective-permute-done.4.other_ref, bf16[2048,512]{1,0:T(8,128)(2,1)} %collective-permute-done.5.near_ref, bf16[2048,512]{1,0:T(8,128)(2,1)} %collective-permute-done.6.far_ref, ...), custom_call_target="tpu_custom_call" | custom-call | flops 536870912 | bytes 4194304 | tf_op jit(solution)/shard_map/pallas_call | solution.py:153
  55.6 2.7 %shard_map.56 = bf16[128,1024]{1,0:T(8,128)(2,1)S(1)} custom-call(bf16[128,1024]{1,0:T(8,128)(2,1)S(1)} %get-tuple-element.24.own_ref.add_ref, bf16[128,1024]{1,0:T(8,128)(2,1)S(1)} %collective-permute-done.9.other_ref, bf16[2048,512]{1,0:T(8,128)(2,1)} %collective-permute-done.5.near_ref, bf16[2048,512]{1,0:T(8,128)(2,1)} %collective-permute-done.6.far_ref, ...), custom_call_target="tpu_custom_call" | custom-call | flops 536870912 | bytes 4194304 | tf_op jit(solution)/shard_map/pallas_call | solution.py:153
  58.3 0.4 collective-permute-start.11
  58.8 8.8 %collective-permute-start.15 = (bf16[2048,512]{1,0:T(8,128)(2,1)S(1)}, bf16[2048,512]{1,0:T(8,128)(2,1)S(1)}, u32[]{:S(2)}, u32[]{:S(2)}) collective-permute-start(bf16[2048,512]{1,0:T(8,128)(2,1)S(1)} %bitcast.26), channel_id=1, source_target_pairs={{0,5},{3,6},{12,9},{15,10},{16,21},{19,22},{28,25},{31,26}} | collective-permute-start | bytes 6291464 | tf_op jit(solution)/shard_map/ppermute | solution.py:101
  67.6 0.5 collective-permute-start.10
  68.2 0.9 collective-permute-done.8.own_ref
  69.3 0.2 collective-permute-done.10.other_ref
  69.5 1.3 shard_map.57.own_ref
  70.9 0.2 collective-permute-start.14
  71.1 1.3 shard_map.58.own_ref
  72.4 0.4 collective-permute-start.17
  72.8 18.1 %collective-permute-done.15.far_ref = bf16[2048,512]{1,0:T(8,128)(2,1)S(1)} collective-permute-done((bf16[2048,512]{1,0:T(8,128)(2,1)S(1)}, bf16[2048,512]{1,0:T(8,128)(2,1)S(1)}, u32[]{:S(2)}, u32[]{:S(2)}) %collective-permute-start.15) | collective-permute-done | bytes 2097184 | tf_op jit(solution)/shard_map/ppermute | solution.py:101
  91.0 2.9 %shard_map.59 = bf16[128,1024]{1,0:T(8,128)(2,1)S(1)} custom-call(bf16[128,1024]{1,0:T(8,128)(2,1)S(1)} %shard_map.57.own_ref, bf16[128,1024]{1,0:T(8,128)(2,1)S(1)} %collective-permute-done.14.other_ref, bf16[2048,512]{1,0:T(8,128)(2,1)} %collective-permute-done.5.near_ref, bf16[2048,512]{1,0:T(8,128)(2,1)S(1)} %collective-permute-done.15.far_ref, ...), custom_call_target="tpu_custom_call" | custom-call | flops 536870912 | bytes 4194304 | tf_op jit(solution)/shard_map/pallas_call | solution.py:153
  93.9 2.2 %shard_map.60 = bf16[128,1024]{1,0:T(8,128)(2,1)S(1)} custom-call(bf16[128,1024]{1,0:T(8,128)(2,1)S(1)} %shard_map.58.own_ref, bf16[128,1024]{1,0:T(8,128)(2,1)S(1)} %collective-permute-done.17.other_ref, bf16[2048,512]{1,0:T(8,128)(2,1)} %collective-permute-done.5.near_ref, bf16[2048,512]{1,0:T(8,128)(2,1)S(1)} %collective-permute-done.15.far_ref, ...), custom_call_target="tpu_custom_call" | custom-call | flops 536870912 | bytes 4194304 | tf_op jit(solution)/shard_map/pallas_call | solution.py:153
  96.2 0.5 collective-permute-start.16
  96.8 0.4 collective-permute-start.20
  97.3 3.4 %collective-permute-done.16.own_ref = bf16[128,1024]{1,0:T(8,128)(2,1)S(1)} collective-permute-done((bf16[128,1024]{1,0:T(8,128)(2,1)S(1)}, bf16[128,1024]{1,0:T(8,128)(2,1)S(1)}, u32[]{:S(2)}, u32[]{:S(2)}) %collective-permute-start.16) | collective-permute-done | bytes 262176 | tf_op jit(solution)/shard_map/ppermute | solution.py:101
  100.7 0.4 collective-permute-done.18.other_ref
  101.1 1.3 shard_map.61.own_ref
  102.5 0.2 collective-permute-start.22
  102.7 1.3 shard_map.62.own_ref
  104.0 0.4 collective-permute-start.24
  104.4 2.5 %shard_map.63 = bf16[128,1024]{1,0:T(8,128)(2,1)S(1)} custom-call(bf16[128,1024]{1,0:T(8,128)(2,1)S(1)} %shard_map.61.own_ref, bf16[128,1024]{1,0:T(8,128)(2,1)S(1)} %collective-permute-done.22.other_ref, bf16[2048,512]{1,0:T(8,128)(2,1)} %collective-permute-done.5.near_ref, bf16[2048,512]{1,0:T(8,128)(2,1)} %collective-permute-done.6.far_ref, ...), custom_call_target="tpu_custom_call" | custom-call | flops 536870912 | bytes 4194304 | tf_op jit(solution)/shard_map/pallas_call | solution.py:153
  107.2 0.4 collective-permute-start.25
  107.6 3.2 %shard_map.64 = bf16[128,1024]{1,0:T(8,128)(2,1)} custom-call(bf16[128,1024]{1,0:T(8,128)(2,1)S(1)} %shard_map.62.own_ref, bf16[128,1024]{1,0:T(8,128)(2,1)S(1)} %collective-permute-done.24.other_ref, bf16[2048,512]{1,0:T(8,128)(2,1)} %collective-permute-done.5.near_ref, bf16[2048,512]{1,0:T(8,128)(2,1)} %collective-permute-done.6.far_ref, ...), custom_call_target="tpu_custom_call" | custom-call | flops 536870912 | bytes 4194304 | tf_op jit(solution)/shard_map/pallas_call | solution.py:153
  110.8 0.2 collective-permute-start.26
  111.0 13.0 %collective-permute-start.31 = (bf16[2048,512]{1,0:T(8,128)(2,1)}, bf16[2048,512]{1,0:T(8,128)(2,1)}, u32[]{:S(2)}, u32[]{:S(2)}) collective-permute-start(bf16[2048,512]{1,0:T(8,128)(2,1)} %bitcast.7.near_ref), channel_id=1, source_target_pairs={{0,1},{3,2},{4,5},{7,6},{8,9},{11,10},{12,13},{15,14},{16,17},{19,... | collective-permute-start | bytes 6291464 | tf_op jit(solution)/shard_map/ppermute | solution.py:101
  124.1 2.0 %shard_map.65.own_ref = bf16[128,1024]{1,0:T(8,128)(2,1)} custom-call(bf16[128,1024]{1,0:T(8,128)(2,1)S(1)} %collective-permute-done.23.own_ref, bf16[128,1024]{1,0:T(8,128)(2,1)S(1)} %collective-permute-done.25.other_ref, bf16[2048,512]{1,0:T(8,128)(2,1)S(1)} %bitcast.31, bf16[2048,512]{1,0:T(8,128)(2,1)S(1)} %collective-permute-done.11.far_ref, ...), custom_call_target="tpu_custom_call" | custom-call | flops 536870912 | bytes 4194304 | tf_op jit(solution)/shard_map/pallas_call | solution.py:153
  126.1 0.5 collective-permute-start.28
  126.6 1.6 copy-done.2
  128.2 1.6 copy-done.6
  129.8 2.5 %shard_map.66.own_ref = bf16[128,1024]{1,0:T(8,128)(2,1)S(1)} custom-call(bf16[128,1024]{1,0:T(8,128)(2,1)} %collective-permute-done.26.own_ref, bf16[128,1024]{1,0:T(8,128)(2,1)} %collective-permute-done.27.other_ref, bf16[2048,512]{1,0:T(8,128)(2,1)S(1)} %bitcast.32, bf16[2048,512]{1,0:T(8,128)(2,1)S(1)} %copy-done.6, ...), custom_call_target="tpu_custom_call" | custom-call | flops 536870912 | bytes 4194304 | tf_op jit(solution)/shard_map/pallas_call | solution.py:153
  132.5 3.2 %shard_map.67 = bf16[128,1024]{1,0:T(8,128)(2,1)S(1)} custom-call(bf16[128,1024]{1,0:T(8,128)(2,1)} %shard_map.65.own_ref, bf16[128,1024]{1,0:T(8,128)(2,1)} %collective-permute-done.28.other_ref, bf16[2048,512]{1,0:T(8,128)(2,1)} %collective-permute-done.5.near_ref, bf16[2048,512]{1,0:T(8,128)(2,1)S(1)} %copy-done.4, ...), custom_call_target="tpu_custom_call" | custom-call | flops 536870912 | bytes 4194304 | tf_op jit(solution)/shard_map/pallas_call | solution.py:153
  135.8 0.4 collective-permute-start.29
  136.3 2.1 %shard_map.69 = bf16[128,1024]{1,0:T(8,128)(2,1)S(1)} custom-call(bf16[128,1024]{1,0:T(8,128)(2,1)S(1)} %shard_map.66.own_ref, bf16[128,1024]{1,0:T(8,128)(2,1)S(1)} %collective-permute-done.33.other_ref, bf16[2048,512]{1,0:T(8,128)(2,1)} %collective-permute-done.5.near_ref, bf16[2048,512]{1,0:T(8,128)(2,1)S(1)} %copy-done.4, ...), custom_call_target="tpu_custom_call" | custom-call | flops 536870912 | bytes 4194304 | tf_op jit(solution)/shard_map/pallas_call | solution.py:153
  138.5 0.3 collective-permute-start.34
  139.0 1.3 collective-permute-start.30
  140.3 0.9 convert_add_fusion
  141.4 26.9 %collective-permute-done.31.far_ref = bf16[2048,512]{1,0:T(8,128)(2,1)} collective-permute-done((bf16[2048,512]{1,0:T(8,128)(2,1)}, bf16[2048,512]{1,0:T(8,128)(2,1)}, u32[]{:S(2)}, u32[]{:S(2)}) %collective-permute-start.31) | collective-permute-done | bytes 2097184 | tf_op jit(solution)/shard_map/ppermute | solution.py:101
  168.4 2.6 %shard_map.68 = bf16[128,1024]{1,0:T(8,128)(2,1)S(1)} custom-call(bf16[128,1024]{1,0:T(8,128)(2,1)S(1)} %fusion.3.own_ref, bf16[128,1024]{1,0:T(8,128)(2,1)S(1)} %collective-permute-done.30.other_ref, bf16[2048,512]{1,0:T(8,128)(2,1)} %bitcast.7.near_ref, bf16[2048,512]{1,0:T(8,128)(2,1)} %collective-permute-done.31.far_ref, ...), custom_call_target="tpu_custom_call" | custom-call | flops 536870912 | bytes 4194304 | tf_op jit(solution)/shard_map/pallas_call | solution.py:153
  171.0 0.7 slice.38
  171.6 2.5 %collective-permute-start.32 = (bf16[128,512]{1,0:T(8,128)(2,1)}, bf16[128,512]{1,0:T(8,128)(2,1)S(1)}, u32[]{:S(2)}, u32[]{:S(2)}) collective-permute-start(bf16[128,512]{1,0:T(8,128)(2,1)} %slice.38), channel_id=1, source_target_pairs={{0,1},{1,0},{3,2},{2,3},{4,5},{5,4},{7,6},{6,7},{8,9},{9,8},{11,10... | collective-permute-start | bytes 393224 | tf_op jit(solution)/shard_map/ppermute | solution.py:101
  174.1 2.5 %shard_map.70 = bf16[128,1024]{1,0:T(8,128)(2,1)S(1)} custom-call(bf16[128,1024]{1,0:T(8,128)(2,1)S(1)} %fusion.5.own_ref, bf16[128,1024]{1,0:T(8,128)(2,1)S(1)} %collective-permute-done.35.other_ref, bf16[2048,512]{1,0:T(8,128)(2,1)} %bitcast.7.near_ref, bf16[2048,512]{1,0:T(8,128)(2,1)} %collective-permute-done.31.far_ref, f32[128,1024]{1,0:T(8,128)S(1)} %copy-done.13), custom_call_target="tpu_custom_call" | custom-call | flops 536870912 | bytes 4194304 | tf_op jit(solution)/shard_map/pallas_call | solution.py:153
  176.8 0.8 collective-permute-done.32
  177.5 4.2 %collective-permute-done.36 = bf16[128,512]{1,0:T(8,128)(2,1)S(1)} collective-permute-done((bf16[128,512]{1,0:T(8,128)(2,1)S(1)}, bf16[128,512]{1,0:T(8,128)(2,1)S(1)}, u32[]{:S(2)}, u32[]{:S(2)}) %collective-permute-start.36) | collective-permute-done | bytes 131104 | tf_op jit(solution)/shard_map/ppermute | solution.py:101
  181.7 0.7 pad_maximum_fusion.1
  (96 shorter events, 2.1 us)
Async XLA Ops:
  0.0 11.9 %copy-start = (bf16[1,2048,512]{2,1,0:T(8,128)(2,1)S(1)}, bf16[1,2048,512]{2,1,0:T(8,128)(2,1)}, u32[]{:S(2)}) copy-start(bf16[1,2048,512]{2,1,0:T(8,128)(2,1)} %param.7) | copy-start | bytes 6291460
  2.7 16.9 %collective-permute-start = (bf16[256,512]{1,0:T(8,128)(2,1)}, bf16[256,512]{1,0:T(8,128)(2,1)}, u32[]{:S(2)}, u32[]{:S(2)}) collective-permute-start(bf16[256,512]{1,0:T(8,128)(2,1)} %fusion.10), channel_id=1, source_target_pairs={{0,1},{1,2},{2,3},{3,0},{4,5},{5,6},{6,7},{7,4},{8,9},{9,10},{10,1... | collective-permute-start | bytes 786440 | tf_op jit(solution)/shard_map/ppermute | solution.py:198
  5.7 13.6 %collective-permute-start.2 = (bf16[256,512]{1,0:T(8,128)(2,1)}, bf16[256,512]{1,0:T(8,128)(2,1)S(1)}, u32[]{:S(2)}, u32[]{:S(2)}) collective-permute-start(bf16[256,512]{1,0:T(8,128)(2,1)} %fusion.10), channel_id=1, source_target_pairs={{0,3},{1,0},{2,1},{3,2},{4,7},{5,4},{6,5},{7,6},{8,11},{9,8},{10,9... | collective-permute-start | bytes 786440 | tf_op jit(solution)/shard_map/ppermute | solution.py:198
  7.8 23.4 %collective-permute-start.1 = (bf16[256,512]{1,0:T(8,128)(2,1)}, bf16[256,512]{1,0:T(8,128)(2,1)S(1)}, u32[]{:S(2)}, u32[]{:S(2)}) collective-permute-start(bf16[256,512]{1,0:T(8,128)(2,1)} %fusion.10), channel_id=1, source_target_pairs={{0,2},{1,3},{2,0},{3,1},{4,6},{5,7},{6,4},{7,5},{8,10},{9,11},{10,... | collective-permute-start | bytes 786440 | tf_op jit(solution)/shard_map/ppermute | solution.py:198
  8.8 44.3 %collective-permute-start.5 = (bf16[2048,512]{1,0:T(8,128)(2,1)}, bf16[2048,512]{1,0:T(8,128)(2,1)}, u32[]{:S(2)}, u32[]{:S(2)}) collective-permute-start(bf16[2048,512]{1,0:T(8,128)(2,1)} %bitcast.24), channel_id=1, source_target_pairs={{0,4},{1,5},{2,6},{3,7},{4,0},{5,1},{6,2},{7,3},{8,12},{9,13},{10,... | collective-permute-start | bytes 6291464 | tf_op jit(solution)/shard_map/ppermute | solution.py:101
  8.8 44.3 %collective-permute-start.6 = (bf16[2048,512]{1,0:T(8,128)(2,1)}, bf16[2048,512]{1,0:T(8,128)(2,1)}, u32[]{:S(2)}, u32[]{:S(2)}) collective-permute-start(bf16[2048,512]{1,0:T(8,128)(2,1)} %bitcast.25), channel_id=1, source_target_pairs={{4,1},{7,2},{8,13},{11,14},{20,17},{23,18},{24,29},{27,30}} | collective-permute-start | bytes 6291464 | tf_op jit(solution)/shard_map/ppermute | solution.py:101
  31.4 8.3 %collective-permute-start.3 = (bf16[256,512]{1,0:T(8,128)(2,1)S(1)}, bf16[256,512]{1,0:T(8,128)(2,1)S(1)}, u32[]{:S(2)}, u32[]{:S(2)}) collective-permute-start(bf16[256,512]{1,0:T(8,128)(2,1)S(1)} %fusion.1), channel_id=1, source_target_pairs={{0,1},{1,0},{3,2},{2,3},{4,5},{5,4},{7,6},{6,7},{8,9},{9,8},{11,10... | collective-permute-start | bytes 786440 | tf_op jit(solution)/shard_map/ppermute | solution.py:101
  39.8 12.9 %collective-permute-start.7 = (bf16[256,1024]{1,0:T(8,128)(2,1)S(1)}, bf16[256,1024]{1,0:T(8,128)(2,1)S(1)}, u32[]{:S(2)}, u32[]{:S(2)}) collective-permute-start(bf16[256,1024]{1,0:T(8,128)(2,1)S(1)} %pad_maximum_fusion), channel_id=1, source_target_pairs={{0,4},{1,5},{2,6},{3,7},{4,0},{5,1},{6,2},{7,3},{8,12},{9,13},{10,... | collective-permute-start | bytes 1572872 | tf_op jit(solution)/shard_map/ppermute | solution.py:101
  51.2 1.8 %collective-permute-start.4 = (bf16[128,1024]{1,0:T(8,128)(2,1)S(1)}, bf16[128,1024]{1,0:T(8,128)(2,1)S(1)}, u32[]{:S(2)}, u32[]{:S(2)}) collective-permute-start(bf16[128,1024]{1,0:T(8,128)(2,1)S(1)} %get-tuple-element.47.add_ref), channel_id=1, source_target_pairs={{0,4},{1,2},{2,1},{3,7},{4,0},{5,25},{6,26},{7,3},{8,12},{9,13},{1... | collective-permute-start | bytes 786440 | tf_op jit(solution)/shard_map/ppermute | solution.py:101
  51.3 4.3 %collective-permute-start.9 = (bf16[128,1024]{1,0:T(8,128)(2,1)S(1)}, bf16[128,1024]{1,0:T(8,128)(2,1)S(1)}, u32[]{:S(2)}, u32[]{:S(2)}) collective-permute-start(bf16[128,1024]{1,0:T(8,128)(2,1)S(1)} %get-tuple-element.24.own_ref.add_ref), channel_id=1, source_target_pairs={{0,4},{1,2},{2,1},{3,7},{4,0},{5,25},{6,26},{7,3},{8,12},{9,13},{1... | collective-permute-start | bytes 786440 | tf_op jit(solution)/shard_map/ppermute | solution.py:101
  55.6 12.0 %copy-start.16 = (bf16[128,1024]{1,0:T(8,128)(2,1)}, bf16[128,1024]{1,0:T(8,128)(2,1)S(1)}, u32[]{:S(2)}) copy-start(bf16[128,1024]{1,0:T(8,128)(2,1)S(1)} %shard_map.55) | copy-start | bytes 786436
  55.6 3.2 %copy-start.1 = (bf16[1,2048,512]{2,1,0:T(8,128)(2,1)S(1)}, bf16[1,2048,512]{2,1,0:T(8,128)(2,1)}, u32[]{:S(2)}) copy-start(bf16[1,2048,512]{2,1,0:T(8,128)(2,1)} %param.5) | copy-start | bytes 6291460
  58.3 12.5 %copy-start.14 = (bf16[128,1024]{1,0:T(8,128)(2,1)}, bf16[128,1024]{1,0:T(8,128)(2,1)S(1)}, u32[]{:S(2)}) copy-start(bf16[128,1024]{1,0:T(8,128)(2,1)S(1)} %shard_map.56) | copy-start | bytes 786436
  58.3 11.2 %collective-permute-start.11 = (bf16[2048,512]{1,0:T(8,128)(2,1)}, bf16[2048,512]{1,0:T(8,128)(2,1)S(1)}, u32[]{:S(2)}, u32[]{:S(2)}) collective-permute-start(bf16[2048,512]{1,0:T(8,128)(2,1)} %collective-permute-done.6.far_ref), channel_id=1, source_target_pairs={{0,4},{1,5},{2,6},{3,7},{4,0},{5,1},{6,2},{7,3},{8,12},{9,13},{10,... | collective-permute-start | bytes 6291464 | tf_op jit(solution)/shard_map/ppermute | solution.py:101
  58.8 32.2 %collective-permute-start.15 = (bf16[2048,512]{1,0:T(8,128)(2,1)S(1)}, bf16[2048,512]{1,0:T(8,128)(2,1)S(1)}, u32[]{:S(2)}, u32[]{:S(2)}) collective-permute-start(bf16[2048,512]{1,0:T(8,128)(2,1)S(1)} %bitcast.26), channel_id=1, source_target_pairs={{0,5},{3,6},{12,9},{15,10},{16,21},{19,22},{28,25},{31,26}} | collective-permute-start | bytes 6291464 | tf_op jit(solution)/shard_map/ppermute | solution.py:101
  67.6 1.6 collective-permute-start.8
  67.6 1.9 %collective-permute-start.10 = (bf16[128,1024]{1,0:T(8,128)(2,1)S(1)}, bf16[128,1024]{1,0:T(8,128)(2,1)S(1)}, u32[]{:S(2)}, u32[]{:S(2)}) collective-permute-start(bf16[128,1024]{1,0:T(8,128)(2,1)S(1)} %shard_map.55), channel_id=1, source_target_pairs={{0,4},{1,10},{2,9},{3,7},{4,0},{5,1},{6,2},{7,3},{8,12},{9,13},{10... | collective-permute-start | bytes 786440 | tf_op jit(solution)/shard_map/ppermute | solution.py:101
  68.1 3.0 %collective-permute-start.12 = (bf16[128,1024]{1,0:T(8,128)(2,1)S(1)}, bf16[128,1024]{1,0:T(8,128)(2,1)S(1)}, u32[]{:S(2)}, u32[]{:S(2)}) collective-permute-start(bf16[128,1024]{1,0:T(8,128)(2,1)S(1)} %shard_map.56), channel_id=1, source_target_pairs={{0,4},{1,9},{2,10},{3,7},{4,0},{5,1},{6,2},{7,3},{8,12},{9,13},{10... | collective-permute-start | bytes 786440 | tf_op jit(solution)/shard_map/ppermute | solution.py:101
  69.2 1.9 %collective-permute-start.13 = (bf16[128,1024]{1,0:T(8,128)(2,1)S(1)}, bf16[128,1024]{1,0:T(8,128)(2,1)S(1)}, u32[]{:S(2)}, u32[]{:S(2)}) collective-permute-start(bf16[128,1024]{1,0:T(8,128)(2,1)S(1)} %shard_map.56), channel_id=1, source_target_pairs={{0,4},{1,10},{2,9},{3,7},{4,0},{5,1},{6,2},{7,3},{8,12},{9,13},{10... | collective-permute-start | bytes 786440 | tf_op jit(solution)/shard_map/ppermute | solution.py:101
  69.5 54.6 %copy-start.5 = (bf16[2048,512]{1,0:T(8,128)(2,1)}, bf16[2048,512]{1,0:T(8,128)(2,1)S(1)}, u32[]{:S(2)}) copy-start(bf16[2048,512]{1,0:T(8,128)(2,1)S(1)} %collective-permute-done.11.far_ref) | copy-start | bytes 6291460
  70.9 20.1 %copy-start.7 = (bf16[128,1024]{1,0:T(8,128)(2,1)}, bf16[128,1024]{1,0:T(8,128)(2,1)S(1)}, u32[]{:S(2)}) copy-start(bf16[128,1024]{1,0:T(8,128)(2,1)S(1)} %shard_map.57.own_ref) | copy-start | bytes 786436
  70.9 20.1 %collective-permute-start.14 = (bf16[128,1024]{1,0:T(8,128)(2,1)S(1)}, bf16[128,1024]{1,0:T(8,128)(2,1)S(1)}, u32[]{:S(2)}, u32[]{:S(2)}) collective-permute-start(bf16[128,1024]{1,0:T(8,128)(2,1)S(1)} %shard_map.57.own_ref), channel_id=1, source_target_pairs={{0,4},{1,5},{2,6},{3,7},{4,0},{5,1},{6,2},{7,3},{8,12},{9,10},{10,... | collective-permute-start | bytes 786440 | tf_op jit(solution)/shard_map/ppermute | solution.py:101
  72.4 21.5 %collective-permute-start.17 = (bf16[128,1024]{1,0:T(8,128)(2,1)S(1)}, bf16[128,1024]{1,0:T(8,128)(2,1)S(1)}, u32[]{:S(2)}, u32[]{:S(2)}) collective-permute-start(bf16[128,1024]{1,0:T(8,128)(2,1)S(1)} %shard_map.58.own_ref), channel_id=1, source_target_pairs={{0,4},{1,5},{2,6},{3,7},{4,0},{5,1},{6,2},{7,3},{8,12},{9,10},{10,... | collective-permute-start | bytes 786440 | tf_op jit(solution)/shard_map/ppermute | solution.py:101
  91.0 5.2 %copy-start.3 = (bf16[2048,512]{1,0:T(8,128)(2,1)}, bf16[2048,512]{1,0:T(8,128)(2,1)S(1)}, u32[]{:S(2)}) copy-start(bf16[2048,512]{1,0:T(8,128)(2,1)S(1)} %collective-permute-done.15.far_ref) | copy-start | bytes 6291460
  93.9 2.9 %copy-start.20 = (bf16[128,1024]{1,0:T(8,128)(2,1)}, bf16[128,1024]{1,0:T(8,128)(2,1)S(1)}, u32[]{:S(2)}) copy-start(bf16[128,1024]{1,0:T(8,128)(2,1)S(1)} %shard_map.59) | copy-start | bytes 786436
  96.1 6.3 %copy-start.18 = (bf16[128,1024]{1,0:T(8,128)(2,1)}, bf16[128,1024]{1,0:T(8,128)(2,1)S(1)}, u32[]{:S(2)}) copy-start(bf16[128,1024]{1,0:T(8,128)(2,1)S(1)} %shard_map.60) | copy-start | bytes 786436
  96.1 5.0 %collective-permute-start.19 = (bf16[2048,512]{1,0:T(8,128)(2,1)S(1)}, bf16[2048,512]{1,0:T(8,128)(2,1)S(1)}, u32[]{:S(2)}, u32[]{:S(2)}) collective-permute-start(bf16[2048,512]{1,0:T(8,128)(2,1)S(1)} %collective-permute-done.15.far_ref), channel_id=1, source_target_pairs={{0,4},{1,5},{2,6},{3,7},{4,0},{5,1},{6,2},{7,3},{8,12},{9,13},{10,... | collective-permute-start | bytes 6291464 | tf_op jit(solution)/shard_map/ppermute | solution.py:101
  96.2 4.5 %collective-permute-start.16 = (bf16[128,1024]{1,0:T(8,128)(2,1)S(1)}, bf16[128,1024]{1,0:T(8,128)(2,1)S(1)}, u32[]{:S(2)}, u32[]{:S(2)}) collective-permute-start(bf16[128,1024]{1,0:T(8,128)(2,1)S(1)} %shard_map.59), channel_id=1, source_target_pairs={{0,4},{1,5},{2,6},{3,7},{4,0},{5,1},{6,2},{7,3},{8,12},{9,17},{10,... | collective-permute-start | bytes 786440 | tf_op jit(solution)/shard_map/ppermute | solution.py:101
  96.7 4.4 %collective-permute-start.18 = (bf16[128,1024]{1,0:T(8,128)(2,1)S(1)}, bf16[128,1024]{1,0:T(8,128)(2,1)S(1)}, u32[]{:S(2)}, u32[]{:S(2)}) collective-permute-start(bf16[128,1024]{1,0:T(8,128)(2,1)S(1)} %shard_map.59), channel_id=1, source_target_pairs={{0,4},{1,5},{2,6},{3,7},{4,0},{5,1},{6,2},{7,3},{8,12},{9,18},{10,... | collective-permute-start | bytes 786440 | tf_op jit(solution)/shard_map/ppermute | solution.py:101
  96.8 5.9 %collective-permute-start.20 = (bf16[128,1024]{1,0:T(8,128)(2,1)S(1)}, bf16[128,1024]{1,0:T(8,128)(2,1)S(1)}, u32[]{:S(2)}, u32[]{:S(2)}) collective-permute-start(bf16[128,1024]{1,0:T(8,128)(2,1)S(1)} %shard_map.60), channel_id=1, source_target_pairs={{0,4},{1,5},{2,6},{3,7},{4,0},{5,1},{6,2},{7,3},{8,12},{9,17},{10,... | collective-permute-start | bytes 786440 | tf_op jit(solution)/shard_map/ppermute | solution.py:101
  97.2 5.4 %collective-permute-start.21 = (bf16[128,1024]{1,0:T(8,128)(2,1)S(1)}, bf16[128,1024]{1,0:T(8,128)(2,1)S(1)}, u32[]{:S(2)}, u32[]{:S(2)}) collective-permute-start(bf16[128,1024]{1,0:T(8,128)(2,1)S(1)} %shard_map.60), channel_id=1, source_target_pairs={{0,4},{1,5},{2,6},{3,7},{4,0},{5,1},{6,2},{7,3},{8,12},{9,18},{10,... | collective-permute-start | bytes 786440 | tf_op jit(solution)/shard_map/ppermute | solution.py:101
  102.5 2.0 %copy-start.11 = (bf16[128,1024]{1,0:T(8,128)(2,1)}, bf16[128,1024]{1,0:T(8,128)(2,1)S(1)}, u32[]{:S(2)}) copy-start(bf16[128,1024]{1,0:T(8,128)(2,1)S(1)} %shard_map.61.own_ref) | copy-start | bytes 786436
  102.5 2.0 %collective-permute-start.22 = (bf16[128,1024]{1,0:T(8,128)(2,1)S(1)}, bf16[128,1024]{1,0:T(8,128)(2,1)S(1)}, u32[]{:S(2)}, u32[]{:S(2)}) collective-permute-start(bf16[128,1024]{1,0:T(8,128)(2,1)S(1)} %shard_map.61.own_ref), channel_id=1, source_target_pairs={{0,4},{1,5},{2,6},{3,7},{4,0},{5,1},{6,2},{7,3},{8,12},{9,21},{10,... | collective-permute-start | bytes 786440 | tf_op jit(solution)/shard_map/ppermute | solution.py:101
  104.0 3.6 %copy-start.9 = (bf16[128,1024]{1,0:T(8,128)(2,1)}, bf16[128,1024]{1,0:T(8,128)(2,1)S(1)}, u32[]{:S(2)}) copy-start(bf16[128,1024]{1,0:T(8,128)(2,1)S(1)} %shard_map.62.own_ref) | copy-start | bytes 786436
  104.0 3.6 %collective-permute-start.24 = (bf16[128,1024]{1,0:T(8,128)(2,1)S(1)}, bf16[128,1024]{1,0:T(8,128)(2,1)S(1)}, u32[]{:S(2)}, u32[]{:S(2)}) collective-permute-start(bf16[128,1024]{1,0:T(8,128)(2,1)S(1)} %shard_map.62.own_ref), channel_id=1, source_target_pairs={{0,4},{1,5},{2,6},{3,7},{4,0},{5,1},{6,2},{7,3},{8,12},{9,21},{10,... | collective-permute-start | bytes 786440 | tf_op jit(solution)/shard_map/ppermute | solution.py:101
  107.0 3.8 %copy-start.22 = (bf16[128,1024]{1,0:T(8,128)(2,1)}, bf16[128,1024]{1,0:T(8,128)(2,1)S(1)}, u32[]{:S(2)}) copy-start(bf16[128,1024]{1,0:T(8,128)(2,1)S(1)} %shard_map.63) | copy-start | bytes 786436
  107.0 17.1 %collective-permute-start.23 = (bf16[128,1024]{1,0:T(8,128)(2,1)S(1)}, bf16[128,1024]{1,0:T(8,128)(2,1)S(1)}, u32[]{:S(2)}, u32[]{:S(2)}) collective-permute-start(bf16[128,1024]{1,0:T(8,128)(2,1)S(1)} %shard_map.63), channel_id=1, source_target_pairs={{0,4},{1,9},{2,10},{3,7},{4,0},{5,1},{6,2},{7,3},{8,12},{9,13},{10... | collective-permute-start | bytes 786440 | tf_op jit(solution)/shard_map/ppermute | solution.py:101
  107.2 16.9 %collective-permute-start.25 = (bf16[128,1024]{1,0:T(8,128)(2,1)S(1)}, bf16[128,1024]{1,0:T(8,128)(2,1)S(1)}, u32[]{:S(2)}, u32[]{:S(2)}) collective-permute-start(bf16[128,1024]{1,0:T(8,128)(2,1)S(1)} %shard_map.63), channel_id=1, source_target_pairs={{0,4},{1,9},{2,10},{3,7},{4,0},{5,1},{6,2},{7,3},{8,12},{9,13},{10... | collective-permute-start | bytes 786440 | tf_op jit(solution)/shard_map/ppermute | solution.py:101
  110.8 15.8 %collective-permute-start.26 = (bf16[128,1024]{1,0:T(8,128)(2,1)}, bf16[128,1024]{1,0:T(8,128)(2,1)}, u32[]{:S(2)}, u32[]{:S(2)}) collective-permute-start(bf16[128,1024]{1,0:T(8,128)(2,1)} %shard_map.64), channel_id=1, source_target_pairs={{0,4},{1,9},{2,10},{3,7},{4,0},{5,1},{6,2},{7,3},{8,12},{9,13},{10... | collective-permute-start | bytes 786440 | tf_op jit(solution)/shard_map/ppermute | solution.py:101
  111.0 57.4 %collective-permute-start.31 = (bf16[2048,512]{1,0:T(8,128)(2,1)}, bf16[2048,512]{1,0:T(8,128)(2,1)}, u32[]{:S(2)}, u32[]{:S(2)}) collective-permute-start(bf16[2048,512]{1,0:T(8,128)(2,1)} %bitcast.7.near_ref), channel_id=1, source_target_pairs={{0,1},{3,2},{4,5},{7,6},{8,9},{11,10},{12,13},{15,14},{16,17},{19,... | collective-permute-start | bytes 6291464 | tf_op jit(solution)/shard_map/ppermute | solution.py:101
  124.0 2.6 %collective-permute-start.27 = (bf16[128,1024]{1,0:T(8,128)(2,1)}, bf16[128,1024]{1,0:T(8,128)(2,1)}, u32[]{:S(2)}, u32[]{:S(2)}) collective-permute-start(bf16[128,1024]{1,0:T(8,128)(2,1)} %shard_map.64), channel_id=1, source_target_pairs={{0,4},{1,9},{2,10},{3,7},{4,0},{5,1},{6,2},{7,3},{8,12},{9,13},{10... | collective-permute-start | bytes 786440 | tf_op jit(solution)/shard_map/ppermute | solution.py:101
  126.1 6.4 %collective-permute-start.28 = (bf16[128,1024]{1,0:T(8,128)(2,1)}, bf16[128,1024]{1,0:T(8,128)(2,1)}, u32[]{:S(2)}, u32[]{:S(2)}) collective-permute-start(bf16[128,1024]{1,0:T(8,128)(2,1)} %shard_map.65.own_ref), channel_id=1, source_target_pairs={{0,4},{1,29},{2,30},{3,7},{4,0},{5,6},{6,5},{7,3},{8,12},{9,13},{1... | collective-permute-start | bytes 786440 | tf_op jit(solution)/shard_map/ppermute | solution.py:101
  126.6 1.6 copy-start.2
  128.2 1.6 copy-start.6
  129.8 2.7 %copy-start.4 = (bf16[2048,512]{1,0:T(8,128)(2,1)S(1)}, bf16[2048,512]{1,0:T(8,128)(2,1)}, u32[]{:S(2)}) copy-start(bf16[2048,512]{1,0:T(8,128)(2,1)} %copy-done.3) | copy-start | bytes 6291460
  132.3 3.4 %copy-start.17 = (bf16[128,1024]{1,0:T(8,128)(2,1)S(1)}, bf16[128,1024]{1,0:T(8,128)(2,1)}, u32[]{:S(2)}) copy-start(bf16[128,1024]{1,0:T(8,128)(2,1)} %copy-done.16) | copy-start | bytes 786436
  132.3 3.4 %copy-start.21 = (bf16[128,1024]{1,0:T(8,128)(2,1)S(1)}, bf16[128,1024]{1,0:T(8,128)(2,1)}, u32[]{:S(2)}) copy-start(bf16[128,1024]{1,0:T(8,128)(2,1)} %copy-done.20) | copy-start | bytes 786436
  132.3 3.4 %copy-start.23 = (bf16[128,1024]{1,0:T(8,128)(2,1)S(1)}, bf16[128,1024]{1,0:T(8,128)(2,1)}, u32[]{:S(2)}) copy-start(bf16[128,1024]{1,0:T(8,128)(2,1)} %copy-done.22) | copy-start | bytes 786436
  132.3 4.0 %collective-permute-start.33 = (bf16[128,1024]{1,0:T(8,128)(2,1)S(1)}, bf16[128,1024]{1,0:T(8,128)(2,1)S(1)}, u32[]{:S(2)}, u32[]{:S(2)}) collective-permute-start(bf16[128,1024]{1,0:T(8,128)(2,1)S(1)} %shard_map.66.own_ref), channel_id=1, source_target_pairs={{0,4},{1,29},{2,30},{3,7},{4,0},{5,6},{6,5},{7,3},{8,12},{9,13},{1... | collective-permute-start | bytes 786440 | tf_op jit(solution)/shard_map/ppermute | solution.py:101
  135.8 2.6 %copy-start.15 = (bf16[128,1024]{1,0:T(8,128)(2,1)S(1)}, bf16[128,1024]{1,0:T(8,128)(2,1)}, u32[]{:S(2)}) copy-start(bf16[128,1024]{1,0:T(8,128)(2,1)} %copy-done.14) | copy-start | bytes 786436
  135.8 2.6 %copy-start.19 = (bf16[128,1024]{1,0:T(8,128)(2,1)S(1)}, bf16[128,1024]{1,0:T(8,128)(2,1)}, u32[]{:S(2)}) copy-start(bf16[128,1024]{1,0:T(8,128)(2,1)} %copy-done.18) | copy-start | bytes 786436
  135.8 3.0 %copy-start.8 = (bf16[128,1024]{1,0:T(8,128)(2,1)S(1)}, bf16[128,1024]{1,0:T(8,128)(2,1)}, u32[]{:S(2)}) copy-start(bf16[128,1024]{1,0:T(8,128)(2,1)} %copy-done.7) | copy-start | bytes 786436
  135.8 3.0 %copy-start.12 = (bf16[128,1024]{1,0:T(8,128)(2,1)S(1)}, bf16[128,1024]{1,0:T(8,128)(2,1)}, u32[]{:S(2)}) copy-start(bf16[128,1024]{1,0:T(8,128)(2,1)} %copy-done.11) | copy-start | bytes 786436
  135.8 3.0 %collective-permute-start.29 = (bf16[128,1024]{1,0:T(8,128)(2,1)S(1)}, bf16[128,1024]{1,0:T(8,128)(2,1)S(1)}, u32[]{:S(2)}, u32[]{:S(2)}) collective-permute-start(bf16[128,1024]{1,0:T(8,128)(2,1)S(1)} %select_select_fusion.2), channel_id=1, source_target_pairs={{0,4},{1,5},{2,6},{3,7},{4,0},{5,1},{6,2},{7,3},{8,12},{9,13},{10,... | collective-permute-start | bytes 786440 | tf_op jit(solution)/shard_map/ppermute | solution.py:101
  138.4 1.9 %copy-start.10 = (bf16[128,1024]{1,0:T(8,128)(2,1)S(1)}, bf16[128,1024]{1,0:T(8,128)(2,1)}, u32[]{:S(2)}) copy-start(bf16[128,1024]{1,0:T(8,128)(2,1)} %copy-done.9) | copy-start | bytes 786436
  138.5 1.8 collective-permute-start.34
  139.0 29.4 %collective-permute-start.30 = (bf16[128,1024]{1,0:T(8,128)(2,1)S(1)}, bf16[128,1024]{1,0:T(8,128)(2,1)S(1)}, u32[]{:S(2)}, u32[]{:S(2)}) collective-permute-start(bf16[128,1024]{1,0:T(8,128)(2,1)S(1)} %fusion.3.own_ref), channel_id=1, source_target_pairs={{0,4},{1,2},{2,1},{3,7},{4,0},{5,6},{6,5},{7,3},{8,12},{9,10},{10,... | collective-permute-start | bytes 786440 | tf_op jit(solution)/shard_map/ppermute | solution.py:101
  141.3 32.8 %collective-permute-start.35 = (bf16[128,1024]{1,0:T(8,128)(2,1)S(1)}, bf16[128,1024]{1,0:T(8,128)(2,1)S(1)}, u32[]{:S(2)}, u32[]{:S(2)}) collective-permute-start(bf16[128,1024]{1,0:T(8,128)(2,1)S(1)} %fusion.5.own_ref), channel_id=1, source_target_pairs={{0,4},{1,2},{2,1},{3,7},{4,0},{5,6},{6,5},{7,3},{8,12},{9,10},{10,... | collective-permute-start | bytes 786440 | tf_op jit(solution)/shard_map/ppermute | solution.py:101
  168.4 5.8 %copy-start.13 = (f32[128,1024]{1,0:T(8,128)S(1)}, f32[128,1024]{1,0:T(8,128)}, u32[]{:S(2)}) copy-start(f32[128,1024]{1,0:T(8,128)} %get-tuple-element.43.add_ref) | copy-start | bytes 1572868
  171.6 5.9 %collective-permute-start.32 = (bf16[128,512]{1,0:T(8,128)(2,1)}, bf16[128,512]{1,0:T(8,128)(2,1)S(1)}, u32[]{:S(2)}, u32[]{:S(2)}) collective-permute-start(bf16[128,512]{1,0:T(8,128)(2,1)} %slice.38), channel_id=1, source_target_pairs={{0,1},{1,0},{3,2},{2,3},{4,5},{5,4},{7,6},{6,7},{8,9},{9,8},{11,10... | collective-permute-start | bytes 393224 | tf_op jit(solution)/shard_map/ppermute | solution.py:101
  176.7 5.0 %collective-permute-start.36 = (bf16[128,512]{1,0:T(8,128)(2,1)S(1)}, bf16[128,512]{1,0:T(8,128)(2,1)S(1)}, u32[]{:S(2)}, u32[]{:S(2)}) collective-permute-start(bf16[128,512]{1,0:T(8,128)(2,1)S(1)} %slice.40), channel_id=1, source_target_pairs={{0,1},{1,0},{3,2},{2,3},{4,5},{5,4},{7,6},{6,7},{8,9},{9,8},{11,10... | collective-permute-start | bytes 393224 | tf_op jit(solution)/shard_map/ppermute | solution.py:101
where the time goes:
time: 183 us; the launch traced here: 182 us
  waiting for transfers between devices  81.9 us (45%)
  starting transfers between devices  51.7 us (28%)
  Pallas kernels  36.3 us (20%)
  other arithmetic  5.83 us (3%)
  local copies, waits for them, and re-layouts  4.06 us (2%)
  matrix products  2.15 us (1%)
    ppermute x34, waiting for transfers between devices, move(): return lax.ppermute(values, AXES, pairs)  64.5 us
    ppermute x34, starting transfers between devices, move(): return lax.ppermute(values, AXES, pairs)  45.6 us
    pallas_call x16, Pallas kernels, applied(): pl.pallas_call(functools.partial(apply_kernel, width), out_shape=jax.Shap...  36.3 us
    ppermute x3, waiting for transfers between devices, shards(): lax.ppermute(flat, 'trace', [(i, (i + k) % trace_count) for i in range(tr...  17.3 us
    ppermute x3, starting transfers between devices, shards(): lax.ppermute(flat, 'trace', [(i, (i + k) % trace_count) for i in range(tr...  6.09 us
  transfers between devices with their start and end apart: 37, of which 13 were waited for; matrix products, arithmetic and copies ran while one was open for 3% of the time, Pallas kernels for 17%

commit v1 on v0

--- a/solution.py
+++ b/solution.py
@@ -83,6 +83,9 @@
             for c in range(self.columns) for k in (0, 1) for end, holder in self.ends(hop)
         ]
 
+    def outward(self, hop):
+        return [(holder, end) for end, holder in self.inward(hop)]
+
     def first_sender(self, column):
         if column < self.columns // 2:
             return 1 if column == 0 else 0
@@ -109,12 +112,11 @@
     return pieces if len(pieces) < 2 else [jnp.concatenate(pieces, 1)]
 
 
-def dot32(rows, matrix):
-    return jnp.dot(rows, matrix, preferred_element_type=jnp.float32)
-
-
-def apply_kernel(width, own_ref, other_ref, near_ref, far_ref, add_ref, out_ref, near_tiles, far_tiles, sems):
-    depth = near_ref.shape[0] // width
+def apply_kernel(width, pieces, own_ref, other_ref, *refs):
+    operators, rest = refs[:pieces], refs[pieces:]
+    add_ref = rest[0] if len(rest) > pieces + 2 else None
+    out_ref, tiles, sems = rest[-pieces - 2], rest[-pieces - 1:-1], rest[-1]
+    depth = operators[0].shape[0] // width
     half = width // 2
     lower = lax.axis_index("trace") < half
     down = [half - 1 - i for i in range(half)]
@@ -123,48 +125,49 @@
     copies = []
     for t, block in enumerate(blocks):
         rows = pl.ds(pl.multiple_of(block * depth, depth), depth)
-        pair = (
-            pltpu.make_async_copy(near_ref.at[rows, :], near_tiles.at[t], sems.at[0, t]),
-            pltpu.make_async_copy(far_ref.at[rows, :], far_tiles.at[t], sems.at[1, t]),
-        )
-        for copy in pair:
+        group = [
+            pltpu.make_async_copy(operator.at[rows, :], tile.at[t], sems.at[i, t])
+            for i, (operator, tile) in enumerate(zip(operators, tiles))
+        ]
+        for copy in group:
             copy.start()
-        copies.append(pair)
-    near = far = 0.0
-    for t, pair in enumerate(copies):
+        copies.append(group)
+    totals = [0.0] * pieces
+    for t, group in enumerate(copies):
         source = own_ref if t < half else other_ref
         rows = source[:, (t % half) * depth:(t % half + 1) * depth]
-        for copy in pair:
+        for i, copy in enumerate(group):
             copy.wait()
-        near += jnp.dot(rows, near_tiles[t], preferred_element_type=jnp.float32)
-        far += jnp.dot(rows, far_tiles[t], preferred_element_type=jnp.float32)
-    cut = near_ref.shape[1]
-    out_ref[:, :cut] = (near + add_ref[:, :cut]).astype(out_ref.dtype)
-    out_ref[:, cut:] = (far + add_ref[:, cut:]).astype(out_ref.dtype)
-
-
-def applied(own, other, pieces, addend):
-    near, far = pieces
+            totals[i] += jnp.dot(rows, tiles[i][t], preferred_element_type=jnp.float32)
+    start = 0
+    for total in totals:
+        stop = start + total.shape[1]
+        if add_ref is not None:
+            total = total + add_ref[:, start:stop]
+        out_ref[:, start:stop] = total.astype(out_ref.dtype)
+        start = stop
+
+
+def applied(own, other, pieces, addend=None):
     width = lax.axis_size("trace")
-    rows, columns = addend.shape
-    depth = near.shape[0] // width
+    rows = own.shape[0]
+    deep = pieces[0].shape[0]
+    columns = sum(piece.shape[1] for piece in pieces)
     vmem = pl.BlockSpec(memory_space=pltpu.VMEM)
     hbm = pl.BlockSpec(memory_space=pltpu.HBM)
+    addends = [] if addend is None else [addend]
     return pl.pallas_call(
-        functools.partial(apply_kernel, width),
+        functools.partial(apply_kernel, width, len(pieces)),
         out_shape=jax.ShapeDtypeStruct((rows, columns), jnp.bfloat16),
-        in_specs=[vmem, vmem, hbm, hbm, vmem],
+        in_specs=[vmem, vmem] + [hbm] * len(pieces) + [vmem] * len(addends),
         out_specs=vmem,
-        scratch_shapes=[
-            pltpu.VMEM((width, depth, near.shape[1]), near.dtype),
-            pltpu.VMEM((width, depth, far.shape[1]), far.dtype),
-            pltpu.SemaphoreType.DMA((2, width)),
-        ],
+        scratch_shapes=[pltpu.VMEM((width, deep // width, piece.shape[1]), piece.dtype) for piece in pieces]
+        + [pltpu.SemaphoreType.DMA((len(pieces), width))],
         compiler_params=pltpu.CompilerParams(vmem_limit_bytes=16 * 1024 * 1024),
         cost_estimate=pl.CostEstimate(
-            flops=2 * rows * columns * near.shape[0], bytes_accessed=2 * columns * near.shape[0], transcendentals=0
+            flops=2 * rows * columns * deep, bytes_accessed=2 * columns * deep, transcendentals=0
         ),
-    )(own, other, near, far, addend)
+    )(own, other, *pieces, *addends)
 
 
 def in_turn(rows, pieces, addends, last):
@@ -193,31 +196,40 @@
     weighted = (own_sources.astype(jnp.float32) * weighting[:, :, None]).astype(jnp.bfloat16)
     flat = weighted.reshape(total_rows, trace_width)
 
-    gathered = [flat]
-    for k in range(1, trace_count):
-        gathered.append(lax.ppermute(flat, "trace", [(i, (i + k) % trace_count) for i in range(trace_count)]))
-    respond = response[0]
-    driven = jnp.zeros((total_rows, trace_width), jnp.float32)
-    for k, rows in enumerate(gathered):
-        block = lax.rem(z - k + trace_count, trace_count)
-        driven = driven + dot32(rows, lax.dynamic_slice_in_dim(respond, block * trace_width, trace_width, 0))
+    step = total_rows // CHUNKS
+
+    def split(values):
+        return [values[i * step:(i + 1) * step] for i in range(CHUNKS)]
+
+    near_halves, far_halves = [], []
+    for rows in split(flat):
+        from_ends = [move(rows, places.exchange_end(hop)) for hop in hops]
+        near = jnp.concatenate([rows] + from_ends, 1)
+        far = move(near, places.swap_all())
+        near_halves.append(near)
+        far_halves.append(far)
+    driven_parts = []
+    for rows, near, far in zip(split(flat), near_halves, far_halves):
+        far_outward = [move(far, places.outward(hop)) for hop in hops]
+        near_outward = [] if places.extra == 1 else [move(near, places.outward(hop)) for hop in hops]
+        if places.extra == 1:
+            near_outward = [jnp.concatenate([near[:, trace_width:], rows], 1)]
+        for hop, one_far, one_near in zip(hops, far_outward, near_outward):
+            here = (z == places.ends(hop)[0][0]) | (z == places.ends(hop)[1][0])
+            near, far = jnp.where(here, one_near, near), jnp.where(here, one_far, far)
+        driven_parts.append(applied(near, far, [response[0]]))
+    driven_sent = jnp.concatenate(driven_parts, 0)
 
     transfer = transmission[0]
     reflect = reflection[0]
     second_own = move(transfer, places.across_cores())
     second_early = joined([move(transfer, places.inward_crossed(hop, True)) for hop in hops])
 
-    driven_sent = driven.astype(jnp.bfloat16)
     first_driven = jnp.concatenate(
         [driven_sent] + [move(driven_sent, places.exchange_end(hop)) for hop in hops], 1
     )
     late_source = after(transfer, first_driven)
     second_late = joined([move(late_source, places.inward_crossed(hop, False)) for hop in hops])
-
-    step = total_rows // CHUNKS
-
-    def split(values):
-        return [values[i * step:(i + 1) * step] for i in range(CHUNKS)]
 
     firsts, seconds = [], []
 

time: 183 us -> 169 us (0.923)
  starting transfers between devices: 51.7 us -> 46.2 us
  Pallas kernels: 36.3 us -> 32.6 us
  waiting for transfers between devices: 81.9 us -> 84.6 us
  other arithmetic: 5.83 us -> 3.31 us
  local copies, waits for them, and re-layouts: 4.06 us -> 1.78 us
  matrix products: 2.15 us -> 0 us
    ppermute x34 -> x40, waiting for transfers between devices: 64.5 us -> 84.6 us  [move(): return lax.ppermute(values, AXES, pairs)]
    ppermute x3 -> x0, waiting for transfers between devices: 17.3 us -> none  [shards(): lax.ppermute(flat, 'trace', [(i, (i + k) % trace_count) for i in range(tr...]
    ppermute x3 -> x0, starting transfers between devices: 6.09 us -> none  [shards(): lax.ppermute(flat, 'trace', [(i, (i + k) % trace_count) for i in range(tr...]
    pallas_call x16 -> x18, Pallas kernels: 36.3 us -> 32.6 us  [applied(): pl.pallas_call(functools.partial(apply_kernel, width, len(pieces)), out_s...]
    dot_general x4 -> x0, matrix products: 2.15 us -> none  [dot32(): return jnp.dot(rows, matrix, preferred_element_type=jnp.float32)]
    ppermute x34 -> x40, starting transfers between devices: 45.6 us -> 46.2 us  [move(): return lax.ppermute(values, AXES, pairs)]
  transfers between devices with their start and end apart: 37 -> 40, of which waited for: 13 -> 18; matrix products, arithmetic and copies ran while one was open for 3% -> 0% of each run, Pallas kernels for 17% -> 17%
where the time goes in v1:
time: 169 us
  waiting for transfers between devices  84.6 us (50%)
  starting transfers between devices  46.2 us (27%)
  Pallas kernels  32.6 us (19%)
  other arithmetic  3.31 us (2%)
  local copies, waits for them, and re-layouts  1.78 us (1%)
    ppermute x40, waiting for transfers between devices, move(): return lax.ppermute(values, AXES, pairs)  84.6 us
    ppermute x40, starting transfers between devices, move(): return lax.ppermute(values, AXES, pairs)  46.2 us
    pallas_call x18, Pallas kernels, applied(): pl.pallas_call(functools.partial(apply_kernel, width, len(pieces)), out_s...  32.6 us
  transfers between devices with their start and end apart: 40, of which 18 were waited for; matrix products, arithmetic and copies ran while one was open for 0% of the time, Pallas kernels for 17%

profile of v1, /device:TPU:0, one launch (start us, length us, event | category | flops | bytes accessed | tf_op | source)
XLA Modules:
  0.0 169.1 jit_solution(16586010411522120483)
XLA Ops:
  0.0 0.7 add_divide_fusion
  0.7 1.1 fusion.4
  1.8 3.1 %collective-permute-start = (bf16[128,512]{1,0:T(8,128)(2,1)S(1)}, bf16[128,512]{1,0:T(8,128)(2,1)S(1)}, u32[]{:S(2)}, u32[]{:S(2)}) collective-permute-start(bf16[128,512]{1,0:T(8,128)(2,1)S(1)} %bitcast.22), channel_id=1, source_target_pairs={{0,1},{1,0},{3,2},{2,3},{4,5},{5,4},{7,6},{6,7},{8,9},{9,8},{11,10... | collective-permute-start | bytes 393224 | tf_op jit(solution)/shard_map/ppermute | solution.py:104
  4.9 3.5 %collective-permute-done = bf16[128,512]{1,0:T(8,128)(2,1)S(1)} collective-permute-done((bf16[128,512]{1,0:T(8,128)(2,1)S(1)}, bf16[128,512]{1,0:T(8,128)(2,1)S(1)}, u32[]{:S(2)}, u32[]{:S(2)}) %collective-permute-start) | collective-permute-done | bytes 131104 | tf_op jit(solution)/shard_map/ppermute | solution.py:104
  8.6 3.3 %collective-permute-start.3 = (bf16[128,512]{1,0:T(8,128)(2,1)S(1)}, bf16[128,512]{1,0:T(8,128)(2,1)S(1)}, u32[]{:S(2)}, u32[]{:S(2)}) collective-permute-start(bf16[128,512]{1,0:T(8,128)(2,1)S(1)} %bitcast.20), channel_id=1, source_target_pairs={{0,1},{1,0},{3,2},{2,3},{4,5},{5,4},{7,6},{6,7},{8,9},{9,8},{11,10... | collective-permute-start | bytes 393224 | tf_op jit(solution)/shard_map/ppermute | solution.py:104
  11.9 0.8 collective-permute-start.9
  12.7 2.1 %collective-permute-done.3 = bf16[128,512]{1,0:T(8,128)(2,1)S(1)} collective-permute-done((bf16[128,512]{1,0:T(8,128)(2,1)S(1)}, bf16[128,512]{1,0:T(8,128)(2,1)S(1)}, u32[]{:S(2)}, u32[]{:S(2)}) %collective-permute-start.3) | collective-permute-done | bytes 131104 | tf_op jit(solution)/shard_map/ppermute | solution.py:104
  15.0 1.3 collective-permute-start.2
  16.3 0.3 collective-permute-done.4
  16.6 1.3 collective-permute-start.5
  17.9 8.3 %collective-permute-done.2 = bf16[128,1024]{1,0:T(8,128)(2,1)S(1)} collective-permute-done((bf16[128,1024]{1,0:T(8,128)(2,1)S(1)}, bf16[128,1024]{1,0:T(8,128)(2,1)S(1)}, u32[]{:S(2)}, u32[]{:S(2)}) %collective-permute-start.2) | collective-permute-done | bytes 262176 | tf_op jit(solution)/shard_map/ppermute | solution.py:104
  26.3 0.8 shard_map.55
  27.1 4.1 %collective-permute-done.5 = bf16[128,1024]{1,0:T(8,128)(2,1)S(1)} collective-permute-done((bf16[128,1024]{1,0:T(8,128)(2,1)S(1)}, bf16[128,1024]{1,0:T(8,128)(2,1)S(1)}, u32[]{:S(2)}, u32[]{:S(2)}) %collective-permute-start.5) | collective-permute-done | bytes 262176 | tf_op jit(solution)/shard_map/ppermute | solution.py:104
  31.3 0.8 shard_map.56
  32.2 7.7 %collective-permute-done.6 = bf16[256,512]{1,0:T(8,128)(2,1)S(1)} collective-permute-done((bf16[256,512]{1,0:T(8,128)(2,1)S(1)}, bf16[256,512]{1,0:T(8,128)(2,1)S(1)}, u32[]{:S(2)}, u32[]{:S(2)}) %collective-permute-start.6) | collective-permute-done | bytes 262176 | tf_op jit(solution)/shard_map/ppermute | solution.py:104
  40.0 2.9 %collective-permute-start.10 = (bf16[256,1024]{1,0:T(8,128)(2,1)S(1)}, bf16[256,1024]{1,0:T(8,128)(2,1)S(1)}, u32[]{:S(2)}, u32[]{:S(2)}) collective-permute-start(bf16[256,1024]{1,0:T(8,128)(2,1)S(1)} %pad_maximum_fusion), channel_id=1, source_target_pairs={{0,4},{1,5},{2,6},{3,7},{4,0},{5,1},{6,2},{7,3},{8,12},{9,13},{10,... | collective-permute-start | bytes 1572872 | tf_op jit(solution)/shard_map/ppermute | solution.py:104
  43.0 0.5 collective-permute-start.12
  43.5 0.9 collective-permute-done.10
  44.4 0.3 collective-permute-done.7.other_ref
  44.8 1.6 shard_map.57
  46.4 1.6 shard_map.58
  48.0 0.4 collective-permute-start.14
  48.5 10.3 %collective-permute-start.18 = (bf16[2048,512]{1,0:T(8,128)(2,1)S(1)}, bf16[2048,512]{1,0:T(8,128)(2,1)S(1)}, u32[]{:S(2)}, u32[]{:S(2)}) collective-permute-start(bf16[2048,512]{1,0:T(8,128)(2,1)S(1)} %bitcast.11), channel_id=1, source_target_pairs={{0,5},{3,6},{12,9},{15,10},{16,21},{19,22},{28,25},{31,26}} | collective-permute-start | bytes 6291464 | tf_op jit(solution)/shard_map/ppermute | solution.py:104
  58.9 0.5 collective-permute-start.13
  59.4 0.9 collective-permute-done.11.own_ref
  60.5 0.2 collective-permute-done.13.other_ref
  60.8 1.6 shard_map.59.own_ref
  62.4 0.2 collective-permute-start.17
  62.6 1.6 shard_map.60.own_ref
  64.2 0.4 collective-permute-start.20
  64.6 17.6 %collective-permute-done.18.refs_1_ = bf16[2048,512]{1,0:T(8,128)(2,1)S(1)} collective-permute-done((bf16[2048,512]{1,0:T(8,128)(2,1)S(1)}, bf16[2048,512]{1,0:T(8,128)(2,1)S(1)}, u32[]{:S(2)}, u32[]{:S(2)}) %collective-permute-start.18) | collective-permute-done | bytes 2097184 | tf_op jit(solution)/shard_map/ppermute | solution.py:104
  82.2 1.6 shard_map.61
  83.8 1.6 shard_map.62
  85.5 0.5 collective-permute-start.19
  86.1 0.4 collective-permute-start.23
  86.6 3.4 %collective-permute-done.19.own_ref = bf16[128,1024]{1,0:T(8,128)(2,1)S(1)} collective-permute-done((bf16[128,1024]{1,0:T(8,128)(2,1)S(1)}, bf16[128,1024]{1,0:T(8,128)(2,1)S(1)}, u32[]{:S(2)}, u32[]{:S(2)}) %collective-permute-start.19) | collective-permute-done | bytes 262176 | tf_op jit(solution)/shard_map/ppermute | solution.py:104
  90.1 0.4 collective-permute-done.21.other_ref
  90.4 1.6 shard_map.63.own_ref
  92.0 0.2 collective-permute-start.25
  92.3 1.6 shard_map.64.own_ref
  93.9 0.4 collective-permute-start.27
  94.3 1.6 shard_map.65
  96.1 0.4 collective-permute-start.28
  96.5 1.6 shard_map.66
  98.3 0.4 collective-permute-start.30
  98.7 12.5 %collective-permute-start.34 = (bf16[2048,512]{1,0:T(8,128)(2,1)}, bf16[2048,512]{1,0:T(8,128)(2,1)}, u32[]{:S(2)}, u32[]{:S(2)}) collective-permute-start(bf16[2048,512]{1,0:T(8,128)(2,1)} %bitcast.5.refs_0_), channel_id=1, source_target_pairs={{0,1},{3,2},{4,5},{7,6},{8,9},{11,10},{12,13},{15,14},{16,17},{19,... | collective-permute-start | bytes 6291464 | tf_op jit(solution)/shard_map/ppermute | solution.py:104
  111.2 2.3 %shard_map.67.own_ref = bf16[128,1024]{1,0:T(8,128)(2,1)} custom-call(bf16[128,1024]{1,0:T(8,128)(2,1)S(1)} %collective-permute-done.26.own_ref, bf16[128,1024]{1,0:T(8,128)(2,1)S(1)} %collective-permute-done.28.other_ref, bf16[2048,512]{1,0:T(8,128)(2,1)S(1)} %bitcast.16, bf16[2048,512]{1,0:T(8,128)(2,1)S(1)} %collective-permute-done.14.refs_1_, ...), custom_call_target="tpu_custom_call" | custom-call | flops 536870912 | bytes 4194304 | tf_op jit(solution)/shard_map/pallas_call | solution.py:159
  113.7 2.3 %shard_map.68.own_ref = bf16[128,1024]{1,0:T(8,128)(2,1)} custom-call(bf16[128,1024]{1,0:T(8,128)(2,1)S(1)} %collective-permute-done.29.own_ref, bf16[128,1024]{1,0:T(8,128)(2,1)S(1)} %collective-permute-done.30.other_ref, bf16[2048,512]{1,0:T(8,128)(2,1)S(1)} %bitcast.17, bf16[2048,512]{1,0:T(8,128)(2,1)S(1)} %collective-permute-done.14.refs_1_, ...), custom_call_target="tpu_custom_call" | custom-call | flops 536870912 | bytes 4194304 | tf_op jit(solution)/shard_map/pallas_call | solution.py:159
  116.0 0.5 collective-permute-start.36
  116.5 1.6 copy-done.2
  118.0 2.6 %shard_map.69 = bf16[128,1024]{1,0:T(8,128)(2,1)S(1)} custom-call(bf16[128,1024]{1,0:T(8,128)(2,1)} %shard_map.67.own_ref, bf16[128,1024]{1,0:T(8,128)(2,1)} %collective-permute-done.31.other_ref, bf16[2048,512]{1,0:T(8,128)(2,1)S(1)} %collective-permute-done.8.refs_0_, bf16[2048,512]{1,0:T(8,128)(2,1)S(1)} %copy-done.2, ...), custom_call_target="tpu_custom_call" | custom-call | flops 536870912 | bytes 4194304 | tf_op jit(solution)/shard_map/pallas_call | solution.py:159
  120.7 2.7 %shard_map.71 = bf16[128,1024]{1,0:T(8,128)(2,1)S(1)} custom-call(bf16[128,1024]{1,0:T(8,128)(2,1)} %shard_map.68.own_ref, bf16[128,1024]{1,0:T(8,128)(2,1)} %collective-permute-done.36.other_ref, bf16[2048,512]{1,0:T(8,128)(2,1)S(1)} %collective-permute-done.8.refs_0_, bf16[2048,512]{1,0:T(8,128)(2,1)S(1)} %copy-done.2, ...), custom_call_target="tpu_custom_call" | custom-call | flops 536870912 | bytes 4194304 | tf_op jit(solution)/shard_map/pallas_call | solution.py:159
  123.9 0.4 collective-permute-start.32
  124.3 1.0 collective-permute-done.37
  125.3 0.4 collective-permute-done.32
  125.8 0.2 fusion.1
  126.0 1.2 collective-permute-start.33
  127.3 28.3 %collective-permute-done.34.refs_1_ = bf16[2048,512]{1,0:T(8,128)(2,1)} collective-permute-done((bf16[2048,512]{1,0:T(8,128)(2,1)}, bf16[2048,512]{1,0:T(8,128)(2,1)}, u32[]{:S(2)}, u32[]{:S(2)}) %collective-permute-start.34) | collective-permute-done | bytes 2097184 | tf_op jit(solution)/shard_map/ppermute | solution.py:104
  155.6 2.6 %shard_map.70 = bf16[128,1024]{1,0:T(8,128)(2,1)S(1)} custom-call(bf16[128,1024]{1,0:T(8,128)(2,1)S(1)} %get-tuple-element.57.own_ref, bf16[128,1024]{1,0:T(8,128)(2,1)S(1)} %collective-permute-done.33.other_ref, bf16[2048,512]{1,0:T(8,128)(2,1)} %bitcast.5.refs_0_, bf16[2048,512]{1,0:T(8,128)(2,1)} %collective-permute-done.34.refs_1_, ...), custom_call_target="tpu_custom_call" | custom-call | flops 536870912 | bytes 4194304 | tf_op jit(solution)/shard_map/pallas_call | solution.py:159
  158.2 2.6 %collective-permute-start.35 = (bf16[128,512]{1,0:T(8,128)(2,1)S(1)}, bf16[128,512]{1,0:T(8,128)(2,1)S(1)}, u32[]{:S(2)}, u32[]{:S(2)}) collective-permute-start(bf16[128,512]{1,0:T(8,128)(2,1)S(1)} %slice.56), channel_id=1, source_target_pairs={{0,1},{1,0},{3,2},{2,3},{4,5},{5,4},{7,6},{6,7},{8,9},{9,8},{11,10... | collective-permute-start | bytes 393224 | tf_op jit(solution)/shard_map/ppermute | solution.py:104
  160.8 2.6 %shard_map.72 = bf16[128,1024]{1,0:T(8,128)(2,1)S(1)} custom-call(bf16[128,1024]{1,0:T(8,128)(2,1)S(1)} %get-tuple-element.58.own_ref, bf16[128,1024]{1,0:T(8,128)(2,1)S(1)} %collective-permute-done.38.other_ref, bf16[2048,512]{1,0:T(8,128)(2,1)} %bitcast.5.refs_0_, bf16[2048,512]{1,0:T(8,128)(2,1)} %collective-permute-done.34.refs_1_, ...), custom_call_target="tpu_custom_call" | custom-call | flops 536870912 | bytes 4194304 | tf_op jit(solution)/shard_map/pallas_call | solution.py:159
  163.5 0.5 collective-permute-done.35
  164.0 4.4 %collective-permute-done.39 = bf16[128,512]{1,0:T(8,128)(2,1)S(1)} collective-permute-done((bf16[128,512]{1,0:T(8,128)(2,1)S(1)}, bf16[128,512]{1,0:T(8,128)(2,1)S(1)}, u32[]{:S(2)}, u32[]{:S(2)}) %collective-permute-start.39) | collective-permute-done | bytes 131104 | tf_op jit(solution)/shard_map/ppermute | solution.py:104
  168.4 0.7 pad_maximum_fusion.4
  (94 shorter events, 2.5 us)
Async XLA Ops:
  1.8 6.6 %collective-permute-start = (bf16[128,512]{1,0:T(8,128)(2,1)S(1)}, bf16[128,512]{1,0:T(8,128)(2,1)S(1)}, u32[]{:S(2)}, u32[]{:S(2)}) collective-permute-start(bf16[128,512]{1,0:T(8,128)(2,1)S(1)} %bitcast.22), channel_id=1, source_target_pairs={{0,1},{1,0},{3,2},{2,3},{4,5},{5,4},{7,6},{6,7},{8,9},{9,8},{11,10... | collective-permute-start | bytes 393224 | tf_op jit(solution)/shard_map/ppermute | solution.py:104
  4.9 21.4 %copy-start.3 = (bf16[1,2048,512]{2,1,0:T(8,128)(2,1)S(1)}, bf16[1,2048,512]{2,1,0:T(8,128)(2,1)}, u32[]{:S(2)}) copy-start(bf16[1,2048,512]{2,1,0:T(8,128)(2,1)} %param.7) | copy-start | bytes 6291460
  8.5 6.5 %collective-permute-start.1 = (bf16[128,1024]{1,0:T(8,128)(2,1)S(1)}, bf16[128,1024]{1,0:T(8,128)(2,1)S(1)}, u32[]{:S(2)}, u32[]{:S(2)}) collective-permute-start(bf16[128,1024]{1,0:T(8,128)(2,1)S(1)} %get-tuple-element.51), channel_id=1, source_target_pairs={{0,4},{1,2},{2,1},{3,7},{4,0},{5,6},{6,5},{7,3},{8,12},{9,10},{10,... | collective-permute-start | bytes 786440 | tf_op jit(solution)/shard_map/ppermute | solution.py:104
  8.6 6.2 %collective-permute-start.3 = (bf16[128,512]{1,0:T(8,128)(2,1)S(1)}, bf16[128,512]{1,0:T(8,128)(2,1)S(1)}, u32[]{:S(2)}, u32[]{:S(2)}) collective-permute-start(bf16[128,512]{1,0:T(8,128)(2,1)S(1)} %bitcast.20), channel_id=1, source_target_pairs={{0,1},{1,0},{3,2},{2,3},{4,5},{5,4},{7,6},{6,7},{8,9},{9,8},{11,10... | collective-permute-start | bytes 393224 | tf_op jit(solution)/shard_map/ppermute | solution.py:104
  11.9 32.9 %collective-permute-start.8 = (bf16[2048,512]{1,0:T(8,128)(2,1)}, bf16[2048,512]{1,0:T(8,128)(2,1)S(1)}, u32[]{:S(2)}, u32[]{:S(2)}) collective-permute-start(bf16[2048,512]{1,0:T(8,128)(2,1)} %bitcast.9), channel_id=1, source_target_pairs={{0,4},{1,5},{2,6},{3,7},{4,0},{5,1},{6,2},{7,3},{8,12},{9,13},{10,... | collective-permute-start | bytes 6291464 | tf_op jit(solution)/shard_map/ppermute | solution.py:104
  11.9 32.9 %collective-permute-start.9 = (bf16[2048,512]{1,0:T(8,128)(2,1)}, bf16[2048,512]{1,0:T(8,128)(2,1)S(1)}, u32[]{:S(2)}, u32[]{:S(2)}) collective-permute-start(bf16[2048,512]{1,0:T(8,128)(2,1)} %bitcast.10), channel_id=1, source_target_pairs={{4,1},{7,2},{8,13},{11,14},{20,17},{23,18},{24,29},{27,30}} | collective-permute-start | bytes 6291464 | tf_op jit(solution)/shard_map/ppermute | solution.py:104
  14.9 1.7 %collective-permute-start.4 = (bf16[128,1024]{1,0:T(8,128)(2,1)S(1)}, bf16[128,1024]{1,0:T(8,128)(2,1)S(1)}, u32[]{:S(2)}, u32[]{:S(2)}) collective-permute-start(bf16[128,1024]{1,0:T(8,128)(2,1)S(1)} %get-tuple-element.55), channel_id=1, source_target_pairs={{0,4},{1,2},{2,1},{3,7},{4,0},{5,6},{6,5},{7,3},{8,12},{9,10},{10,... | collective-permute-start | bytes 786440 | tf_op jit(solution)/shard_map/ppermute | solution.py:104
  15.0 11.2 %collective-permute-start.2 = (bf16[128,1024]{1,0:T(8,128)(2,1)S(1)}, bf16[128,1024]{1,0:T(8,128)(2,1)S(1)}, u32[]{:S(2)}, u32[]{:S(2)}) collective-permute-start(bf16[128,1024]{1,0:T(8,128)(2,1)S(1)} %collective-permute-done.1), channel_id=1, source_target_pairs={{1,0},{2,3},{5,4},{6,7},{9,8},{10,11},{13,12},{14,15},{17,16},{18,... | collective-permute-start | bytes 786440 | tf_op jit(solution)/shard_map/ppermute | solution.py:104
  16.6 14.6 %collective-permute-start.5 = (bf16[128,1024]{1,0:T(8,128)(2,1)S(1)}, bf16[128,1024]{1,0:T(8,128)(2,1)S(1)}, u32[]{:S(2)}, u32[]{:S(2)}) collective-permute-start(bf16[128,1024]{1,0:T(8,128)(2,1)S(1)} %collective-permute-done.4), channel_id=1, source_target_pairs={{1,0},{2,3},{5,4},{6,7},{9,8},{10,11},{13,12},{14,15},{17,16},{18,... | collective-permute-start | bytes 786440 | tf_op jit(solution)/shard_map/ppermute | solution.py:104
  32.1 7.8 %collective-permute-start.6 = (bf16[256,512]{1,0:T(8,128)(2,1)S(1)}, bf16[256,512]{1,0:T(8,128)(2,1)S(1)}, u32[]{:S(2)}, u32[]{:S(2)}) collective-permute-start(bf16[256,512]{1,0:T(8,128)(2,1)S(1)} %pad_maximum_fusion.3), channel_id=1, source_target_pairs={{0,1},{1,0},{3,2},{2,3},{4,5},{5,4},{7,6},{6,7},{8,9},{9,8},{11,10... | collective-permute-start | bytes 786440 | tf_op jit(solution)/shard_map/ppermute | solution.py:104
  39.9 6.4 %copy-start.18 = (bf16[256,1024]{1,0:T(8,128)(2,1)}, bf16[256,1024]{1,0:T(8,128)(2,1)S(1)}, u32[]{:S(2)}) copy-start(bf16[256,1024]{1,0:T(8,128)(2,1)S(1)} %pad_maximum_fusion) | copy-start | bytes 1572868
  40.0 4.4 %collective-permute-start.10 = (bf16[256,1024]{1,0:T(8,128)(2,1)S(1)}, bf16[256,1024]{1,0:T(8,128)(2,1)S(1)}, u32[]{:S(2)}, u32[]{:S(2)}) collective-permute-start(bf16[256,1024]{1,0:T(8,128)(2,1)S(1)} %pad_maximum_fusion), channel_id=1, source_target_pairs={{0,4},{1,5},{2,6},{3,7},{4,0},{5,1},{6,2},{7,3},{8,12},{9,13},{10,... | collective-permute-start | bytes 1572872 | tf_op jit(solution)/shard_map/ppermute | solution.py:104
  42.9 1.9 %collective-permute-start.7 = (bf16[128,1024]{1,0:T(8,128)(2,1)S(1)}, bf16[128,1024]{1,0:T(8,128)(2,1)S(1)}, u32[]{:S(2)}, u32[]{:S(2)}) collective-permute-start(bf16[128,1024]{1,0:T(8,128)(2,1)S(1)} %get-tuple-element.49.refs_2_), channel_id=1, source_target_pairs={{0,4},{1,2},{2,1},{3,7},{4,0},{5,25},{6,26},{7,3},{8,12},{9,13},{1... | collective-permute-start | bytes 786440 | tf_op jit(solution)/shard_map/ppermute | solution.py:104
  43.0 3.4 %collective-permute-start.12 = (bf16[128,1024]{1,0:T(8,128)(2,1)S(1)}, bf16[128,1024]{1,0:T(8,128)(2,1)S(1)}, u32[]{:S(2)}, u32[]{:S(2)}) collective-permute-start(bf16[128,1024]{1,0:T(8,128)(2,1)S(1)} %get-tuple-element.24.own_ref.refs_2_), channel_id=1, source_target_pairs={{0,4},{1,2},{2,1},{3,7},{4,0},{5,25},{6,26},{7,3},{8,12},{9,13},{1... | collective-permute-start | bytes 786440 | tf_op jit(solution)/shard_map/ppermute | solution.py:104
  46.4 12.5 %copy-start.6 = (bf16[128,1024]{1,0:T(8,128)(2,1)}, bf16[128,1024]{1,0:T(8,128)(2,1)S(1)}, u32[]{:S(2)}) copy-start(bf16[128,1024]{1,0:T(8,128)(2,1)S(1)} %shard_map.57) | copy-start | bytes 786436
  46.4 2.1 %copy-start = (bf16[1,2048,512]{2,1,0:T(8,128)(2,1)S(1)}, bf16[1,2048,512]{2,1,0:T(8,128)(2,1)}, u32[]{:S(2)}) copy-start(bf16[1,2048,512]{2,1,0:T(8,128)(2,1)} %param.5) | copy-start | bytes 6291460
  48.0 14.3 %copy-start.8 = (bf16[128,1024]{1,0:T(8,128)(2,1)}, bf16[128,1024]{1,0:T(8,128)(2,1)S(1)}, u32[]{:S(2)}) copy-start(bf16[128,1024]{1,0:T(8,128)(2,1)S(1)} %shard_map.58) | copy-start | bytes 786436
  48.0 12.7 %collective-permute-start.14 = (bf16[2048,512]{1,0:T(8,128)(2,1)S(1)}, bf16[2048,512]{1,0:T(8,128)(2,1)S(1)}, u32[]{:S(2)}, u32[]{:S(2)}) collective-permute-start(bf16[2048,512]{1,0:T(8,128)(2,1)S(1)} %collective-permute-done.9.refs_1_), channel_id=1, source_target_pairs={{0,4},{1,5},{2,6},{3,7},{4,0},{5,1},{6,2},{7,3},{8,12},{9,13},{10,... | collective-permute-start | bytes 6291464 | tf_op jit(solution)/shard_map/ppermute | solution.py:104
  48.5 33.7 %collective-permute-start.18 = (bf16[2048,512]{1,0:T(8,128)(2,1)S(1)}, bf16[2048,512]{1,0:T(8,128)(2,1)S(1)}, u32[]{:S(2)}, u32[]{:S(2)}) collective-permute-start(bf16[2048,512]{1,0:T(8,128)(2,1)S(1)} %bitcast.11), channel_id=1, source_target_pairs={{0,5},{3,6},{12,9},{15,10},{16,21},{19,22},{28,25},{31,26}} | collective-permute-start | bytes 6291464 | tf_op jit(solution)/shard_map/ppermute | solution.py:104
  58.8 1.6 collective-permute-start.11
  58.9 1.9 %collective-permute-start.13 = (bf16[128,1024]{1,0:T(8,128)(2,1)S(1)}, bf16[128,1024]{1,0:T(8,128)(2,1)S(1)}, u32[]{:S(2)}, u32[]{:S(2)}) collective-permute-start(bf16[128,1024]{1,0:T(8,128)(2,1)S(1)} %shard_map.57), channel_id=1, source_target_pairs={{0,4},{1,10},{2,9},{3,7},{4,0},{5,1},{6,2},{7,3},{8,12},{9,13},{10... | collective-permute-start | bytes 786440 | tf_op jit(solution)/shard_map/ppermute | solution.py:104
  59.4 3.2 %collective-permute-start.15 = (bf16[128,1024]{1,0:T(8,128)(2,1)S(1)}, bf16[128,1024]{1,0:T(8,128)(2,1)S(1)}, u32[]{:S(2)}, u32[]{:S(2)}) collective-permute-start(bf16[128,1024]{1,0:T(8,128)(2,1)S(1)} %shard_map.58), channel_id=1, source_target_pairs={{0,4},{1,9},{2,10},{3,7},{4,0},{5,1},{6,2},{7,3},{8,12},{9,13},{10... | collective-permute-start | bytes 786440 | tf_op jit(solution)/shard_map/ppermute | solution.py:104
  60.4 2.2 %collective-permute-start.16 = (bf16[128,1024]{1,0:T(8,128)(2,1)S(1)}, bf16[128,1024]{1,0:T(8,128)(2,1)S(1)}, u32[]{:S(2)}, u32[]{:S(2)}) collective-permute-start(bf16[128,1024]{1,0:T(8,128)(2,1)S(1)} %shard_map.58), channel_id=1, source_target_pairs={{0,4},{1,10},{2,9},{3,7},{4,0},{5,1},{6,2},{7,3},{8,12},{9,13},{10... | collective-permute-start | bytes 786440 | tf_op jit(solution)/shard_map/ppermute | solution.py:104
  62.4 19.8 %collective-permute-start.17 = (bf16[128,1024]{1,0:T(8,128)(2,1)S(1)}, bf16[128,1024]{1,0:T(8,128)(2,1)S(1)}, u32[]{:S(2)}, u32[]{:S(2)}) collective-permute-start(bf16[128,1024]{1,0:T(8,128)(2,1)S(1)} %shard_map.59.own_ref), channel_id=1, source_target_pairs={{0,4},{1,5},{2,6},{3,7},{4,0},{5,1},{6,2},{7,3},{8,12},{9,10},{10,... | collective-permute-start | bytes 786440 | tf_op jit(solution)/shard_map/ppermute | solution.py:104
  64.2 19.6 %collective-permute-start.20 = (bf16[128,1024]{1,0:T(8,128)(2,1)S(1)}, bf16[128,1024]{1,0:T(8,128)(2,1)S(1)}, u32[]{:S(2)}, u32[]{:S(2)}) collective-permute-start(bf16[128,1024]{1,0:T(8,128)(2,1)S(1)} %shard_map.60.own_ref), channel_id=1, source_target_pairs={{0,4},{1,5},{2,6},{3,7},{4,0},{5,1},{6,2},{7,3},{8,12},{9,10},{10,... | collective-permute-start | bytes 786440 | tf_op jit(solution)/shard_map/ppermute | solution.py:104
  82.2 3.2 %copy-start.1 = (bf16[2048,512]{1,0:T(8,128)(2,1)}, bf16[2048,512]{1,0:T(8,128)(2,1)S(1)}, u32[]{:S(2)}) copy-start(bf16[2048,512]{1,0:T(8,128)(2,1)S(1)} %collective-permute-done.18.refs_1_) | copy-start | bytes 6291460
  83.8 2.2 %copy-start.10 = (bf16[128,1024]{1,0:T(8,128)(2,1)}, bf16[128,1024]{1,0:T(8,128)(2,1)S(1)}, u32[]{:S(2)}) copy-start(bf16[128,1024]{1,0:T(8,128)(2,1)S(1)} %shard_map.61) | copy-start | bytes 786436
  85.4 6.6 %copy-start.12 = (bf16[128,1024]{1,0:T(8,128)(2,1)}, bf16[128,1024]{1,0:T(8,128)(2,1)S(1)}, u32[]{:S(2)}) copy-start(bf16[128,1024]{1,0:T(8,128)(2,1)S(1)} %shard_map.62) | copy-start | bytes 786436
  85.5 5.0 %collective-permute-start.22 = (bf16[2048,512]{1,0:T(8,128)(2,1)S(1)}, bf16[2048,512]{1,0:T(8,128)(2,1)S(1)}, u32[]{:S(2)}, u32[]{:S(2)}) collective-permute-start(bf16[2048,512]{1,0:T(8,128)(2,1)S(1)} %collective-permute-done.18.refs_1_), channel_id=1, source_target_pairs={{0,4},{1,5},{2,6},{3,7},{4,0},{5,1},{6,2},{7,3},{8,12},{9,13},{10,... | collective-permute-start | bytes 6291464 | tf_op jit(solution)/shard_map/ppermute | solution.py:104
  85.5 4.5 %collective-permute-start.19 = (bf16[128,1024]{1,0:T(8,128)(2,1)S(1)}, bf16[128,1024]{1,0:T(8,128)(2,1)S(1)}, u32[]{:S(2)}, u32[]{:S(2)}) collective-permute-start(bf16[128,1024]{1,0:T(8,128)(2,1)S(1)} %shard_map.61), channel_id=1, source_target_pairs={{0,4},{1,5},{2,6},{3,7},{4,0},{5,1},{6,2},{7,3},{8,12},{9,17},{10,... | collective-permute-start | bytes 786440 | tf_op jit(solution)/shard_map/ppermute | solution.py:104
  86.0 4.4 %collective-permute-start.21 = (bf16[128,1024]{1,0:T(8,128)(2,1)S(1)}, bf16[128,1024]{1,0:T(8,128)(2,1)S(1)}, u32[]{:S(2)}, u32[]{:S(2)}) collective-permute-start(bf16[128,1024]{1,0:T(8,128)(2,1)S(1)} %shard_map.61), channel_id=1, source_target_pairs={{0,4},{1,5},{2,6},{3,7},{4,0},{5,1},{6,2},{7,3},{8,12},{9,18},{10,... | collective-permute-start | bytes 786440 | tf_op jit(solution)/shard_map/ppermute | solution.py:104
  86.1 6.1 %collective-permute-start.23 = (bf16[128,1024]{1,0:T(8,128)(2,1)S(1)}, bf16[128,1024]{1,0:T(8,128)(2,1)S(1)}, u32[]{:S(2)}, u32[]{:S(2)}) collective-permute-start(bf16[128,1024]{1,0:T(8,128)(2,1)S(1)} %shard_map.62), channel_id=1, source_target_pairs={{0,4},{1,5},{2,6},{3,7},{4,0},{5,1},{6,2},{7,3},{8,12},{9,17},{10,... | collective-permute-start | bytes 786440 | tf_op jit(solution)/shard_map/ppermute | solution.py:104
  86.5 5.7 %collective-permute-start.24 = (bf16[128,1024]{1,0:T(8,128)(2,1)S(1)}, bf16[128,1024]{1,0:T(8,128)(2,1)S(1)}, u32[]{:S(2)}, u32[]{:S(2)}) collective-permute-start(bf16[128,1024]{1,0:T(8,128)(2,1)S(1)} %shard_map.62), channel_id=1, source_target_pairs={{0,4},{1,5},{2,6},{3,7},{4,0},{5,1},{6,2},{7,3},{8,12},{9,18},{10,... | collective-permute-start | bytes 786440 | tf_op jit(solution)/shard_map/ppermute | solution.py:104
  92.0 2.3 %collective-permute-start.25 = (bf16[128,1024]{1,0:T(8,128)(2,1)S(1)}, bf16[128,1024]{1,0:T(8,128)(2,1)S(1)}, u32[]{:S(2)}, u32[]{:S(2)}) collective-permute-start(bf16[128,1024]{1,0:T(8,128)(2,1)S(1)} %shard_map.63.own_ref), channel_id=1, source_target_pairs={{0,4},{1,5},{2,6},{3,7},{4,0},{5,1},{6,2},{7,3},{8,12},{9,21},{10,... | collective-permute-start | bytes 786440 | tf_op jit(solution)/shard_map/ppermute | solution.py:104
  93.9 2.6 %copy-start.4 = (bf16[128,1024]{1,0:T(8,128)(2,1)}, bf16[128,1024]{1,0:T(8,128)(2,1)S(1)}, u32[]{:S(2)}) copy-start(bf16[128,1024]{1,0:T(8,128)(2,1)S(1)} %shard_map.64.own_ref) | copy-start | bytes 786436
  93.9 2.6 %collective-permute-start.27 = (bf16[128,1024]{1,0:T(8,128)(2,1)S(1)}, bf16[128,1024]{1,0:T(8,128)(2,1)S(1)}, u32[]{:S(2)}, u32[]{:S(2)}) collective-permute-start(bf16[128,1024]{1,0:T(8,128)(2,1)S(1)} %shard_map.64.own_ref), channel_id=1, source_target_pairs={{0,4},{1,5},{2,6},{3,7},{4,0},{5,1},{6,2},{7,3},{8,12},{9,21},{10,... | collective-permute-start | bytes 786440 | tf_op jit(solution)/shard_map/ppermute | solution.py:104
  95.9 2.2 %copy-start.14 = (bf16[128,1024]{1,0:T(8,128)(2,1)}, bf16[128,1024]{1,0:T(8,128)(2,1)S(1)}, u32[]{:S(2)}) copy-start(bf16[128,1024]{1,0:T(8,128)(2,1)S(1)} %shard_map.65) | copy-start | bytes 786436
  95.9 15.3 %collective-permute-start.26 = (bf16[128,1024]{1,0:T(8,128)(2,1)S(1)}, bf16[128,1024]{1,0:T(8,128)(2,1)S(1)}, u32[]{:S(2)}, u32[]{:S(2)}) collective-permute-start(bf16[128,1024]{1,0:T(8,128)(2,1)S(1)} %shard_map.65), channel_id=1, source_target_pairs={{0,4},{1,9},{2,10},{3,7},{4,0},{5,1},{6,2},{7,3},{8,12},{9,13},{10... | collective-permute-start | bytes 786440 | tf_op jit(solution)/shard_map/ppermute | solution.py:104
  96.1 15.1 %collective-permute-start.28 = (bf16[128,1024]{1,0:T(8,128)(2,1)S(1)}, bf16[128,1024]{1,0:T(8,128)(2,1)S(1)}, u32[]{:S(2)}, u32[]{:S(2)}) collective-permute-start(bf16[128,1024]{1,0:T(8,128)(2,1)S(1)} %shard_map.65), channel_id=1, source_target_pairs={{0,4},{1,9},{2,10},{3,7},{4,0},{5,1},{6,2},{7,3},{8,12},{9,13},{10... | collective-permute-start | bytes 786440 | tf_op jit(solution)/shard_map/ppermute | solution.py:104
  98.1 15.4 %copy-start.16 = (bf16[128,1024]{1,0:T(8,128)(2,1)}, bf16[128,1024]{1,0:T(8,128)(2,1)S(1)}, u32[]{:S(2)}) copy-start(bf16[128,1024]{1,0:T(8,128)(2,1)S(1)} %shard_map.66) | copy-start | bytes 786436
  98.1 15.6 %collective-permute-start.29 = (bf16[128,1024]{1,0:T(8,128)(2,1)S(1)}, bf16[128,1024]{1,0:T(8,128)(2,1)S(1)}, u32[]{:S(2)}, u32[]{:S(2)}) collective-permute-start(bf16[128,1024]{1,0:T(8,128)(2,1)S(1)} %shard_map.66), channel_id=1, source_target_pairs={{0,4},{1,9},{2,10},{3,7},{4,0},{5,1},{6,2},{7,3},{8,12},{9,13},{10... | collective-permute-start | bytes 786440 | tf_op jit(solution)/shard_map/ppermute | solution.py:104
  98.3 15.4 %collective-permute-start.30 = (bf16[128,1024]{1,0:T(8,128)(2,1)S(1)}, bf16[128,1024]{1,0:T(8,128)(2,1)S(1)}, u32[]{:S(2)}, u32[]{:S(2)}) collective-permute-start(bf16[128,1024]{1,0:T(8,128)(2,1)S(1)} %shard_map.66), channel_id=1, source_target_pairs={{0,4},{1,9},{2,10},{3,7},{4,0},{5,1},{6,2},{7,3},{8,12},{9,13},{10... | collective-permute-start | bytes 786440 | tf_op jit(solution)/shard_map/ppermute | solution.py:104
  98.7 56.9 %collective-permute-start.34 = (bf16[2048,512]{1,0:T(8,128)(2,1)}, bf16[2048,512]{1,0:T(8,128)(2,1)}, u32[]{:S(2)}, u32[]{:S(2)}) collective-permute-start(bf16[2048,512]{1,0:T(8,128)(2,1)} %bitcast.5.refs_0_), channel_id=1, source_target_pairs={{0,1},{3,2},{4,5},{7,6},{8,9},{11,10},{12,13},{15,14},{16,17},{19,... | collective-permute-start | bytes 6291464 | tf_op jit(solution)/shard_map/ppermute | solution.py:104
  113.5 3.0 %collective-permute-start.31 = (bf16[128,1024]{1,0:T(8,128)(2,1)}, bf16[128,1024]{1,0:T(8,128)(2,1)}, u32[]{:S(2)}, u32[]{:S(2)}) collective-permute-start(bf16[128,1024]{1,0:T(8,128)(2,1)} %shard_map.67.own_ref), channel_id=1, source_target_pairs={{0,4},{1,29},{2,30},{3,7},{4,0},{5,6},{6,5},{7,3},{8,12},{9,13},{1... | collective-permute-start | bytes 786440 | tf_op jit(solution)/shard_map/ppermute | solution.py:104
  116.0 4.8 %collective-permute-start.36 = (bf16[128,1024]{1,0:T(8,128)(2,1)}, bf16[128,1024]{1,0:T(8,128)(2,1)}, u32[]{:S(2)}, u32[]{:S(2)}) collective-permute-start(bf16[128,1024]{1,0:T(8,128)(2,1)} %shard_map.68.own_ref), channel_id=1, source_target_pairs={{0,4},{1,29},{2,30},{3,7},{4,0},{5,6},{6,5},{7,3},{8,12},{9,13},{1... | collective-permute-start | bytes 786440 | tf_op jit(solution)/shard_map/ppermute | solution.py:104
  116.5 1.6 copy-start.2
  120.7 2.8 %copy-start.7 = (bf16[128,1024]{1,0:T(8,128)(2,1)S(1)}, bf16[128,1024]{1,0:T(8,128)(2,1)}, u32[]{:S(2)}) copy-start(bf16[128,1024]{1,0:T(8,128)(2,1)} %copy-done.6) | copy-start | bytes 786436
  120.7 2.8 %copy-start.11 = (bf16[128,1024]{1,0:T(8,128)(2,1)S(1)}, bf16[128,1024]{1,0:T(8,128)(2,1)}, u32[]{:S(2)}) copy-start(bf16[128,1024]{1,0:T(8,128)(2,1)} %copy-done.10) | copy-start | bytes 786436
  120.7 2.8 %copy-start.15 = (bf16[128,1024]{1,0:T(8,128)(2,1)S(1)}, bf16[128,1024]{1,0:T(8,128)(2,1)}, u32[]{:S(2)}) copy-start(bf16[128,1024]{1,0:T(8,128)(2,1)} %copy-done.14) | copy-start | bytes 786436
  120.7 2.9 %copy-start.9 = (bf16[128,1024]{1,0:T(8,128)(2,1)S(1)}, bf16[128,1024]{1,0:T(8,128)(2,1)}, u32[]{:S(2)}) copy-start(bf16[128,1024]{1,0:T(8,128)(2,1)} %copy-done.8) | copy-start | bytes 786436
  120.7 2.9 %copy-start.13 = (bf16[128,1024]{1,0:T(8,128)(2,1)S(1)}, bf16[128,1024]{1,0:T(8,128)(2,1)}, u32[]{:S(2)}) copy-start(bf16[128,1024]{1,0:T(8,128)(2,1)} %copy-done.12) | copy-start | bytes 786436
  120.7 2.9 %copy-start.17 = (bf16[128,1024]{1,0:T(8,128)(2,1)S(1)}, bf16[128,1024]{1,0:T(8,128)(2,1)}, u32[]{:S(2)}) copy-start(bf16[128,1024]{1,0:T(8,128)(2,1)} %copy-done.16) | copy-start | bytes 786436
  123.5 2.1 %copy-start.5 = (bf16[128,1024]{1,0:T(8,128)(2,1)S(1)}, bf16[128,1024]{1,0:T(8,128)(2,1)}, u32[]{:S(2)}) copy-start(bf16[128,1024]{1,0:T(8,128)(2,1)} %copy-done.4) | copy-start | bytes 786436
  123.5 2.1 %copy-start.19 = (bf16[256,1024]{1,0:T(8,128)(2,1)S(1)}, bf16[256,1024]{1,0:T(8,128)(2,1)}, u32[]{:S(2)}) copy-start(bf16[256,1024]{1,0:T(8,128)(2,1)} %copy-done.18) | copy-start | bytes 1572868
  123.7 1.6 collective-permute-start.37
  123.9 1.8 %collective-permute-start.32 = (bf16[128,1024]{1,0:T(8,128)(2,1)S(1)}, bf16[128,1024]{1,0:T(8,128)(2,1)S(1)}, u32[]{:S(2)}, u32[]{:S(2)}) collective-permute-start(bf16[128,1024]{1,0:T(8,128)(2,1)S(1)} %select_select_fusion.2), channel_id=1, source_target_pairs={{0,4},{1,5},{2,6},{3,7},{4,0},{5,1},{6,2},{7,3},{8,12},{9,13},{10,... | collective-permute-start | bytes 786440 | tf_op jit(solution)/shard_map/ppermute | solution.py:104
  126.0 29.6 %collective-permute-start.33 = (bf16[128,1024]{1,0:T(8,128)(2,1)S(1)}, bf16[128,1024]{1,0:T(8,128)(2,1)S(1)}, u32[]{:S(2)}, u32[]{:S(2)}) collective-permute-start(bf16[128,1024]{1,0:T(8,128)(2,1)S(1)} %get-tuple-element.57.own_ref), channel_id=1, source_target_pairs={{0,4},{1,2},{2,1},{3,7},{4,0},{5,6},{6,5},{7,3},{8,12},{9,10},{10,... | collective-permute-start | bytes 786440 | tf_op jit(solution)/shard_map/ppermute | solution.py:104
  127.3 33.5 %collective-permute-start.38 = (bf16[128,1024]{1,0:T(8,128)(2,1)S(1)}, bf16[128,1024]{1,0:T(8,128)(2,1)S(1)}, u32[]{:S(2)}, u32[]{:S(2)}) collective-permute-start(bf16[128,1024]{1,0:T(8,128)(2,1)S(1)} %get-tuple-element.58.own_ref), channel_id=1, source_target_pairs={{0,4},{1,2},{2,1},{3,7},{4,0},{5,6},{6,5},{7,3},{8,12},{9,10},{10,... | collective-permute-start | bytes 786440 | tf_op jit(solution)/shard_map/ppermute | solution.py:104
  158.2 5.7 %collective-permute-start.35 = (bf16[128,512]{1,0:T(8,128)(2,1)S(1)}, bf16[128,512]{1,0:T(8,128)(2,1)S(1)}, u32[]{:S(2)}, u32[]{:S(2)}) collective-permute-start(bf16[128,512]{1,0:T(8,128)(2,1)S(1)} %slice.56), channel_id=1, source_target_pairs={{0,1},{1,0},{3,2},{2,3},{4,5},{5,4},{7,6},{6,7},{8,9},{9,8},{11,10... | collective-permute-start | bytes 393224 | tf_op jit(solution)/shard_map/ppermute | solution.py:104
  163.4 5.0 %collective-permute-start.39 = (bf16[128,512]{1,0:T(8,128)(2,1)S(1)}, bf16[128,512]{1,0:T(8,128)(2,1)S(1)}, u32[]{:S(2)}, u32[]{:S(2)}) collective-permute-start(bf16[128,512]{1,0:T(8,128)(2,1)S(1)} %slice.58), channel_id=1, source_target_pairs={{0,1},{1,0},{3,2},{2,3},{4,5},{5,4},{7,6},{6,7},{8,9},{9,8},{11,10... | collective-permute-start | bytes 393224 | tf_op jit(solution)/shard_map/ppermute | solution.py:104

commit v2 on v1

--- a/solution.py
+++ b/solution.py
@@ -112,10 +112,33 @@
     return pieces if len(pieces) < 2 else [jnp.concatenate(pieces, 1)]
 
 
-def apply_kernel(width, pieces, own_ref, other_ref, *refs):
-    operators, rest = refs[:pieces], refs[pieces:]
-    add_ref = rest[0] if len(rest) > pieces + 2 else None
-    out_ref, tiles, sems = rest[-pieces - 2], rest[-pieces - 1:-1], rest[-1]
+def apply_kernel(width, pieces, extras, turn, own_ref, other_ref, *refs):
+    operators, rest = refs[:pieces], list(refs[pieces:])
+    named = {name: rest.pop(0) for name in extras}
+    out_ref = rest.pop(0)
+    kept_ref = rest.pop(0) if "kept" in extras else None
+    work = functools.partial(
+        multiply, width, own_ref, other_ref, operators, named.get("addend"), out_ref, kept_ref, rest[:-1], rest[-1]
+    )
+    if turn is None:
+        work()
+        return
+    z = lax.axis_index("trace")
+    ours = (z == width // 2 - 1) | (z == width // 2)
+    stage, columns = turn
+    if stage is not None:
+        slab = lax.axis_index("slab")
+        column = lax.div(slab, 2)
+        ours &= jnp.where(lax.rem(slab, 2) == 0, column, columns - 1 - column) == stage
+    pl.when(ours)(work)
+    if kept_ref is not None:
+        @pl.when(jnp.logical_not(ours))
+        def _():
+            kept_ref[...] = named["kept"][...]
+
+
+def multiply(width, own_ref, other_ref, operators, add_ref, out_ref, kept_ref, tiles, sems):
+    pieces = len(operators)
     depth = operators[0].shape[0] // width
     half = width // 2
     lower = lax.axis_index("trace") < half
@@ -144,38 +167,43 @@
         stop = start + total.shape[1]
         if add_ref is not None:
             total = total + add_ref[:, start:stop]
-        out_ref[:, start:stop] = total.astype(out_ref.dtype)
+        result = total.astype(out_ref.dtype)
+        out_ref[:, start:stop] = result
+        if kept_ref is not None:
+            kept_ref[:, start:stop] = result
         start = stop
 
 
-def applied(own, other, pieces, addend=None):
+def applied(own, other, pieces, addend=None, kept=None, turn=None):
     width = lax.axis_size("trace")
     rows = own.shape[0]
     deep = pieces[0].shape[0]
     columns = sum(piece.shape[1] for piece in pieces)
     vmem = pl.BlockSpec(memory_space=pltpu.VMEM)
     hbm = pl.BlockSpec(memory_space=pltpu.HBM)
-    addends = [] if addend is None else [addend]
+    extras = {name: value for name, value in (("addend", addend), ("kept", kept)) if value is not None}
+    outs = 1 if kept is None else 2
     return pl.pallas_call(
-        functools.partial(apply_kernel, width, len(pieces)),
-        out_shape=jax.ShapeDtypeStruct((rows, columns), jnp.bfloat16),
-        in_specs=[vmem, vmem] + [hbm] * len(pieces) + [vmem] * len(addends),
-        out_specs=vmem,
+        functools.partial(apply_kernel, width, len(pieces), tuple(extras), turn),
+        out_shape=[jax.ShapeDtypeStruct((rows, columns), jnp.bfloat16)] * outs,
+        in_specs=[vmem, vmem] + [hbm] * len(pieces) + [vmem] * len(extras),
+        out_specs=[vmem] * outs,
         scratch_shapes=[pltpu.VMEM((width, deep // width, piece.shape[1]), piece.dtype) for piece in pieces]
         + [pltpu.SemaphoreType.DMA((len(pieces), width))],
         compiler_params=pltpu.CompilerParams(vmem_limit_bytes=16 * 1024 * 1024),
         cost_estimate=pl.CostEstimate(
             flops=2 * rows * columns * deep, bytes_accessed=2 * columns * deep, transcendentals=0
         ),
-    )(own, other, *pieces, *addends)
-
-
-def in_turn(rows, pieces, addends, last):
-    results = []
-    for (own, other), addend in zip(rows, addends):
-        last = applied(after(own, last), other, pieces, addend)
-        results.append(last)
-    return results
+    )(own, other, *pieces, *extras.values())
+
+
+def in_turn(rows, pieces, addends, last, kept, turn):
+    fresh = []
+    for i, ((own, other), addend) in enumerate(zip(rows, addends)):
+        outs = applied(after(own, last), other, pieces, addend, kept[i] if kept else None, turn)
+        last = outs[0]
+        fresh.append(outs)
+    return [outs[0] for outs in fresh], [outs[-1] for outs in fresh]
 
 
 def shards(transmission, reflection, response, sources, placement):
@@ -187,8 +215,6 @@
     trace_count = lax.axis_size("trace")
     places = Places(lax.axis_size("slab"), trace_count)
     core = slab_index % 2
-    column = slab_index // 2
-    my_stage = jnp.where(core == 0, column, places.columns - 1 - column)
     hops = range(1, places.extra + 1)
 
     distance = jnp.abs(slab_index - placement).astype(jnp.float32)
@@ -217,7 +243,7 @@
         for hop, one_far, one_near in zip(hops, far_outward, near_outward):
             here = (z == places.ends(hop)[0][0]) | (z == places.ends(hop)[1][0])
             near, far = jnp.where(here, one_near, near), jnp.where(here, one_far, far)
-        driven_parts.append(applied(near, far, [response[0]]))
+        driven_parts += applied(near, far, [response[0]])
     driven_sent = jnp.concatenate(driven_parts, 0)
 
     transfer = transmission[0]
@@ -231,18 +257,12 @@
     late_source = after(transfer, first_driven)
     second_late = joined([move(late_source, places.inward_crossed(hop, False)) for hop in hops])
 
-    firsts, seconds = [], []
-
-    def chosen(stages, part):
-        result = stages[0][part]
-        for stage in range(1, places.columns):
-            result = jnp.where(my_stage == stage, stages[stage][part], result)
-        return result
-
     first_parts = split(first_driven)
     second_parts = split(move(first_driven, places.across_cores()))
     traces = first_parts
+    firsts, seconds = first_parts, None
     for stage in range(places.columns):
+        turn = (stage, places.columns)
         early = places.first_sender(stage) == 0
         second_pieces = [second_own] + (second_late if early else second_early)
         if stage:
@@ -251,13 +271,11 @@
             for part in traces:
                 crossed = move(part, places.hop(stage, True))
                 arrived.append((move(part, places.hop(stage, False)), crossed))
-            traces = in_turn(arrived, first_pieces, first_parts, traces[-1])
-        firsts.append(traces)
+            traces, firsts = in_turn(arrived, first_pieces, first_parts, traces[-1], firsts, turn)
         others = []
         for part in traces:
             others.append(move(part, places.swap(stage)))
-        traces = in_turn(list(zip(traces, others)), second_pieces, second_parts, traces[-1])
-        seconds.append(traces)
+        traces, seconds = in_turn(list(zip(traces, others)), second_pieces, second_parts, traces[-1], seconds, turn)
         if stage == 0:
             first_early = [move(after(piece, traces[-1]), places.across_cores()) for piece in second_early]
         if stage == min(1, places.columns - 1):
@@ -267,11 +285,13 @@
 
     outs = []
     for part in range(CHUNKS):
-        mine = chosen(firsts, part).astype(jnp.float32)
-        opposite = move(chosen(seconds, part), places.across_cores()).astype(jnp.float32)
+        mine = firsts[part].astype(jnp.float32)
+        opposite = move(seconds[part], places.across_cores()).astype(jnp.float32)
         contrast = jnp.where(core == 0, mine - opposite, opposite - mine).astype(jnp.bfloat16)
         other = move(contrast, places.swap_all())
-        combined = applied(contrast, other, [reflect] + reflect_rest, mine + opposite)
+        combined, = applied(
+            contrast, other, [reflect] + reflect_rest, mine + opposite, turn=(None, places.columns)
+        )
         own = combined[:, :trace_width]
         for hop in hops:
             piece = move(combined[:, hop * trace_width:(hop + 1) * trace_width], places.exchange_end(hop))

time: 169 us -> 151 us (0.89)
  Pallas kernels: 32.6 us -> 4.43 us
  waiting for transfers between devices: 84.6 us -> 91.7 us
  starting transfers between devices: 46.2 us -> 48.9 us
    pallas_call x18, Pallas kernels: 32.6 us -> 4.43 us  [applied(): pl.pallas_call(functools.partial(apply_kernel, width, len(pieces), tuple(...]
    ppermute x40, waiting for transfers between devices: 84.6 us -> 91.7 us  [move(): return lax.ppermute(values, AXES, pairs)]
    ppermute x40, starting transfers between devices: 46.2 us -> 48.9 us  [move(): return lax.ppermute(values, AXES, pairs)]
  transfers between devices with their start and end apart: 40 -> 40, of which waited for: 18 -> 24; matrix products, arithmetic and copies ran while one was open for 0% -> 1% of each run, Pallas kernels for 17% -> 3%
where the time goes in v2:
time: 151 us
  waiting for transfers between devices  91.7 us (61%)
  starting transfers between devices  48.9 us (32%)
  Pallas kernels  4.43 us (3%)
  other arithmetic  4.16 us (3%)
    ppermute x40, waiting for transfers between devices, move(): return lax.ppermute(values, AXES, pairs)  91.7 us
    ppermute x40, starting transfers between devices, move(): return lax.ppermute(values, AXES, pairs)  48.9 us
    pallas_call x18, Pallas kernels, applied(): pl.pallas_call(functools.partial(apply_kernel, width, len(pieces), tuple(...  4.43 us
  transfers between devices with their start and end apart: 40, of which 24 were waited for; matrix products, arithmetic and copies ran while one was open for 1% of the time, Pallas kernels for 3%

profile of v2, /device:TPU:0, one launch (start us, length us, event | category | flops | bytes accessed | tf_op | source)
XLA Modules:
  0.0 150.7 jit_solution(3254462762583191486)
XLA Ops:
  0.0 0.8 add_divide_fusion
  0.8 1.1 fusion.4
  1.9 3.1 %collective-permute-start.3 = (bf16[128,512]{1,0:T(8,128)(2,1)S(1)}, bf16[128,512]{1,0:T(8,128)(2,1)S(1)}, u32[]{:S(2)}, u32[]{:S(2)}) collective-permute-start(bf16[128,512]{1,0:T(8,128)(2,1)S(1)} %bitcast.25), channel_id=1, source_target_pairs={{0,1},{1,0},{3,2},{2,3},{4,5},{5,4},{7,6},{6,7},{8,9},{9,8},{11,10... | collective-permute-start | bytes 393224 | tf_op jit(solution)/shard_map/ppermute | solution.py:104
  5.1 3.5 %collective-permute-done.3 = bf16[128,512]{1,0:T(8,128)(2,1)S(1)} collective-permute-done((bf16[128,512]{1,0:T(8,128)(2,1)S(1)}, bf16[128,512]{1,0:T(8,128)(2,1)S(1)}, u32[]{:S(2)}, u32[]{:S(2)}) %collective-permute-start.3) | collective-permute-done | bytes 131104 | tf_op jit(solution)/shard_map/ppermute | solution.py:104
  8.7 3.3 %collective-permute-start = (bf16[128,512]{1,0:T(8,128)(2,1)S(1)}, bf16[128,512]{1,0:T(8,128)(2,1)S(1)}, u32[]{:S(2)}, u32[]{:S(2)}) collective-permute-start(bf16[128,512]{1,0:T(8,128)(2,1)S(1)} %bitcast.23), channel_id=1, source_target_pairs={{0,1},{1,0},{3,2},{2,3},{4,5},{5,4},{7,6},{6,7},{8,9},{9,8},{11,10... | collective-permute-start | bytes 393224 | tf_op jit(solution)/shard_map/ppermute | solution.py:104
  12.0 0.8 collective-permute-start.9
  12.8 1.4 collective-permute-start.8
  14.3 0.7 collective-permute-done
  15.2 1.3 collective-permute-start.5
  16.5 2.2 %collective-permute-done.1 = bf16[128,1024]{1,0:T(8,128)(2,1)S(1)} collective-permute-done((bf16[128,1024]{1,0:T(8,128)(2,1)S(1)}, bf16[128,1024]{1,0:T(8,128)(2,1)S(1)}, u32[]{:S(2)}, u32[]{:S(2)}) %collective-permute-start.1) | collective-permute-done | bytes 262176 | tf_op jit(solution)/shard_map/ppermute | solution.py:104
  18.6 1.3 collective-permute-start.2
  19.9 6.5 %collective-permute-done.5 = bf16[128,1024]{1,0:T(8,128)(2,1)S(1)} collective-permute-done((bf16[128,1024]{1,0:T(8,128)(2,1)S(1)}, bf16[128,1024]{1,0:T(8,128)(2,1)S(1)}, u32[]{:S(2)}, u32[]{:S(2)}) %collective-permute-start.5) | collective-permute-done | bytes 262176 | tf_op jit(solution)/shard_map/ppermute | solution.py:104
  26.4 0.8 shard_map.56
  27.2 4.1 %collective-permute-done.2 = bf16[128,1024]{1,0:T(8,128)(2,1)S(1)} collective-permute-done((bf16[128,1024]{1,0:T(8,128)(2,1)S(1)}, bf16[128,1024]{1,0:T(8,128)(2,1)S(1)}, u32[]{:S(2)}, u32[]{:S(2)}) %collective-permute-start.2) | collective-permute-done | bytes 262176 | tf_op jit(solution)/shard_map/ppermute | solution.py:104
  31.4 0.8 shard_map.55
  32.3 7.7 %collective-permute-done.6 = bf16[256,512]{1,0:T(8,128)(2,1)S(1)} collective-permute-done((bf16[256,512]{1,0:T(8,128)(2,1)S(1)}, bf16[256,512]{1,0:T(8,128)(2,1)S(1)}, u32[]{:S(2)}, u32[]{:S(2)}) %collective-permute-start.6) | collective-permute-done | bytes 262176 | tf_op jit(solution)/shard_map/ppermute | solution.py:104
  40.1 2.9 %collective-permute-start.10 = (bf16[256,1024]{1,0:T(8,128)(2,1)S(1)}, bf16[256,1024]{1,0:T(8,128)(2,1)S(1)}, u32[]{:S(2)}, u32[]{:S(2)}) collective-permute-start(bf16[256,1024]{1,0:T(8,128)(2,1)S(1)} %pad_maximum_fusion), channel_id=1, source_target_pairs={{0,4},{1,5},{2,6},{3,7},{4,0},{5,1},{6,2},{7,3},{8,12},{9,13},{10,... | collective-permute-start | bytes 1572872 | tf_op jit(solution)/shard_map/ppermute | solution.py:104
  43.1 0.5 collective-permute-start.12
  43.6 0.9 collective-permute-done.10
  44.6 0.3 collective-permute-done.7.other_ref
  45.0 0.3 collective-permute-done.12.other_ref
  45.3 0.4 collective-permute-start.14
  45.8 1.1 copy-done
  46.9 11.4 %collective-permute-start.18 = (bf16[2048,512]{1,0:T(8,128)(2,1)S(1)}, bf16[2048,512]{1,0:T(8,128)(2,1)S(1)}, u32[]{:S(2)}, u32[]{:S(2)}) collective-permute-start(bf16[2048,512]{1,0:T(8,128)(2,1)S(1)} %bitcast.11), channel_id=1, source_target_pairs={{0,5},{3,6},{12,9},{15,10},{16,21},{19,22},{28,25},{31,26}} | collective-permute-start | bytes 6291464 | tf_op jit(solution)/shard_map/ppermute | solution.py:104
  58.3 0.5 collective-permute-start.13
  58.9 1.0 collective-permute-done.11.own_ref
  59.9 0.1 collective-permute-start.16
  60.0 0.2 collective-permute-done.13.other_ref
  60.3 0.2 collective-permute-start.17
  60.6 0.8 collective-permute-done.16.other_ref
  61.5 0.2 collective-permute-start.20
  61.7 20.0 %collective-permute-done.18.refs_1_ = bf16[2048,512]{1,0:T(8,128)(2,1)S(1)} collective-permute-done((bf16[2048,512]{1,0:T(8,128)(2,1)S(1)}, bf16[2048,512]{1,0:T(8,128)(2,1)S(1)}, u32[]{:S(2)}, u32[]{:S(2)}) %collective-permute-start.18) | collective-permute-done | bytes 2097184 | tf_op jit(solution)/shard_map/ppermute | solution.py:104
  82.0 0.5 collective-permute-start.19
  82.6 0.4 collective-permute-start.23
  83.1 3.4 %collective-permute-done.19.own_ref = bf16[128,1024]{1,0:T(8,128)(2,1)S(1)} collective-permute-done((bf16[128,1024]{1,0:T(8,128)(2,1)S(1)}, bf16[128,1024]{1,0:T(8,128)(2,1)S(1)}, u32[]{:S(2)}, u32[]{:S(2)}) %collective-permute-start.19) | collective-permute-done | bytes 262176 | tf_op jit(solution)/shard_map/ppermute | solution.py:104
  86.5 5.2 %collective-permute-start.34 = (bf16[2048,512]{1,0:T(8,128)(2,1)S(1)}, bf16[2048,512]{1,0:T(8,128)(2,1)}, u32[]{:S(2)}, u32[]{:S(2)}) collective-permute-start(bf16[2048,512]{1,0:T(8,128)(2,1)S(1)} %bitcast.20), channel_id=1, source_target_pairs={{0,1},{3,2},{4,5},{7,6},{8,9},{11,10},{12,13},{15,14},{16,17},{19,... | collective-permute-start | bytes 6291464 | tf_op jit(solution)/shard_map/ppermute | solution.py:104
  91.8 0.2 collective-permute-start.25
  92.1 0.5 collective-permute-start.27
  92.6 0.9 collective-permute-done.25.other_ref
  93.5 0.2 collective-permute-start.28
  93.7 0.4 collective-permute-start.26
  94.2 0.2 collective-permute-start.29
  94.4 0.4 collective-permute-start.30
  94.7 0.7 collective-permute-done.26.own_ref
  95.6 0.3 collective-permute-done.29.own_ref
  95.9 0.4 collective-permute-done.30.other_ref
  96.3 0.2 collective-permute-start.36
  96.5 0.4 collective-permute-start.31
  96.9 1.0 collective-permute-done.36.other_ref
  97.9 0.8 shard_map.71
  98.7 0.2 collective-permute-start.37
  98.9 0.8 shard_map.69
  99.7 0.4 collective-permute-start.32
  100.2 0.2 collective-permute-done.37
  100.3 0.1 convert_add_fusion
  100.4 0.2 collective-permute-start.38
  100.6 0.8 collective-permute-done.32
  101.5 1.1 convert_add_fusion.1
  102.5 0.4 collective-permute-start.33
  103.0 32.8 %collective-permute-done.34.refs_1_ = bf16[2048,512]{1,0:T(8,128)(2,1)} collective-permute-done((bf16[2048,512]{1,0:T(8,128)(2,1)S(1)}, bf16[2048,512]{1,0:T(8,128)(2,1)}, u32[]{:S(2)}, u32[]{:S(2)}) %collective-permute-start.34) | collective-permute-done | bytes 2097184 | tf_op jit(solution)/shard_map/ppermute | solution.py:104
  135.9 6.5 %collective-permute-start.39 = (bf16[128,512]{1,0:T(8,128)(2,1)S(1)}, bf16[128,512]{1,0:T(8,128)(2,1)S(1)}, u32[]{:S(2)}, u32[]{:S(2)}) collective-permute-start(bf16[128,512]{1,0:T(8,128)(2,1)S(1)} %slice.58), channel_id=1, source_target_pairs={{0,1},{1,0},{3,2},{2,3},{4,5},{5,4},{7,6},{6,7},{8,9},{9,8},{11,10... | collective-permute-start | bytes 393224 | tf_op jit(solution)/shard_map/ppermute | solution.py:104
  142.4 4.6 %collective-permute-start.35 = (bf16[128,512]{1,0:T(8,128)(2,1)S(1)}, bf16[128,512]{1,0:T(8,128)(2,1)S(1)}, u32[]{:S(2)}, u32[]{:S(2)}) collective-permute-start(bf16[128,512]{1,0:T(8,128)(2,1)S(1)} %slice.56), channel_id=1, source_target_pairs={{0,1},{1,0},{3,2},{2,3},{4,5},{5,4},{7,6},{6,7},{8,9},{9,8},{11,10... | collective-permute-start | bytes 393224 | tf_op jit(solution)/shard_map/ppermute | solution.py:104
  147.0 2.9 %collective-permute-done.35 = bf16[128,512]{1,0:T(8,128)(2,1)S(1)} collective-permute-done((bf16[128,512]{1,0:T(8,128)(2,1)S(1)}, bf16[128,512]{1,0:T(8,128)(2,1)S(1)}, u32[]{:S(2)}, u32[]{:S(2)}) %collective-permute-start.35) | collective-permute-done | bytes 131104 | tf_op jit(solution)/shard_map/ppermute | solution.py:104
  150.0 0.7 pad_maximum_fusion.4
  (58 shorter events, 2.4 us)
Async XLA Ops:
  0.0 26.4 %copy-start.1 = (bf16[1,2048,512]{2,1,0:T(8,128)(2,1)S(1)}, bf16[1,2048,512]{2,1,0:T(8,128)(2,1)}, u32[]{:S(2)}) copy-start(bf16[1,2048,512]{2,1,0:T(8,128)(2,1)} %param.7) | copy-start | bytes 6291460
  1.9 6.6 %collective-permute-start.3 = (bf16[128,512]{1,0:T(8,128)(2,1)S(1)}, bf16[128,512]{1,0:T(8,128)(2,1)S(1)}, u32[]{:S(2)}, u32[]{:S(2)}) collective-permute-start(bf16[128,512]{1,0:T(8,128)(2,1)S(1)} %bitcast.25), channel_id=1, source_target_pairs={{0,1},{1,0},{3,2},{2,3},{4,5},{5,4},{7,6},{6,7},{8,9},{9,8},{11,10... | collective-permute-start | bytes 393224 | tf_op jit(solution)/shard_map/ppermute | solution.py:104
  8.7 6.5 %collective-permute-start.4 = (bf16[128,1024]{1,0:T(8,128)(2,1)S(1)}, bf16[128,1024]{1,0:T(8,128)(2,1)S(1)}, u32[]{:S(2)}, u32[]{:S(2)}) collective-permute-start(bf16[128,1024]{1,0:T(8,128)(2,1)S(1)} %get-tuple-element.95), channel_id=1, source_target_pairs={{0,4},{1,2},{2,1},{3,7},{4,0},{5,6},{6,5},{7,3},{8,12},{9,10},{10,... | collective-permute-start | bytes 786440 | tf_op jit(solution)/shard_map/ppermute | solution.py:104
  8.7 6.2 %collective-permute-start = (bf16[128,512]{1,0:T(8,128)(2,1)S(1)}, bf16[128,512]{1,0:T(8,128)(2,1)S(1)}, u32[]{:S(2)}, u32[]{:S(2)}) collective-permute-start(bf16[128,512]{1,0:T(8,128)(2,1)S(1)} %bitcast.23), channel_id=1, source_target_pairs={{0,1},{1,0},{3,2},{2,3},{4,5},{5,4},{7,6},{6,7},{8,9},{9,8},{11,10... | collective-permute-start | bytes 393224 | tf_op jit(solution)/shard_map/ppermute | solution.py:104
  12.0 32.9 %collective-permute-start.9 = (bf16[2048,512]{1,0:T(8,128)(2,1)}, bf16[2048,512]{1,0:T(8,128)(2,1)S(1)}, u32[]{:S(2)}, u32[]{:S(2)}) collective-permute-start(bf16[2048,512]{1,0:T(8,128)(2,1)} %bitcast.9), channel_id=1, source_target_pairs={{4,1},{7,2},{8,13},{11,14},{20,17},{23,18},{24,29},{27,30}} | collective-permute-start | bytes 6291464 | tf_op jit(solution)/shard_map/ppermute | solution.py:104
  12.8 32.1 %collective-permute-start.8 = (bf16[2048,512]{1,0:T(8,128)(2,1)}, bf16[2048,512]{1,0:T(8,128)(2,1)S(1)}, u32[]{:S(2)}, u32[]{:S(2)}) collective-permute-start(bf16[2048,512]{1,0:T(8,128)(2,1)} %bitcast.10), channel_id=1, source_target_pairs={{0,4},{1,5},{2,6},{3,7},{4,0},{5,1},{6,2},{7,3},{8,12},{9,13},{10,... | collective-permute-start | bytes 6291464 | tf_op jit(solution)/shard_map/ppermute | solution.py:104
  15.1 3.5 %collective-permute-start.1 = (bf16[128,1024]{1,0:T(8,128)(2,1)S(1)}, bf16[128,1024]{1,0:T(8,128)(2,1)S(1)}, u32[]{:S(2)}, u32[]{:S(2)}) collective-permute-start(bf16[128,1024]{1,0:T(8,128)(2,1)S(1)} %get-tuple-element.91), channel_id=1, source_target_pairs={{0,4},{1,2},{2,1},{3,7},{4,0},{5,6},{6,5},{7,3},{8,12},{9,10},{10,... | collective-permute-start | bytes 786440 | tf_op jit(solution)/shard_map/ppermute | solution.py:104
  15.2 11.2 %collective-permute-start.5 = (bf16[128,1024]{1,0:T(8,128)(2,1)S(1)}, bf16[128,1024]{1,0:T(8,128)(2,1)S(1)}, u32[]{:S(2)}, u32[]{:S(2)}) collective-permute-start(bf16[128,1024]{1,0:T(8,128)(2,1)S(1)} %collective-permute-done.4), channel_id=1, source_target_pairs={{1,0},{2,3},{5,4},{6,7},{9,8},{10,11},{13,12},{14,15},{17,16},{18,... | collective-permute-start | bytes 786440 | tf_op jit(solution)/shard_map/ppermute | solution.py:104
  18.6 12.7 %collective-permute-start.2 = (bf16[128,1024]{1,0:T(8,128)(2,1)S(1)}, bf16[128,1024]{1,0:T(8,128)(2,1)S(1)}, u32[]{:S(2)}, u32[]{:S(2)}) collective-permute-start(bf16[128,1024]{1,0:T(8,128)(2,1)S(1)} %collective-permute-done.1), channel_id=1, source_target_pairs={{1,0},{2,3},{5,4},{6,7},{9,8},{10,11},{13,12},{14,15},{17,16},{18,... | collective-permute-start | bytes 786440 | tf_op jit(solution)/shard_map/ppermute | solution.py:104
  32.3 7.8 %collective-permute-start.6 = (bf16[256,512]{1,0:T(8,128)(2,1)S(1)}, bf16[256,512]{1,0:T(8,128)(2,1)S(1)}, u32[]{:S(2)}, u32[]{:S(2)}) collective-permute-start(bf16[256,512]{1,0:T(8,128)(2,1)S(1)} %pad_maximum_fusion.3), channel_id=1, source_target_pairs={{0,1},{1,0},{3,2},{2,3},{4,5},{5,4},{7,6},{6,7},{8,9},{9,8},{11,10... | collective-permute-start | bytes 786440 | tf_op jit(solution)/shard_map/ppermute | solution.py:104
  40.1 4.4 %collective-permute-start.10 = (bf16[256,1024]{1,0:T(8,128)(2,1)S(1)}, bf16[256,1024]{1,0:T(8,128)(2,1)S(1)}, u32[]{:S(2)}, u32[]{:S(2)}) collective-permute-start(bf16[256,1024]{1,0:T(8,128)(2,1)S(1)} %pad_maximum_fusion), channel_id=1, source_target_pairs={{0,4},{1,5},{2,6},{3,7},{4,0},{5,1},{6,2},{7,3},{8,12},{9,13},{10,... | collective-permute-start | bytes 1572872 | tf_op jit(solution)/shard_map/ppermute | solution.py:104
  43.0 1.9 %collective-permute-start.7 = (bf16[128,1024]{1,0:T(8,128)(2,1)S(1)}, bf16[128,1024]{1,0:T(8,128)(2,1)S(1)}, u32[]{:S(2)}, u32[]{:S(2)}) collective-permute-start(bf16[128,1024]{1,0:T(8,128)(2,1)S(1)} %get-tuple-element.89.refs_2_.refs_3_), channel_id=1, source_target_pairs={{0,4},{1,2},{2,1},{3,7},{4,0},{5,25},{6,26},{7,3},{8,12},{9,13},{1... | collective-permute-start | bytes 786440 | tf_op jit(solution)/shard_map/ppermute | solution.py:104
  43.1 2.2 %collective-permute-start.12 = (bf16[128,1024]{1,0:T(8,128)(2,1)S(1)}, bf16[128,1024]{1,0:T(8,128)(2,1)S(1)}, u32[]{:S(2)}, u32[]{:S(2)}) collective-permute-start(bf16[128,1024]{1,0:T(8,128)(2,1)S(1)} %get-tuple-element.45.own_ref.refs_2_.refs_3_), channel_id=1, source_target_pairs={{0,4},{1,2},{2,1},{3,7},{4,0},{5,25},{6,26},{7,3},{8,12},{9,13},{1... | collective-permute-start | bytes 786440 | tf_op jit(solution)/shard_map/ppermute | solution.py:104
  45.3 1.6 %copy-start = (bf16[1,2048,512]{2,1,0:T(8,128)(2,1)S(1)}, bf16[1,2048,512]{2,1,0:T(8,128)(2,1)}, u32[]{:S(2)}) copy-start(bf16[1,2048,512]{2,1,0:T(8,128)(2,1)} %param.5) | copy-start | bytes 6291460
  45.3 14.9 %collective-permute-start.14 = (bf16[2048,512]{1,0:T(8,128)(2,1)S(1)}, bf16[2048,512]{1,0:T(8,128)(2,1)S(1)}, u32[]{:S(2)}, u32[]{:S(2)}) collective-permute-start(bf16[2048,512]{1,0:T(8,128)(2,1)S(1)} %collective-permute-done.9.refs_1_), channel_id=1, source_target_pairs={{0,4},{1,5},{2,6},{3,7},{4,0},{5,1},{6,2},{7,3},{8,12},{9,13},{10,... | collective-permute-start | bytes 6291464 | tf_op jit(solution)/shard_map/ppermute | solution.py:104
  46.9 34.8 %collective-permute-start.18 = (bf16[2048,512]{1,0:T(8,128)(2,1)S(1)}, bf16[2048,512]{1,0:T(8,128)(2,1)S(1)}, u32[]{:S(2)}, u32[]{:S(2)}) collective-permute-start(bf16[2048,512]{1,0:T(8,128)(2,1)S(1)} %bitcast.11), channel_id=1, source_target_pairs={{0,5},{3,6},{12,9},{15,10},{16,21},{19,22},{28,25},{31,26}} | collective-permute-start | bytes 6291464 | tf_op jit(solution)/shard_map/ppermute | solution.py:104
  58.3 1.6 %collective-permute-start.11 = (bf16[128,1024]{1,0:T(8,128)(2,1)S(1)}, bf16[128,1024]{1,0:T(8,128)(2,1)S(1)}, u32[]{:S(2)}, u32[]{:S(2)}) collective-permute-start(bf16[128,1024]{1,0:T(8,128)(2,1)S(1)} %shard_map.57.refs_3_), channel_id=1, source_target_pairs={{0,4},{1,9},{2,10},{3,7},{4,0},{5,1},{6,2},{7,3},{8,12},{9,13},{10... | collective-permute-start | bytes 786440 | tf_op jit(solution)/shard_map/ppermute | solution.py:104
  58.3 1.9 %collective-permute-start.13 = (bf16[128,1024]{1,0:T(8,128)(2,1)S(1)}, bf16[128,1024]{1,0:T(8,128)(2,1)S(1)}, u32[]{:S(2)}, u32[]{:S(2)}) collective-permute-start(bf16[128,1024]{1,0:T(8,128)(2,1)S(1)} %shard_map.57.refs_3_), channel_id=1, source_target_pairs={{0,4},{1,10},{2,9},{3,7},{4,0},{5,1},{6,2},{7,3},{8,12},{9,13},{10... | collective-permute-start | bytes 786440 | tf_op jit(solution)/shard_map/ppermute | solution.py:104
  58.8 1.8 %collective-permute-start.15 = (bf16[128,1024]{1,0:T(8,128)(2,1)S(1)}, bf16[128,1024]{1,0:T(8,128)(2,1)S(1)}, u32[]{:S(2)}, u32[]{:S(2)}) collective-permute-start(bf16[128,1024]{1,0:T(8,128)(2,1)S(1)} %shard_map.58.refs_3_), channel_id=1, source_target_pairs={{0,4},{1,9},{2,10},{3,7},{4,0},{5,1},{6,2},{7,3},{8,12},{9,13},{10... | collective-permute-start | bytes 786440 | tf_op jit(solution)/shard_map/ppermute | solution.py:104
  59.9 1.5 %collective-permute-start.16 = (bf16[128,1024]{1,0:T(8,128)(2,1)S(1)}, bf16[128,1024]{1,0:T(8,128)(2,1)S(1)}, u32[]{:S(2)}, u32[]{:S(2)}) collective-permute-start(bf16[128,1024]{1,0:T(8,128)(2,1)S(1)} %shard_map.58.refs_3_), channel_id=1, source_target_pairs={{0,4},{1,10},{2,9},{3,7},{4,0},{5,1},{6,2},{7,3},{8,12},{9,13},{10... | collective-permute-start | bytes 786440 | tf_op jit(solution)/shard_map/ppermute | solution.py:104
  60.3 21.3 %collective-permute-start.17 = (bf16[128,1024]{1,0:T(8,128)(2,1)S(1)}, bf16[128,1024]{1,0:T(8,128)(2,1)S(1)}, u32[]{:S(2)}, u32[]{:S(2)}) collective-permute-start(bf16[128,1024]{1,0:T(8,128)(2,1)S(1)} %get-tuple-element.51.own_ref), channel_id=1, source_target_pairs={{0,4},{1,5},{2,6},{3,7},{4,0},{5,1},{6,2},{7,3},{8,12},{9,10},{10,... | collective-permute-start | bytes 786440 | tf_op jit(solution)/shard_map/ppermute | solution.py:104
  61.5 20.3 %collective-permute-start.20 = (bf16[128,1024]{1,0:T(8,128)(2,1)S(1)}, bf16[128,1024]{1,0:T(8,128)(2,1)S(1)}, u32[]{:S(2)}, u32[]{:S(2)}) collective-permute-start(bf16[128,1024]{1,0:T(8,128)(2,1)S(1)} %get-tuple-element.54.own_ref), channel_id=1, source_target_pairs={{0,4},{1,5},{2,6},{3,7},{4,0},{5,1},{6,2},{7,3},{8,12},{9,10},{10,... | collective-permute-start | bytes 786440 | tf_op jit(solution)/shard_map/ppermute | solution.py:104
  81.8 4.7 %copy-start.2 = (bf16[1,2048,512]{2,1,0:T(8,128)(2,1)S(1)}, bf16[1,2048,512]{2,1,0:T(8,128)(2,1)}, u32[]{:S(2)}) copy-start(bf16[1,2048,512]{2,1,0:T(8,128)(2,1)} %param.6) | copy-start | bytes 6291460
  81.9 9.8 %collective-permute-start.22 = (bf16[2048,512]{1,0:T(8,128)(2,1)S(1)}, bf16[2048,512]{1,0:T(8,128)(2,1)S(1)}, u32[]{:S(2)}, u32[]{:S(2)}) collective-permute-start(bf16[2048,512]{1,0:T(8,128)(2,1)S(1)} %collective-permute-done.18.refs_1_), channel_id=1, source_target_pairs={{0,4},{1,5},{2,6},{3,7},{4,0},{5,1},{6,2},{7,3},{8,12},{9,13},{10,... | collective-permute-start | bytes 6291464 | tf_op jit(solution)/shard_map/ppermute | solution.py:104
  82.0 4.5 %collective-permute-start.19 = (bf16[128,1024]{1,0:T(8,128)(2,1)S(1)}, bf16[128,1024]{1,0:T(8,128)(2,1)S(1)}, u32[]{:S(2)}, u32[]{:S(2)}) collective-permute-start(bf16[128,1024]{1,0:T(8,128)(2,1)S(1)} %get-tuple-element.53), channel_id=1, source_target_pairs={{0,4},{1,5},{2,6},{3,7},{4,0},{5,1},{6,2},{7,3},{8,12},{9,17},{10,... | collective-permute-start | bytes 786440 | tf_op jit(solution)/shard_map/ppermute | solution.py:104
  82.5 9.2 %collective-permute-start.21 = (bf16[128,1024]{1,0:T(8,128)(2,1)S(1)}, bf16[128,1024]{1,0:T(8,128)(2,1)S(1)}, u32[]{:S(2)}, u32[]{:S(2)}) collective-permute-start(bf16[128,1024]{1,0:T(8,128)(2,1)S(1)} %get-tuple-element.53), channel_id=1, source_target_pairs={{0,4},{1,5},{2,6},{3,7},{4,0},{5,1},{6,2},{7,3},{8,12},{9,18},{10,... | collective-permute-start | bytes 786440 | tf_op jit(solution)/shard_map/ppermute | solution.py:104
  82.6 9.4 %collective-permute-start.23 = (bf16[128,1024]{1,0:T(8,128)(2,1)S(1)}, bf16[128,1024]{1,0:T(8,128)(2,1)S(1)}, u32[]{:S(2)}, u32[]{:S(2)}) collective-permute-start(bf16[128,1024]{1,0:T(8,128)(2,1)S(1)} %get-tuple-element.55), channel_id=1, source_target_pairs={{0,4},{1,5},{2,6},{3,7},{4,0},{5,1},{6,2},{7,3},{8,12},{9,17},{10,... | collective-permute-start | bytes 786440 | tf_op jit(solution)/shard_map/ppermute | solution.py:104
  83.0 9.0 %collective-permute-start.24 = (bf16[128,1024]{1,0:T(8,128)(2,1)S(1)}, bf16[128,1024]{1,0:T(8,128)(2,1)S(1)}, u32[]{:S(2)}, u32[]{:S(2)}) collective-permute-start(bf16[128,1024]{1,0:T(8,128)(2,1)S(1)} %get-tuple-element.55), channel_id=1, source_target_pairs={{0,4},{1,5},{2,6},{3,7},{4,0},{5,1},{6,2},{7,3},{8,12},{9,18},{10,... | collective-permute-start | bytes 786440 | tf_op jit(solution)/shard_map/ppermute | solution.py:104
  86.5 49.2 %collective-permute-start.34 = (bf16[2048,512]{1,0:T(8,128)(2,1)S(1)}, bf16[2048,512]{1,0:T(8,128)(2,1)}, u32[]{:S(2)}, u32[]{:S(2)}) collective-permute-start(bf16[2048,512]{1,0:T(8,128)(2,1)S(1)} %bitcast.20), channel_id=1, source_target_pairs={{0,1},{3,2},{4,5},{7,6},{8,9},{11,10},{12,13},{15,14},{16,17},{19,... | collective-permute-start | bytes 6291464 | tf_op jit(solution)/shard_map/ppermute | solution.py:104
  91.8 1.6 %collective-permute-start.25 = (bf16[128,1024]{1,0:T(8,128)(2,1)S(1)}, bf16[128,1024]{1,0:T(8,128)(2,1)S(1)}, u32[]{:S(2)}, u32[]{:S(2)}) collective-permute-start(bf16[128,1024]{1,0:T(8,128)(2,1)S(1)} %get-tuple-element.63.own_ref), channel_id=1, source_target_pairs={{0,4},{1,5},{2,6},{3,7},{4,0},{5,1},{6,2},{7,3},{8,12},{9,21},{10,... | collective-permute-start | bytes 786440 | tf_op jit(solution)/shard_map/ppermute | solution.py:104
  92.1 2.0 %collective-permute-start.27 = (bf16[128,1024]{1,0:T(8,128)(2,1)S(1)}, bf16[128,1024]{1,0:T(8,128)(2,1)S(1)}, u32[]{:S(2)}, u32[]{:S(2)}) collective-permute-start(bf16[128,1024]{1,0:T(8,128)(2,1)S(1)} %get-tuple-element.66.own_ref), channel_id=1, source_target_pairs={{0,4},{1,5},{2,6},{3,7},{4,0},{5,1},{6,2},{7,3},{8,12},{9,21},{10,... | collective-permute-start | bytes 786440 | tf_op jit(solution)/shard_map/ppermute | solution.py:104
  93.5 2.0 %collective-permute-start.28 = (bf16[128,1024]{1,0:T(8,128)(2,1)S(1)}, bf16[128,1024]{1,0:T(8,128)(2,1)S(1)}, u32[]{:S(2)}, u32[]{:S(2)}) collective-permute-start(bf16[128,1024]{1,0:T(8,128)(2,1)S(1)} %get-tuple-element.65), channel_id=1, source_target_pairs={{0,4},{1,9},{2,10},{3,7},{4,0},{5,1},{6,2},{7,3},{8,12},{9,13},{10... | collective-permute-start | bytes 786440 | tf_op jit(solution)/shard_map/ppermute | solution.py:104
  93.7 1.8 %collective-permute-start.26 = (bf16[128,1024]{1,0:T(8,128)(2,1)S(1)}, bf16[128,1024]{1,0:T(8,128)(2,1)S(1)}, u32[]{:S(2)}, u32[]{:S(2)}) collective-permute-start(bf16[128,1024]{1,0:T(8,128)(2,1)S(1)} %get-tuple-element.65), channel_id=1, source_target_pairs={{0,4},{1,9},{2,10},{3,7},{4,0},{5,1},{6,2},{7,3},{8,12},{9,13},{10... | collective-permute-start | bytes 786440 | tf_op jit(solution)/shard_map/ppermute | solution.py:104
  94.2 1.7 %collective-permute-start.29 = (bf16[128,1024]{1,0:T(8,128)(2,1)S(1)}, bf16[128,1024]{1,0:T(8,128)(2,1)S(1)}, u32[]{:S(2)}, u32[]{:S(2)}) collective-permute-start(bf16[128,1024]{1,0:T(8,128)(2,1)S(1)} %get-tuple-element.68), channel_id=1, source_target_pairs={{0,4},{1,9},{2,10},{3,7},{4,0},{5,1},{6,2},{7,3},{8,12},{9,13},{10... | collective-permute-start | bytes 786440 | tf_op jit(solution)/shard_map/ppermute | solution.py:104
  94.4 1.9 %collective-permute-start.30 = (bf16[128,1024]{1,0:T(8,128)(2,1)S(1)}, bf16[128,1024]{1,0:T(8,128)(2,1)S(1)}, u32[]{:S(2)}, u32[]{:S(2)}) collective-permute-start(bf16[128,1024]{1,0:T(8,128)(2,1)S(1)} %get-tuple-element.68), channel_id=1, source_target_pairs={{0,4},{1,9},{2,10},{3,7},{4,0},{5,1},{6,2},{7,3},{8,12},{9,13},{10... | collective-permute-start | bytes 786440 | tf_op jit(solution)/shard_map/ppermute | solution.py:104
  96.3 1.6 %collective-permute-start.36 = (bf16[128,1024]{1,0:T(8,128)(2,1)S(1)}, bf16[128,1024]{1,0:T(8,128)(2,1)S(1)}, u32[]{:S(2)}, u32[]{:S(2)}) collective-permute-start(bf16[128,1024]{1,0:T(8,128)(2,1)S(1)} %get-tuple-element.75.own_ref), channel_id=1, source_target_pairs={{0,4},{1,29},{2,30},{3,7},{4,0},{5,6},{6,5},{7,3},{8,12},{9,13},{1... | collective-permute-start | bytes 786440 | tf_op jit(solution)/shard_map/ppermute | solution.py:104
  96.5 2.4 %collective-permute-start.31 = (bf16[128,1024]{1,0:T(8,128)(2,1)S(1)}, bf16[128,1024]{1,0:T(8,128)(2,1)S(1)}, u32[]{:S(2)}, u32[]{:S(2)}) collective-permute-start(bf16[128,1024]{1,0:T(8,128)(2,1)S(1)} %get-tuple-element.76.own_ref), channel_id=1, source_target_pairs={{0,4},{1,29},{2,30},{3,7},{4,0},{5,6},{6,5},{7,3},{8,12},{9,13},{1... | collective-permute-start | bytes 786440 | tf_op jit(solution)/shard_map/ppermute | solution.py:104
  98.7 1.6 %collective-permute-start.37 = (bf16[128,1024]{1,0:T(8,128)(2,1)S(1)}, bf16[128,1024]{1,0:T(8,128)(2,1)S(1)}, u32[]{:S(2)}, u32[]{:S(2)}) collective-permute-start(bf16[128,1024]{1,0:T(8,128)(2,1)S(1)} %get-tuple-element.82), channel_id=1, source_target_pairs={{0,4},{1,5},{2,6},{3,7},{4,0},{5,1},{6,2},{7,3},{8,12},{9,13},{10,... | collective-permute-start | bytes 786440 | tf_op jit(solution)/shard_map/ppermute | solution.py:104
  99.7 1.7 %collective-permute-start.32 = (bf16[128,1024]{1,0:T(8,128)(2,1)S(1)}, bf16[128,1024]{1,0:T(8,128)(2,1)}, u32[]{:S(2)}, u32[]{:S(2)}) collective-permute-start(bf16[128,1024]{1,0:T(8,128)(2,1)S(1)} %get-tuple-element.78), channel_id=1, source_target_pairs={{0,4},{1,5},{2,6},{3,7},{4,0},{5,1},{6,2},{7,3},{8,12},{9,13},{10,... | collective-permute-start | bytes 786440 | tf_op jit(solution)/shard_map/ppermute | solution.py:104
  100.4 35.3 %collective-permute-start.38 = (bf16[128,1024]{1,0:T(8,128)(2,1)S(1)}, bf16[128,1024]{1,0:T(8,128)(2,1)S(1)}, u32[]{:S(2)}, u32[]{:S(2)}) collective-permute-start(bf16[128,1024]{1,0:T(8,128)(2,1)S(1)} %get-tuple-element.86.own_ref), channel_id=1, source_target_pairs={{0,4},{1,2},{2,1},{3,7},{4,0},{5,6},{6,5},{7,3},{8,12},{9,10},{10,... | collective-permute-start | bytes 786440 | tf_op jit(solution)/shard_map/ppermute | solution.py:104
  102.5 39.8 %collective-permute-start.33 = (bf16[128,1024]{1,0:T(8,128)(2,1)S(1)}, bf16[128,1024]{1,0:T(8,128)(2,1)S(1)}, u32[]{:S(2)}, u32[]{:S(2)}) collective-permute-start(bf16[128,1024]{1,0:T(8,128)(2,1)S(1)} %get-tuple-element.84.own_ref), channel_id=1, source_target_pairs={{0,4},{1,2},{2,1},{3,7},{4,0},{5,6},{6,5},{7,3},{8,12},{9,10},{10,... | collective-permute-start | bytes 786440 | tf_op jit(solution)/shard_map/ppermute | solution.py:104
  135.9 11.2 %collective-permute-start.39 = (bf16[128,512]{1,0:T(8,128)(2,1)S(1)}, bf16[128,512]{1,0:T(8,128)(2,1)S(1)}, u32[]{:S(2)}, u32[]{:S(2)}) collective-permute-start(bf16[128,512]{1,0:T(8,128)(2,1)S(1)} %slice.58), channel_id=1, source_target_pairs={{0,1},{1,0},{3,2},{2,3},{4,5},{5,4},{7,6},{6,7},{8,9},{9,8},{11,10... | collective-permute-start | bytes 393224 | tf_op jit(solution)/shard_map/ppermute | solution.py:104
  142.4 7.5 %collective-permute-start.35 = (bf16[128,512]{1,0:T(8,128)(2,1)S(1)}, bf16[128,512]{1,0:T(8,128)(2,1)S(1)}, u32[]{:S(2)}, u32[]{:S(2)}) collective-permute-start(bf16[128,512]{1,0:T(8,128)(2,1)S(1)} %slice.56), channel_id=1, source_target_pairs={{0,1},{1,0},{3,2},{2,3},{4,5},{5,4},{7,6},{6,7},{8,9},{9,8},{11,10... | collective-permute-start | bytes 393224 | tf_op jit(solution)/shard_map/ppermute | solution.py:104

commit v3 on v2

--- a/solution.py
+++ b/solution.py
@@ -82,6 +82,29 @@
             (self.at(c, k, end), self.at(c, k, holder))
             for c in range(self.columns) for k in (0, 1) for end, holder in self.ends(hop)
         ]
+
+    def crossed_partners(self, moves, zs):
+        (ca, ka), (cb, kb) = self.working(0)
+        for z in zs:
+            moves[self.at(ca, 1 - ka, z)] = self.at(cb, 1 - kb, z)
+            moves[self.at(cb, 1 - kb, z)] = self.at(ca, 1 - ka, z)
+        return list(moves.items())
+
+    def swap_settled(self):
+        moves = dict(self.swap_all())
+        (ca, ka), (cb, kb) = self.working(0)
+        for z in self.holders:
+            moves[self.at(ca, ka, z)] = self.at(cb, kb, z)
+            moves[self.at(cb, kb, z)] = self.at(ca, ka, z)
+        return list(moves.items())
+
+    def exchange_end_last(self, hop):
+        moves = self.partner_map()
+        for end, holder in self.ends(hop):
+            for c, k in self.working(0):
+                moves[self.at(c, k, end)] = self.at(c, k, holder)
+                moves[self.at(c, k, holder)] = self.at(c, k, end)
+        return self.crossed_partners(moves, [z for pair in self.ends(hop) for z in pair])
 
     def outward(self, hop):
         return [(holder, end) for end, holder in self.inward(hop)]
@@ -125,11 +148,10 @@
         return
     z = lax.axis_index("trace")
     ours = (z == width // 2 - 1) | (z == width // 2)
-    stage, columns = turn
-    if stage is not None:
-        slab = lax.axis_index("slab")
-        column = lax.div(slab, 2)
-        ours &= jnp.where(lax.rem(slab, 2) == 0, column, columns - 1 - column) == stage
+    stage, columns, there = turn
+    slab = lax.axis_index("slab")
+    column = lax.div(slab, 2)
+    ours &= (jnp.where(lax.rem(slab, 2) == 0, column, columns - 1 - column) == stage) == there
     pl.when(ours)(work)
     if kept_ref is not None:
         @pl.when(jnp.logical_not(ours))
@@ -262,9 +284,12 @@
     traces = first_parts
     firsts, seconds = first_parts, None
     for stage in range(places.columns):
-        turn = (stage, places.columns)
+        turn = (stage, places.columns, True)
         early = places.first_sender(stage) == 0
         second_pieces = [second_own] + (second_late if early else second_early)
+        final = stage == places.columns - 1
+        if final:
+            settled = seconds
         if stage:
             first_pieces = [transfer] + (first_early if early else first_late)
             arrived = []
@@ -272,6 +297,10 @@
                 crossed = move(part, places.hop(stage, True))
                 arrived.append((move(part, places.hop(stage, False)), crossed))
             traces, firsts = in_turn(arrived, first_pieces, first_parts, traces[-1], firsts, turn)
+        if final:
+            given = []
+            for part in settled:
+                given.append(move(after(part, traces[-1]), places.across_cores()))
         others = []
         for part in traces:
             others.append(move(part, places.swap(stage)))
@@ -283,19 +312,52 @@
             reflect_source = after(reflect, traces[-1])
             reflect_rest = joined([move(reflect_source, places.inward(hop)) for hop in hops])
 
+    def contrasts(ours, theirs):
+        pairs = [(mine.astype(jnp.float32), other.astype(jnp.float32)) for mine, other in zip(ours, theirs)]
+        return [
+            (jnp.where(core == 0, mine - other, other - mine).astype(jnp.bfloat16), mine + other)
+            for mine, other in pairs
+        ]
+
+    def swapped(rows, pairs):
+        result = []
+        for contrast, _ in rows:
+            result.append(move(contrast, pairs))
+        return result
+
+    def sent_out(combined, pairs_of):
+        result = []
+        for rows in combined:
+            result.append([
+                move(rows[:, hop * trace_width:(hop + 1) * trace_width], pairs_of(hop)) for hop in hops
+            ])
+        return result
+
+    reflect_pieces = [reflect] + reflect_rest
+    settled_rows = contrasts(firsts, given)
+    settled_others = swapped(settled_rows, places.swap_settled())
+    last_given = []
+    for part in seconds:
+        last_given.append(move(part, places.across_cores()))
+    last_rows = contrasts([after(mine, other) for mine, other in zip(firsts, last_given)], last_given)
+    last_others = swapped(last_rows, places.swap(0))
+    combined = []
+    for (contrast, total), other in zip(settled_rows, settled_others):
+        combined += applied(
+            after(contrast, traces[-1]), other, reflect_pieces, total, turn=(0, places.columns, False)
+        )
+    settled_out = sent_out(combined, places.exchange_end)
+    complete = []
+    for (contrast, total), other, kept in zip(last_rows, last_others, combined):
+        complete.append(applied(contrast, other, reflect_pieces, total, kept, (0, places.columns, True))[-1])
+    last_out = sent_out(complete, places.exchange_end_last)
+    in_last = (slab_index == 0) | (slab_index == 2 * places.columns - 1)
     outs = []
-    for part in range(CHUNKS):
-        mine = firsts[part].astype(jnp.float32)
-        opposite = move(seconds[part], places.across_cores()).astype(jnp.float32)
-        contrast = jnp.where(core == 0, mine - opposite, opposite - mine).astype(jnp.bfloat16)
-        other = move(contrast, places.swap_all())
-        combined, = applied(
-            contrast, other, [reflect] + reflect_rest, mine + opposite, turn=(None, places.columns)
-        )
-        own = combined[:, :trace_width]
-        for hop in hops:
-            piece = move(combined[:, hop * trace_width:(hop + 1) * trace_width], places.exchange_end(hop))
-            own = jnp.where((z == places.ends(hop)[0][0]) | (z == places.ends(hop)[1][0]), piece, own)
+    for rows, from_settled, from_last in zip(complete, settled_out, last_out):
+        own = rows[:, :trace_width]
+        for hop, one, other in zip(hops, from_settled, from_last):
+            here = (z == places.ends(hop)[0][0]) | (z == places.ends(hop)[1][0])
+            own = jnp.where(here, jnp.where(in_last, other, one), own)
         outs.append(own)
     return jnp.concatenate(outs, 0).reshape(1, tick_count, batch_count, trace_width)
 

time: 151 us -> 157 us (1.040)
  Pallas kernels: 4.43 us -> 8.61 us
  local copies, waits for them, and re-layouts: 1.19 us -> 4.6 us
  waiting for transfers between devices: 91.7 us -> 88.9 us
    pallas_call x18 -> x20, Pallas kernels: 4.43 us -> 8.61 us  [applied(): pl.pallas_call(functools.partial(apply_kernel, width, len(pieces), tuple(...]
    unnamed x6 -> x12, local copies, waits for them, and re-layouts: 1.08 us -> 4.47 us
    ppermute x40 -> x46, waiting for transfers between devices: 91.7 us -> 88.9 us  [move(): return lax.ppermute(values, AXES, pairs)]
    ppermute x40 -> x46, starting transfers between devices: 48.9 us -> 48.5 us  [move(): return lax.ppermute(values, AXES, pairs)]
  transfers between devices with their start and end apart: 40 -> 46, of which waited for: 24 -> 24; matrix products, arithmetic and copies ran while one was open for 1% -> 1% of each run, Pallas kernels for 3% -> 5%
where the time goes in v3:
time: 157 us; the launch traced here: 155 us
  waiting for transfers between devices  88.9 us (57%)
  starting transfers between devices  48.5 us (31%)
  Pallas kernels  8.61 us (5%)
  local copies, waits for them, and re-layouts  4.6 us (3%)
  other arithmetic  4.25 us (3%)
    ppermute x46, waiting for transfers between devices, move(): return lax.ppermute(values, AXES, pairs)  88.9 us
    ppermute x46, starting transfers between devices, move(): return lax.ppermute(values, AXES, pairs)  48.5 us
    pallas_call x20, Pallas kernels, applied(): pl.pallas_call(functools.partial(apply_kernel, width, len(pieces), tuple(...  8.61 us
    unnamed x12, local copies, waits for them, and re-layouts  4.47 us
  transfers between devices with their start and end apart: 46, of which 24 were waited for; matrix products, arithmetic and copies ran while one was open for 1% of the time, Pallas kernels for 5%

profile of v3, /device:TPU:0, one launch (start us, length us, event | category | flops | bytes accessed | tf_op | source)
XLA Modules:
  0.0 155.3 jit_solution(17148776741933476403)
XLA Ops:
  0.0 0.7 add_divide_fusion
  0.7 1.1 fusion.8
  1.8 3.1 %collective-permute-start = (bf16[128,512]{1,0:T(8,128)(2,1)S(1)}, bf16[128,512]{1,0:T(8,128)(2,1)S(1)}, u32[]{:S(2)}, u32[]{:S(2)}) collective-permute-start(bf16[128,512]{1,0:T(8,128)(2,1)S(1)} %bitcast.22), channel_id=1, source_target_pairs={{0,1},{1,0},{3,2},{2,3},{4,5},{5,4},{7,6},{6,7},{8,9},{9,8},{11,10... | collective-permute-start | bytes 393224 | tf_op jit(solution)/shard_map/ppermute | solution.py:127
  4.9 3.5 %collective-permute-done = bf16[128,512]{1,0:T(8,128)(2,1)S(1)} collective-permute-done((bf16[128,512]{1,0:T(8,128)(2,1)S(1)}, bf16[128,512]{1,0:T(8,128)(2,1)S(1)}, u32[]{:S(2)}, u32[]{:S(2)}) %collective-permute-start) | collective-permute-done | bytes 131104 | tf_op jit(solution)/shard_map/ppermute | solution.py:127
  8.6 3.3 %collective-permute-start.3 = (bf16[128,512]{1,0:T(8,128)(2,1)S(1)}, bf16[128,512]{1,0:T(8,128)(2,1)S(1)}, u32[]{:S(2)}, u32[]{:S(2)}) collective-permute-start(bf16[128,512]{1,0:T(8,128)(2,1)S(1)} %bitcast.20), channel_id=1, source_target_pairs={{0,1},{1,0},{3,2},{2,3},{4,5},{5,4},{7,6},{6,7},{8,9},{9,8},{11,10... | collective-permute-start | bytes 393224 | tf_op jit(solution)/shard_map/ppermute | solution.py:127
  11.9 0.8 collective-permute-start.9
  12.7 2.1 %collective-permute-done.3 = bf16[128,512]{1,0:T(8,128)(2,1)S(1)} collective-permute-done((bf16[128,512]{1,0:T(8,128)(2,1)S(1)}, bf16[128,512]{1,0:T(8,128)(2,1)S(1)}, u32[]{:S(2)}, u32[]{:S(2)}) %collective-permute-start.3) | collective-permute-done | bytes 131104 | tf_op jit(solution)/shard_map/ppermute | solution.py:127
  15.0 1.3 collective-permute-start.2
  16.3 0.3 collective-permute-done.4
  16.6 1.3 collective-permute-start.5
  17.9 8.3 %collective-permute-done.2 = bf16[128,1024]{1,0:T(8,128)(2,1)S(1)} collective-permute-done((bf16[128,1024]{1,0:T(8,128)(2,1)S(1)}, bf16[128,1024]{1,0:T(8,128)(2,1)S(1)}, u32[]{:S(2)}, u32[]{:S(2)}) %collective-permute-start.2) | collective-permute-done | bytes 262176 | tf_op jit(solution)/shard_map/ppermute | solution.py:127
  26.3 0.8 shard_map.55
  27.1 4.1 %collective-permute-done.5 = bf16[128,1024]{1,0:T(8,128)(2,1)S(1)} collective-permute-done((bf16[128,1024]{1,0:T(8,128)(2,1)S(1)}, bf16[128,1024]{1,0:T(8,128)(2,1)S(1)}, u32[]{:S(2)}, u32[]{:S(2)}) %collective-permute-start.5) | collective-permute-done | bytes 262176 | tf_op jit(solution)/shard_map/ppermute | solution.py:127
  31.3 0.8 shard_map.56
  32.2 7.7 %collective-permute-done.6 = bf16[256,512]{1,0:T(8,128)(2,1)S(1)} collective-permute-done((bf16[256,512]{1,0:T(8,128)(2,1)S(1)}, bf16[256,512]{1,0:T(8,128)(2,1)S(1)}, u32[]{:S(2)}, u32[]{:S(2)}) %collective-permute-start.6) | collective-permute-done | bytes 262176 | tf_op jit(solution)/shard_map/ppermute | solution.py:127
  39.9 2.9 %collective-permute-start.10 = (bf16[256,1024]{1,0:T(8,128)(2,1)S(1)}, bf16[256,1024]{1,0:T(8,128)(2,1)S(1)}, u32[]{:S(2)}, u32[]{:S(2)}) collective-permute-start(bf16[256,1024]{1,0:T(8,128)(2,1)S(1)} %pad_maximum_fusion), channel_id=1, source_target_pairs={{0,4},{1,5},{2,6},{3,7},{4,0},{5,1},{6,2},{7,3},{8,12},{9,13},{10,... | collective-permute-start | bytes 1572872 | tf_op jit(solution)/shard_map/ppermute | solution.py:127
  43.0 0.5 collective-permute-start.12
  43.4 0.9 collective-permute-done.10
  44.4 0.3 collective-permute-done.7.other_ref
  44.8 0.3 collective-permute-done.12.other_ref
  45.2 0.4 collective-permute-start.14
  45.6 1.1 copy-done
  46.7 11.9 %collective-permute-start.18 = (bf16[2048,512]{1,0:T(8,128)(2,1)S(1)}, bf16[2048,512]{1,0:T(8,128)(2,1)S(1)}, u32[]{:S(2)}, u32[]{:S(2)}) collective-permute-start(bf16[2048,512]{1,0:T(8,128)(2,1)S(1)} %bitcast.11), channel_id=1, source_target_pairs={{0,5},{3,6},{12,9},{15,10},{16,21},{19,22},{28,25},{31,26}} | collective-permute-start | bytes 6291464 | tf_op jit(solution)/shard_map/ppermute | solution.py:127
  58.7 0.5 collective-permute-start.13
  59.3 1.0 collective-permute-done.11.own_ref
  60.4 0.2 collective-permute-done.13.other_ref
  60.7 0.2 collective-permute-start.17
  61.0 0.8 collective-permute-done.16.other_ref
  61.9 0.2 collective-permute-start.20
  62.1 20.0 %collective-permute-done.18.refs_1_ = bf16[2048,512]{1,0:T(8,128)(2,1)S(1)} collective-permute-done((bf16[2048,512]{1,0:T(8,128)(2,1)S(1)}, bf16[2048,512]{1,0:T(8,128)(2,1)S(1)}, u32[]{:S(2)}, u32[]{:S(2)}) %collective-permute-start.18) | collective-permute-done | bytes 2097184 | tf_op jit(solution)/shard_map/ppermute | solution.py:127
  82.3 1.1 copy-done.1
  83.4 0.5 collective-permute-start.19
  83.9 0.5 collective-permute-start.23
  84.4 3.5 %collective-permute-done.19.own_ref = bf16[128,1024]{1,0:T(8,128)(2,1)S(1)} collective-permute-done((bf16[128,1024]{1,0:T(8,128)(2,1)S(1)}, bf16[128,1024]{1,0:T(8,128)(2,1)S(1)}, u32[]{:S(2)}, u32[]{:S(2)}) %collective-permute-start.19) | collective-permute-done | bytes 262176 | tf_op jit(solution)/shard_map/ppermute | solution.py:127
  87.9 0.4 collective-permute-done.21.other_ref
  88.4 0.2 collective-permute-start.25
  88.7 0.4 collective-permute-done.24.other_ref
  89.2 0.2 collective-permute-start.27
  89.4 5.4 %collective-permute-start.34 = (bf16[2048,512]{1,0:T(8,128)(2,1)}, bf16[2048,512]{1,0:T(8,128)(2,1)}, u32[]{:S(2)}, u32[]{:S(2)}) collective-permute-start(bf16[2048,512]{1,0:T(8,128)(2,1)} %bitcast.5.refs_0_), channel_id=1, source_target_pairs={{0,1},{3,2},{4,5},{7,6},{8,9},{11,10},{12,13},{15,14},{16,17},{19,... | collective-permute-start | bytes 6291464 | tf_op jit(solution)/shard_map/ppermute | solution.py:127
  94.8 0.8 shard_map.65
  95.6 0.5 collective-permute-start.28
  96.4 0.4 collective-permute-start.30
  96.8 0.4 collective-permute-done.26.own_ref
  97.2 0.4 collective-permute-done.28.other_ref
  97.5 0.8 shard_map.67
  98.5 0.7 copy-done.4
  99.3 0.4 collective-permute-start.31
  99.8 0.4 collective-permute-start.42
  100.2 0.9 collective-permute-done.35
  101.1 1.1 convert_add_fusion.2
  102.3 1.6 %copy-done.2 = bf16[2048,512]{1,0:T(8,128)(2,1)S(1)} copy-done((bf16[2048,512]{1,0:T(8,128)(2,1)S(1)}, bf16[2048,512]{1,0:T(8,128)(2,1)}, u32[]{:S(2)}) %copy-start.2) | copy-done | bytes 2097176
  103.9 1.9 %shard_map.69 = (bf16[128,1024]{1,0:T(8,128)(2,1)}, bf16[128,1024]{1,0:T(8,128)(2,1)S(1)}) custom-call(bf16[128,1024]{1,0:T(8,128)(2,1)} %get-tuple-element.85.own_ref, bf16[128,1024]{1,0:T(8,128)(2,1)} %collective-permute-done.31.other_ref, bf16[2048,512]{1,0:T(8,128)(2,1)S(1)} %collective-permute-done.8.refs_0_, bf16[2048,512]{1,0:T(8,128)(2,1)S(1)} %copy-done.2, ...), custom_call_target="tpu_custom_call" | custom-call | flops 536870912 | bytes 4194304 | tf_op jit(solution)/shard_map/pallas_call | solution.py:208
  105.9 0.4 collective-permute-start.32
  106.3 0.8 shard_map.70
  107.5 0.4 collective-permute-start.43
  108.2 0.5 collective-permute-done.40
  109.1 29.9 %collective-permute-done.34.refs_1_ = bf16[2048,512]{1,0:T(8,128)(2,1)} collective-permute-done((bf16[2048,512]{1,0:T(8,128)(2,1)}, bf16[2048,512]{1,0:T(8,128)(2,1)}, u32[]{:S(2)}, u32[]{:S(2)}) %collective-permute-start.34) | collective-permute-done | bytes 2097184 | tf_op jit(solution)/shard_map/ppermute | solution.py:127
  139.0 2.5 %collective-permute-start.39 = (bf16[128,512]{1,0:T(8,128)(2,1)S(1)}, bf16[128,512]{1,0:T(8,128)(2,1)S(1)}, u32[]{:S(2)}, u32[]{:S(2)}) collective-permute-start(bf16[128,512]{1,0:T(8,128)(2,1)S(1)} %slice.64), channel_id=1, source_target_pairs={{0,1},{1,0},{3,2},{2,3},{4,5},{5,4},{7,6},{6,7},{8,9},{9,8},{11,10... | collective-permute-start | bytes 393224 | tf_op jit(solution)/shard_map/ppermute | solution.py:127
  141.6 0.8 shard_map.72
  142.4 3.7 %collective-permute-start.38 = (bf16[128,512]{1,0:T(8,128)(2,1)S(1)}, bf16[128,512]{1,0:T(8,128)(2,1)S(1)}, u32[]{:S(2)}, u32[]{:S(2)}) collective-permute-start(bf16[128,512]{1,0:T(8,128)(2,1)S(1)} %slice.52), channel_id=1, source_target_pairs={{0,1},{1,0},{2,3},{3,2},{4,24},{5,25},{6,26},{7,27},{8,12},{9,13},... | collective-permute-start | bytes 393224 | tf_op jit(solution)/shard_map/ppermute | solution.py:127
  146.3 0.8 shard_map.74
  147.1 4.5 %collective-permute-start.44 = (bf16[128,512]{1,0:T(8,128)(2,1)S(1)}, bf16[128,512]{1,0:T(8,128)(2,1)S(1)}, u32[]{:S(2)}, u32[]{:S(2)}) collective-permute-start(bf16[128,512]{1,0:T(8,128)(2,1)S(1)} %slice.55), channel_id=1, source_target_pairs={{0,1},{1,0},{2,3},{3,2},{4,24},{5,25},{6,26},{7,27},{8,12},{9,13},... | collective-permute-start | bytes 393224 | tf_op jit(solution)/shard_map/ppermute | solution.py:127
  151.7 2.9 %collective-permute-done.44 = bf16[128,512]{1,0:T(8,128)(2,1)S(1)} collective-permute-done((bf16[128,512]{1,0:T(8,128)(2,1)S(1)}, bf16[128,512]{1,0:T(8,128)(2,1)S(1)}, u32[]{:S(2)}, u32[]{:S(2)}) %collective-permute-start.44) | collective-permute-done | bytes 131104 | tf_op jit(solution)/shard_map/ppermute | solution.py:127
  154.6 0.7 pad_maximum_fusion.4
  (82 shorter events, 4.1 us)
Async XLA Ops:
  1.8 6.6 %collective-permute-start = (bf16[128,512]{1,0:T(8,128)(2,1)S(1)}, bf16[128,512]{1,0:T(8,128)(2,1)S(1)}, u32[]{:S(2)}, u32[]{:S(2)}) collective-permute-start(bf16[128,512]{1,0:T(8,128)(2,1)S(1)} %bitcast.22), channel_id=1, source_target_pairs={{0,1},{1,0},{3,2},{2,3},{4,5},{5,4},{7,6},{6,7},{8,9},{9,8},{11,10... | collective-permute-start | bytes 393224 | tf_op jit(solution)/shard_map/ppermute | solution.py:127
  4.9 21.4 %copy-start.3 = (bf16[1,2048,512]{2,1,0:T(8,128)(2,1)S(1)}, bf16[1,2048,512]{2,1,0:T(8,128)(2,1)}, u32[]{:S(2)}) copy-start(bf16[1,2048,512]{2,1,0:T(8,128)(2,1)} %param.7) | copy-start | bytes 6291460
  8.5 6.5 %collective-permute-start.1 = (bf16[128,1024]{1,0:T(8,128)(2,1)S(1)}, bf16[128,1024]{1,0:T(8,128)(2,1)S(1)}, u32[]{:S(2)}, u32[]{:S(2)}) collective-permute-start(bf16[128,1024]{1,0:T(8,128)(2,1)S(1)} %get-tuple-element.113), channel_id=1, source_target_pairs={{0,4},{1,2},{2,1},{3,7},{4,0},{5,6},{6,5},{7,3},{8,12},{9,10},{10,... | collective-permute-start | bytes 786440 | tf_op jit(solution)/shard_map/ppermute | solution.py:127
  8.6 6.2 %collective-permute-start.3 = (bf16[128,512]{1,0:T(8,128)(2,1)S(1)}, bf16[128,512]{1,0:T(8,128)(2,1)S(1)}, u32[]{:S(2)}, u32[]{:S(2)}) collective-permute-start(bf16[128,512]{1,0:T(8,128)(2,1)S(1)} %bitcast.20), channel_id=1, source_target_pairs={{0,1},{1,0},{3,2},{2,3},{4,5},{5,4},{7,6},{6,7},{8,9},{9,8},{11,10... | collective-permute-start | bytes 393224 | tf_op jit(solution)/shard_map/ppermute | solution.py:127
  11.9 32.9 %collective-permute-start.8 = (bf16[2048,512]{1,0:T(8,128)(2,1)}, bf16[2048,512]{1,0:T(8,128)(2,1)S(1)}, u32[]{:S(2)}, u32[]{:S(2)}) collective-permute-start(bf16[2048,512]{1,0:T(8,128)(2,1)} %bitcast.9), channel_id=1, source_target_pairs={{0,4},{1,5},{2,6},{3,7},{4,0},{5,1},{6,2},{7,3},{8,12},{9,13},{10,... | collective-permute-start | bytes 6291464 | tf_op jit(solution)/shard_map/ppermute | solution.py:127
  11.9 32.9 %collective-permute-start.9 = (bf16[2048,512]{1,0:T(8,128)(2,1)}, bf16[2048,512]{1,0:T(8,128)(2,1)S(1)}, u32[]{:S(2)}, u32[]{:S(2)}) collective-permute-start(bf16[2048,512]{1,0:T(8,128)(2,1)} %bitcast.10), channel_id=1, source_target_pairs={{4,1},{7,2},{8,13},{11,14},{20,17},{23,18},{24,29},{27,30}} | collective-permute-start | bytes 6291464 | tf_op jit(solution)/shard_map/ppermute | solution.py:127
  14.9 1.7 %collective-permute-start.4 = (bf16[128,1024]{1,0:T(8,128)(2,1)S(1)}, bf16[128,1024]{1,0:T(8,128)(2,1)S(1)}, u32[]{:S(2)}, u32[]{:S(2)}) collective-permute-start(bf16[128,1024]{1,0:T(8,128)(2,1)S(1)} %get-tuple-element.117), channel_id=1, source_target_pairs={{0,4},{1,2},{2,1},{3,7},{4,0},{5,6},{6,5},{7,3},{8,12},{9,10},{10,... | collective-permute-start | bytes 786440 | tf_op jit(solution)/shard_map/ppermute | solution.py:127
  15.0 11.2 %collective-permute-start.2 = (bf16[128,1024]{1,0:T(8,128)(2,1)S(1)}, bf16[128,1024]{1,0:T(8,128)(2,1)S(1)}, u32[]{:S(2)}, u32[]{:S(2)}) collective-permute-start(bf16[128,1024]{1,0:T(8,128)(2,1)S(1)} %collective-permute-done.1), channel_id=1, source_target_pairs={{1,0},{2,3},{5,4},{6,7},{9,8},{10,11},{13,12},{14,15},{17,16},{18,... | collective-permute-start | bytes 786440 | tf_op jit(solution)/shard_map/ppermute | solution.py:127
  16.6 14.6 %collective-permute-start.5 = (bf16[128,1024]{1,0:T(8,128)(2,1)S(1)}, bf16[128,1024]{1,0:T(8,128)(2,1)S(1)}, u32[]{:S(2)}, u32[]{:S(2)}) collective-permute-start(bf16[128,1024]{1,0:T(8,128)(2,1)S(1)} %collective-permute-done.4), channel_id=1, source_target_pairs={{1,0},{2,3},{5,4},{6,7},{9,8},{10,11},{13,12},{14,15},{17,16},{18,... | collective-permute-start | bytes 786440 | tf_op jit(solution)/shard_map/ppermute | solution.py:127
  32.1 7.8 %collective-permute-start.6 = (bf16[256,512]{1,0:T(8,128)(2,1)S(1)}, bf16[256,512]{1,0:T(8,128)(2,1)S(1)}, u32[]{:S(2)}, u32[]{:S(2)}) collective-permute-start(bf16[256,512]{1,0:T(8,128)(2,1)S(1)} %pad_maximum_fusion.3), channel_id=1, source_target_pairs={{0,1},{1,0},{3,2},{2,3},{4,5},{5,4},{7,6},{6,7},{8,9},{9,8},{11,10... | collective-permute-start | bytes 786440 | tf_op jit(solution)/shard_map/ppermute | solution.py:127
  39.9 4.4 %collective-permute-start.10 = (bf16[256,1024]{1,0:T(8,128)(2,1)S(1)}, bf16[256,1024]{1,0:T(8,128)(2,1)S(1)}, u32[]{:S(2)}, u32[]{:S(2)}) collective-permute-start(bf16[256,1024]{1,0:T(8,128)(2,1)S(1)} %pad_maximum_fusion), channel_id=1, source_target_pairs={{0,4},{1,5},{2,6},{3,7},{4,0},{5,1},{6,2},{7,3},{8,12},{9,13},{10,... | collective-permute-start | bytes 1572872 | tf_op jit(solution)/shard_map/ppermute | solution.py:127
  42.9 1.9 %collective-permute-start.7 = (bf16[128,1024]{1,0:T(8,128)(2,1)S(1)}, bf16[128,1024]{1,0:T(8,128)(2,1)S(1)}, u32[]{:S(2)}, u32[]{:S(2)}) collective-permute-start(bf16[128,1024]{1,0:T(8,128)(2,1)S(1)} %get-tuple-element.111.refs_2_.refs_3_), channel_id=1, source_target_pairs={{0,4},{1,2},{2,1},{3,7},{4,0},{5,25},{6,26},{7,3},{8,12},{9,13},{1... | collective-permute-start | bytes 786440 | tf_op jit(solution)/shard_map/ppermute | solution.py:127
  43.0 2.2 %collective-permute-start.12 = (bf16[128,1024]{1,0:T(8,128)(2,1)S(1)}, bf16[128,1024]{1,0:T(8,128)(2,1)S(1)}, u32[]{:S(2)}, u32[]{:S(2)}) collective-permute-start(bf16[128,1024]{1,0:T(8,128)(2,1)S(1)} %get-tuple-element.54.own_ref.refs_2_.refs_3_), channel_id=1, source_target_pairs={{0,4},{1,2},{2,1},{3,7},{4,0},{5,25},{6,26},{7,3},{8,12},{9,13},{1... | collective-permute-start | bytes 786440 | tf_op jit(solution)/shard_map/ppermute | solution.py:127
  45.1 1.6 %copy-start = (bf16[1,2048,512]{2,1,0:T(8,128)(2,1)S(1)}, bf16[1,2048,512]{2,1,0:T(8,128)(2,1)}, u32[]{:S(2)}) copy-start(bf16[1,2048,512]{2,1,0:T(8,128)(2,1)} %param.5) | copy-start | bytes 6291460
  45.2 15.4 %collective-permute-start.14 = (bf16[2048,512]{1,0:T(8,128)(2,1)S(1)}, bf16[2048,512]{1,0:T(8,128)(2,1)S(1)}, u32[]{:S(2)}, u32[]{:S(2)}) collective-permute-start(bf16[2048,512]{1,0:T(8,128)(2,1)S(1)} %collective-permute-done.9.refs_1_), channel_id=1, source_target_pairs={{0,4},{1,5},{2,6},{3,7},{4,0},{5,1},{6,2},{7,3},{8,12},{9,13},{10,... | collective-permute-start | bytes 6291464 | tf_op jit(solution)/shard_map/ppermute | solution.py:127
  46.7 35.4 %collective-permute-start.18 = (bf16[2048,512]{1,0:T(8,128)(2,1)S(1)}, bf16[2048,512]{1,0:T(8,128)(2,1)S(1)}, u32[]{:S(2)}, u32[]{:S(2)}) collective-permute-start(bf16[2048,512]{1,0:T(8,128)(2,1)S(1)} %bitcast.11), channel_id=1, source_target_pairs={{0,5},{3,6},{12,9},{15,10},{16,21},{19,22},{28,25},{31,26}} | collective-permute-start | bytes 6291464 | tf_op jit(solution)/shard_map/ppermute | solution.py:127
  58.7 1.6 %collective-permute-start.11 = (bf16[128,1024]{1,0:T(8,128)(2,1)S(1)}, bf16[128,1024]{1,0:T(8,128)(2,1)S(1)}, u32[]{:S(2)}, u32[]{:S(2)}) collective-permute-start(bf16[128,1024]{1,0:T(8,128)(2,1)S(1)} %shard_map.57.refs_3_), channel_id=1, source_target_pairs={{0,4},{1,9},{2,10},{3,7},{4,0},{5,1},{6,2},{7,3},{8,12},{9,13},{10... | collective-permute-start | bytes 786440 | tf_op jit(solution)/shard_map/ppermute | solution.py:127
  58.7 1.9 %collective-permute-start.13 = (bf16[128,1024]{1,0:T(8,128)(2,1)S(1)}, bf16[128,1024]{1,0:T(8,128)(2,1)S(1)}, u32[]{:S(2)}, u32[]{:S(2)}) collective-permute-start(bf16[128,1024]{1,0:T(8,128)(2,1)S(1)} %shard_map.57.refs_3_), channel_id=1, source_target_pairs={{0,4},{1,10},{2,9},{3,7},{4,0},{5,1},{6,2},{7,3},{8,12},{9,13},{10... | collective-permute-start | bytes 786440 | tf_op jit(solution)/shard_map/ppermute | solution.py:127
  59.2 1.8 %collective-permute-start.15 = (bf16[128,1024]{1,0:T(8,128)(2,1)S(1)}, bf16[128,1024]{1,0:T(8,128)(2,1)S(1)}, u32[]{:S(2)}, u32[]{:S(2)}) collective-permute-start(bf16[128,1024]{1,0:T(8,128)(2,1)S(1)} %shard_map.58.refs_3_), channel_id=1, source_target_pairs={{0,4},{1,9},{2,10},{3,7},{4,0},{5,1},{6,2},{7,3},{8,12},{9,13},{10... | collective-permute-start | bytes 786440 | tf_op jit(solution)/shard_map/ppermute | solution.py:127
  60.3 1.5 collective-permute-start.16
  60.7 21.3 %collective-permute-start.17 = (bf16[128,1024]{1,0:T(8,128)(2,1)S(1)}, bf16[128,1024]{1,0:T(8,128)(2,1)S(1)}, u32[]{:S(2)}, u32[]{:S(2)}) collective-permute-start(bf16[128,1024]{1,0:T(8,128)(2,1)S(1)} %get-tuple-element.60.own_ref), channel_id=1, source_target_pairs={{0,4},{1,5},{2,6},{3,7},{4,0},{5,1},{6,2},{7,3},{8,12},{9,10},{10,... | collective-permute-start | bytes 786440 | tf_op jit(solution)/shard_map/ppermute | solution.py:127
  61.9 20.3 %collective-permute-start.20 = (bf16[128,1024]{1,0:T(8,128)(2,1)S(1)}, bf16[128,1024]{1,0:T(8,128)(2,1)S(1)}, u32[]{:S(2)}, u32[]{:S(2)}) collective-permute-start(bf16[128,1024]{1,0:T(8,128)(2,1)S(1)} %get-tuple-element.63.own_ref), channel_id=1, source_target_pairs={{0,4},{1,5},{2,6},{3,7},{4,0},{5,1},{6,2},{7,3},{8,12},{9,10},{10,... | collective-permute-start | bytes 786440 | tf_op jit(solution)/shard_map/ppermute | solution.py:127
  82.1 1.3 copy-start.1
  83.4 4.9 %collective-permute-start.22 = (bf16[2048,512]{1,0:T(8,128)(2,1)S(1)}, bf16[2048,512]{1,0:T(8,128)(2,1)S(1)}, u32[]{:S(2)}, u32[]{:S(2)}) collective-permute-start(bf16[2048,512]{1,0:T(8,128)(2,1)S(1)} %collective-permute-done.18.refs_1_), channel_id=1, source_target_pairs={{0,4},{1,5},{2,6},{3,7},{4,0},{5,1},{6,2},{7,3},{8,12},{9,13},{10,... | collective-permute-start | bytes 6291464 | tf_op jit(solution)/shard_map/ppermute | solution.py:127
  83.4 4.5 %collective-permute-start.19 = (bf16[128,1024]{1,0:T(8,128)(2,1)S(1)}, bf16[128,1024]{1,0:T(8,128)(2,1)S(1)}, u32[]{:S(2)}, u32[]{:S(2)}) collective-permute-start(bf16[128,1024]{1,0:T(8,128)(2,1)S(1)} %get-tuple-element.62), channel_id=1, source_target_pairs={{0,4},{1,5},{2,6},{3,7},{4,0},{5,1},{6,2},{7,3},{8,12},{9,17},{10,... | collective-permute-start | bytes 786440 | tf_op jit(solution)/shard_map/ppermute | solution.py:127
  83.9 4.4 %collective-permute-start.21 = (bf16[128,1024]{1,0:T(8,128)(2,1)S(1)}, bf16[128,1024]{1,0:T(8,128)(2,1)S(1)}, u32[]{:S(2)}, u32[]{:S(2)}) collective-permute-start(bf16[128,1024]{1,0:T(8,128)(2,1)S(1)} %get-tuple-element.62), channel_id=1, source_target_pairs={{0,4},{1,5},{2,6},{3,7},{4,0},{5,1},{6,2},{7,3},{8,12},{9,18},{10,... | collective-permute-start | bytes 786440 | tf_op jit(solution)/shard_map/ppermute | solution.py:127
  83.9 4.8 %collective-permute-start.23 = (bf16[128,1024]{1,0:T(8,128)(2,1)S(1)}, bf16[128,1024]{1,0:T(8,128)(2,1)S(1)}, u32[]{:S(2)}, u32[]{:S(2)}) collective-permute-start(bf16[128,1024]{1,0:T(8,128)(2,1)S(1)} %get-tuple-element.64), channel_id=1, source_target_pairs={{0,4},{1,5},{2,6},{3,7},{4,0},{5,1},{6,2},{7,3},{8,12},{9,17},{10,... | collective-permute-start | bytes 786440 | tf_op jit(solution)/shard_map/ppermute | solution.py:127
  84.4 4.6 %collective-permute-start.24 = (bf16[128,1024]{1,0:T(8,128)(2,1)S(1)}, bf16[128,1024]{1,0:T(8,128)(2,1)S(1)}, u32[]{:S(2)}, u32[]{:S(2)}) collective-permute-start(bf16[128,1024]{1,0:T(8,128)(2,1)S(1)} %get-tuple-element.64), channel_id=1, source_target_pairs={{0,4},{1,5},{2,6},{3,7},{4,0},{5,1},{6,2},{7,3},{8,12},{9,18},{10,... | collective-permute-start | bytes 786440 | tf_op jit(solution)/shard_map/ppermute | solution.py:127
  88.4 6.3 %collective-permute-start.25 = (bf16[128,1024]{1,0:T(8,128)(2,1)S(1)}, bf16[128,1024]{1,0:T(8,128)(2,1)S(1)}, u32[]{:S(2)}, u32[]{:S(2)}) collective-permute-start(bf16[128,1024]{1,0:T(8,128)(2,1)S(1)} %get-tuple-element.72.own_ref), channel_id=1, source_target_pairs={{0,4},{1,5},{2,6},{3,7},{4,0},{5,1},{6,2},{7,3},{8,12},{9,21},{10,... | collective-permute-start | bytes 786440 | tf_op jit(solution)/shard_map/ppermute | solution.py:127
  89.2 7.0 %collective-permute-start.27 = (bf16[128,1024]{1,0:T(8,128)(2,1)S(1)}, bf16[128,1024]{1,0:T(8,128)(2,1)S(1)}, u32[]{:S(2)}, u32[]{:S(2)}) collective-permute-start(bf16[128,1024]{1,0:T(8,128)(2,1)S(1)} %get-tuple-element.75.own_ref), channel_id=1, source_target_pairs={{0,4},{1,5},{2,6},{3,7},{4,0},{5,1},{6,2},{7,3},{8,12},{9,21},{10,... | collective-permute-start | bytes 786440 | tf_op jit(solution)/shard_map/ppermute | solution.py:127
  89.4 49.6 %collective-permute-start.34 = (bf16[2048,512]{1,0:T(8,128)(2,1)}, bf16[2048,512]{1,0:T(8,128)(2,1)}, u32[]{:S(2)}, u32[]{:S(2)}) collective-permute-start(bf16[2048,512]{1,0:T(8,128)(2,1)} %bitcast.5.refs_0_), channel_id=1, source_target_pairs={{0,1},{3,2},{4,5},{7,6},{8,9},{11,10},{12,13},{15,14},{16,17},{19,... | collective-permute-start | bytes 6291464 | tf_op jit(solution)/shard_map/ppermute | solution.py:127
  95.6 1.6 %collective-permute-start.26 = (bf16[128,1024]{1,0:T(8,128)(2,1)S(1)}, bf16[128,1024]{1,0:T(8,128)(2,1)S(1)}, u32[]{:S(2)}, u32[]{:S(2)}) collective-permute-start(bf16[128,1024]{1,0:T(8,128)(2,1)S(1)} %get-tuple-element.74), channel_id=1, source_target_pairs={{0,4},{1,9},{2,10},{3,7},{4,0},{5,1},{6,2},{7,3},{8,12},{9,13},{10... | collective-permute-start | bytes 786440 | tf_op jit(solution)/shard_map/ppermute | solution.py:127
  95.6 1.9 %collective-permute-start.28 = (bf16[128,1024]{1,0:T(8,128)(2,1)S(1)}, bf16[128,1024]{1,0:T(8,128)(2,1)S(1)}, u32[]{:S(2)}, u32[]{:S(2)}) collective-permute-start(bf16[128,1024]{1,0:T(8,128)(2,1)S(1)} %get-tuple-element.74), channel_id=1, source_target_pairs={{0,4},{1,9},{2,10},{3,7},{4,0},{5,1},{6,2},{7,3},{8,12},{9,13},{10... | collective-permute-start | bytes 786440 | tf_op jit(solution)/shard_map/ppermute | solution.py:127
  96.2 2.1 %collective-permute-start.29 = (bf16[128,1024]{1,0:T(8,128)(2,1)S(1)}, bf16[128,1024]{1,0:T(8,128)(2,1)S(1)}, u32[]{:S(2)}, u32[]{:S(2)}) collective-permute-start(bf16[128,1024]{1,0:T(8,128)(2,1)S(1)} %get-tuple-element.77), channel_id=1, source_target_pairs={{0,4},{1,9},{2,10},{3,7},{4,0},{5,1},{6,2},{7,3},{8,12},{9,13},{10... | collective-permute-start | bytes 786440 | tf_op jit(solution)/shard_map/ppermute | solution.py:127
  96.4 2.0 %collective-permute-start.30 = (bf16[128,1024]{1,0:T(8,128)(2,1)S(1)}, bf16[128,1024]{1,0:T(8,128)(2,1)S(1)}, u32[]{:S(2)}, u32[]{:S(2)}) collective-permute-start(bf16[128,1024]{1,0:T(8,128)(2,1)S(1)} %get-tuple-element.77), channel_id=1, source_target_pairs={{0,4},{1,9},{2,10},{3,7},{4,0},{5,1},{6,2},{7,3},{8,12},{9,13},{10... | collective-permute-start | bytes 786440 | tf_op jit(solution)/shard_map/ppermute | solution.py:127
  98.5 0.7 copy-start.4
  99.2 1.9 %collective-permute-start.35 = (bf16[128,1024]{1,0:T(8,128)(2,1)}, bf16[128,1024]{1,0:T(8,128)(2,1)}, u32[]{:S(2)}, u32[]{:S(2)}) collective-permute-start(bf16[128,1024]{1,0:T(8,128)(2,1)} %get-tuple-element.90.refs_3_), channel_id=1, source_target_pairs={{0,4},{1,5},{2,6},{3,7},{4,0},{5,1},{6,2},{7,3},{8,12},{9,13},{10,... | collective-permute-start | bytes 786440 | tf_op jit(solution)/shard_map/ppermute | solution.py:127
  99.3 3.0 %collective-permute-start.31 = (bf16[128,1024]{1,0:T(8,128)(2,1)}, bf16[128,1024]{1,0:T(8,128)(2,1)}, u32[]{:S(2)}, u32[]{:S(2)}) collective-permute-start(bf16[128,1024]{1,0:T(8,128)(2,1)} %get-tuple-element.85.own_ref), channel_id=1, source_target_pairs={{0,4},{1,29},{2,30},{3,7},{4,0},{5,6},{6,5},{7,3},{8,12},{9,13},{1... | collective-permute-start | bytes 786440 | tf_op jit(solution)/shard_map/ppermute | solution.py:127
  99.7 6.6 %collective-permute-start.36 = (bf16[128,1024]{1,0:T(8,128)(2,1)}, bf16[128,1024]{1,0:T(8,128)(2,1)S(1)}, u32[]{:S(2)}, u32[]{:S(2)}) collective-permute-start(bf16[128,1024]{1,0:T(8,128)(2,1)} %copy-done.4), channel_id=1, source_target_pairs={{0,4},{1,29},{2,30},{3,7},{4,0},{5,6},{6,5},{7,3},{8,12},{9,13},{1... | collective-permute-start | bytes 786440 | tf_op jit(solution)/shard_map/ppermute | solution.py:127
  99.8 7.5 %collective-permute-start.42 = (bf16[128,1024]{1,0:T(8,128)(2,1)S(1)}, bf16[128,1024]{1,0:T(8,128)(2,1)S(1)}, u32[]{:S(2)}, u32[]{:S(2)}) collective-permute-start(bf16[128,1024]{1,0:T(8,128)(2,1)S(1)} %get-tuple-element.98.refs_3_), channel_id=1, source_target_pairs={{0,4},{1,5},{2,6},{3,7},{4,0},{5,1},{6,2},{7,3},{8,12},{9,13},{10,... | collective-permute-start | bytes 786440 | tf_op jit(solution)/shard_map/ppermute | solution.py:127
  102.1 36.8 %collective-permute-start.37 = (bf16[128,1024]{1,0:T(8,128)(2,1)S(1)}, bf16[128,1024]{1,0:T(8,128)(2,1)S(1)}, u32[]{:S(2)}, u32[]{:S(2)}) collective-permute-start(bf16[128,1024]{1,0:T(8,128)(2,1)S(1)} %get-tuple-element.93.own_ref), channel_id=1, source_target_pairs={{0,4},{1,29},{2,30},{3,7},{4,0},{5,6},{6,5},{7,3},{8,12},{9,10},{1... | collective-permute-start | bytes 786440 | tf_op jit(solution)/shard_map/ppermute | solution.py:127
  102.3 1.6 %copy-start.2 = (bf16[2048,512]{1,0:T(8,128)(2,1)S(1)}, bf16[2048,512]{1,0:T(8,128)(2,1)}, u32[]{:S(2)}) copy-start(bf16[2048,512]{1,0:T(8,128)(2,1)} %copy-done.1) | copy-start | bytes 6291460
  103.9 2.4 %copy-start.5 = (bf16[128,1024]{1,0:T(8,128)(2,1)S(1)}, bf16[128,1024]{1,0:T(8,128)(2,1)}, u32[]{:S(2)}) copy-start(bf16[128,1024]{1,0:T(8,128)(2,1)} %copy-done.4) | copy-start | bytes 786436
  105.9 2.0 %collective-permute-start.32 = (bf16[128,1024]{1,0:T(8,128)(2,1)S(1)}, bf16[128,1024]{1,0:T(8,128)(2,1)S(1)}, u32[]{:S(2)}, u32[]{:S(2)}) collective-permute-start(bf16[128,1024]{1,0:T(8,128)(2,1)S(1)} %get-tuple-element.87), channel_id=1, source_target_pairs={{0,4},{1,5},{2,6},{3,7},{4,0},{5,1},{6,2},{7,3},{8,12},{9,13},{10,... | collective-permute-start | bytes 786440 | tf_op jit(solution)/shard_map/ppermute | solution.py:127
  107.1 1.6 %collective-permute-start.40 = (bf16[128,1024]{1,0:T(8,128)(2,1)S(1)}, bf16[128,1024]{1,0:T(8,128)(2,1)S(1)}, u32[]{:S(2)}, u32[]{:S(2)}) collective-permute-start(bf16[128,1024]{1,0:T(8,128)(2,1)S(1)} %get-tuple-element.96), channel_id=1, source_target_pairs={{0,4},{1,5},{2,6},{3,7},{4,0},{5,1},{6,2},{7,3},{8,12},{9,13},{10,... | collective-permute-start | bytes 786440 | tf_op jit(solution)/shard_map/ppermute | solution.py:127
  107.5 38.6 %collective-permute-start.43 = (bf16[128,1024]{1,0:T(8,128)(2,1)S(1)}, bf16[128,1024]{1,0:T(8,128)(2,1)S(1)}, u32[]{:S(2)}, u32[]{:S(2)}) collective-permute-start(bf16[128,1024]{1,0:T(8,128)(2,1)S(1)} %get-tuple-element.99.own_ref), channel_id=1, source_target_pairs={{0,4},{1,29},{2,30},{3,7},{4,0},{5,6},{6,5},{7,3},{8,12},{9,10},{1... | collective-permute-start | bytes 786440 | tf_op jit(solution)/shard_map/ppermute | solution.py:127
  108.0 33.6 %collective-permute-start.33 = (bf16[128,1024]{1,0:T(8,128)(2,1)S(1)}, bf16[128,1024]{1,0:T(8,128)(2,1)S(1)}, u32[]{:S(2)}, u32[]{:S(2)}) collective-permute-start(bf16[128,1024]{1,0:T(8,128)(2,1)S(1)} %get-tuple-element.104.own_ref), channel_id=1, source_target_pairs={{0,4},{1,2},{2,1},{3,7},{4,0},{5,25},{6,26},{7,3},{8,12},{9,13},{1... | collective-permute-start | bytes 786440 | tf_op jit(solution)/shard_map/ppermute | solution.py:127
  108.8 37.4 %collective-permute-start.41 = (bf16[128,1024]{1,0:T(8,128)(2,1)S(1)}, bf16[128,1024]{1,0:T(8,128)(2,1)S(1)}, u32[]{:S(2)}, u32[]{:S(2)}) collective-permute-start(bf16[128,1024]{1,0:T(8,128)(2,1)S(1)} %get-tuple-element.108.own_ref), channel_id=1, source_target_pairs={{0,4},{1,2},{2,1},{3,7},{4,0},{5,25},{6,26},{7,3},{8,12},{9,13},{1... | collective-permute-start | bytes 786440 | tf_op jit(solution)/shard_map/ppermute | solution.py:127
  139.0 12.6 %collective-permute-start.39 = (bf16[128,512]{1,0:T(8,128)(2,1)S(1)}, bf16[128,512]{1,0:T(8,128)(2,1)S(1)}, u32[]{:S(2)}, u32[]{:S(2)}) collective-permute-start(bf16[128,512]{1,0:T(8,128)(2,1)S(1)} %slice.64), channel_id=1, source_target_pairs={{0,1},{1,0},{3,2},{2,3},{4,5},{5,4},{7,6},{6,7},{8,9},{9,8},{11,10... | collective-permute-start | bytes 393224 | tf_op jit(solution)/shard_map/ppermute | solution.py:127
  142.4 9.2 %collective-permute-start.38 = (bf16[128,512]{1,0:T(8,128)(2,1)S(1)}, bf16[128,512]{1,0:T(8,128)(2,1)S(1)}, u32[]{:S(2)}, u32[]{:S(2)}) collective-permute-start(bf16[128,512]{1,0:T(8,128)(2,1)S(1)} %slice.52), channel_id=1, source_target_pairs={{0,1},{1,0},{2,3},{3,2},{4,24},{5,25},{6,26},{7,27},{8,12},{9,13},... | collective-permute-start | bytes 393224 | tf_op jit(solution)/shard_map/ppermute | solution.py:127
  146.1 5.5 %collective-permute-start.45 = (bf16[128,512]{1,0:T(8,128)(2,1)S(1)}, bf16[128,512]{1,0:T(8,128)(2,1)S(1)}, u32[]{:S(2)}, u32[]{:S(2)}) collective-permute-start(bf16[128,512]{1,0:T(8,128)(2,1)S(1)} %slice.65), channel_id=1, source_target_pairs={{0,1},{1,0},{3,2},{2,3},{4,5},{5,4},{7,6},{6,7},{8,9},{9,8},{11,10... | collective-permute-start | bytes 393224 | tf_op jit(solution)/shard_map/ppermute | solution.py:127
  147.1 7.5 %collective-permute-start.44 = (bf16[128,512]{1,0:T(8,128)(2,1)S(1)}, bf16[128,512]{1,0:T(8,128)(2,1)S(1)}, u32[]{:S(2)}, u32[]{:S(2)}) collective-permute-start(bf16[128,512]{1,0:T(8,128)(2,1)S(1)} %slice.55), channel_id=1, source_target_pairs={{0,1},{1,0},{2,3},{3,2},{4,24},{5,25},{6,26},{7,27},{8,12},{9,13},... | collective-permute-start | bytes 393224 | tf_op jit(solution)/shard_map/ppermute | solution.py:127

commit v4 on v3

--- a/solution.py
+++ b/solution.py
@@ -141,7 +141,7 @@
     out_ref = rest.pop(0)
     kept_ref = rest.pop(0) if "kept" in extras else None
     work = functools.partial(
-        multiply, width, own_ref, other_ref, operators, named.get("addend"), out_ref, kept_ref, rest[:-1], rest[-1]
+        multiply, width, own_ref, other_ref, operators, named.get("addend"), out_ref, kept_ref
     )
     if turn is None:
         work()
@@ -159,7 +159,7 @@
             kept_ref[...] = named["kept"][...]
 
 
-def multiply(width, own_ref, other_ref, operators, add_ref, out_ref, kept_ref, tiles, sems):
+def multiply(width, own_ref, other_ref, operators, add_ref, out_ref, kept_ref):
     pieces = len(operators)
     depth = operators[0].shape[0] // width
     half = width // 2
@@ -167,23 +167,13 @@
     down = [half - 1 - i for i in range(half)]
     up = [half + i for i in range(half)]
     blocks = [jnp.where(lower, x, y) for x, y in zip(down + up, up + down)]
-    copies = []
+    totals = [0.0] * pieces
     for t, block in enumerate(blocks):
-        rows = pl.ds(pl.multiple_of(block * depth, depth), depth)
-        group = [
-            pltpu.make_async_copy(operator.at[rows, :], tile.at[t], sems.at[i, t])
-            for i, (operator, tile) in enumerate(zip(operators, tiles))
-        ]
-        for copy in group:
-            copy.start()
-        copies.append(group)
-    totals = [0.0] * pieces
-    for t, group in enumerate(copies):
         source = own_ref if t < half else other_ref
         rows = source[:, (t % half) * depth:(t % half + 1) * depth]
-        for i, copy in enumerate(group):
-            copy.wait()
-            totals[i] += jnp.dot(rows, tiles[i][t], preferred_element_type=jnp.float32)
+        deep = pl.ds(pl.multiple_of(block * depth, depth), depth)
+        for i, operator in enumerate(operators):
+            totals[i] += jnp.dot(rows, operator[deep, :], preferred_element_type=jnp.float32)
     start = 0
     for total in totals:
         stop = start + total.shape[1]
@@ -202,17 +192,14 @@
     deep = pieces[0].shape[0]
     columns = sum(piece.shape[1] for piece in pieces)
     vmem = pl.BlockSpec(memory_space=pltpu.VMEM)
-    hbm = pl.BlockSpec(memory_space=pltpu.HBM)
     extras = {name: value for name, value in (("addend", addend), ("kept", kept)) if value is not None}
     outs = 1 if kept is None else 2
     return pl.pallas_call(
         functools.partial(apply_kernel, width, len(pieces), tuple(extras), turn),
         out_shape=[jax.ShapeDtypeStruct((rows, columns), jnp.bfloat16)] * outs,
-        in_specs=[vmem, vmem] + [hbm] * len(pieces) + [vmem] * len(extras),
+        in_specs=[vmem] * (2 + len(pieces) + len(extras)),
         out_specs=[vmem] * outs,
-        scratch_shapes=[pltpu.VMEM((width, deep // width, piece.shape[1]), piece.dtype) for piece in pieces]
-        + [pltpu.SemaphoreType.DMA((len(pieces), width))],
-        compiler_params=pltpu.CompilerParams(vmem_limit_bytes=16 * 1024 * 1024),
+        compiler_params=pltpu.CompilerParams(vmem_limit_bytes=8 * 1024 * 1024),
         cost_estimate=pl.CostEstimate(
             flops=2 * rows * columns * deep, bytes_accessed=2 * columns * deep, transcendentals=0
         ),
@@ -300,7 +287,7 @@
         if final:
             given = []
             for part in settled:
-                given.append(move(after(part, traces[-1]), places.across_cores()))
+                given.append(move(part, places.across_cores()))
         others = []
         for part in traces:
             others.append(move(part, places.swap(stage)))
@@ -338,7 +325,7 @@
     settled_others = swapped(settled_rows, places.swap_settled())
     last_given = []
     for part in seconds:
-        last_given.append(move(part, places.across_cores()))
+        last_given.append(move(after(part, traces[-1]), places.across_cores()))
     last_rows = contrasts([after(mine, other) for mine, other in zip(firsts, last_given)], last_given)
     last_others = swapped(last_rows, places.swap(0))
     combined = []

time: 157 us -> 162 us (1.032)
  Pallas kernels: 8.61 us -> 16.5 us
  starting transfers between devices: 48.5 us -> 44.2 us
    pallas_call x20, Pallas kernels: 8.61 us -> 16.5 us  [applied(): pl.pallas_call(functools.partial(apply_kernel, width, len(pieces), tuple(...]
    ppermute x46, starting transfers between devices: 48.5 us -> 44.2 us  [move(): return lax.ppermute(values, AXES, pairs)]
  transfers between devices with their start and end apart: 46 -> 46, of which waited for: 24 -> 25; matrix products, arithmetic and copies ran while one was open for 1% -> 1% of each run, Pallas kernels for 5% -> 10%
where the time goes in v4:
time: 162 us; the launch traced here: 160 us
  waiting for transfers between devices  88.7 us (55%)
  starting transfers between devices  44.2 us (27%)
  Pallas kernels  16.5 us (10%)
  local copies, waits for them, and re-layouts  5.85 us (4%)
  other arithmetic  4.27 us (3%)
    ppermute x46, waiting for transfers between devices, move(): return lax.ppermute(values, AXES, pairs)  88.7 us
    ppermute x46, starting transfers between devices, move(): return lax.ppermute(values, AXES, pairs)  44.2 us
    pallas_call x20, Pallas kernels, applied(): pl.pallas_call(functools.partial(apply_kernel, width, len(pieces), tuple(...  16.5 us
    unnamed x12, local copies, waits for them, and re-layouts  5.72 us
  transfers between devices with their start and end apart: 46, of which 25 were waited for; matrix products, arithmetic and copies ran while one was open for 1% of the time, Pallas kernels for 10%

profile of v4, /device:TPU:0, one launch (start us, length us, event | category | flops | bytes accessed | tf_op | source)
XLA Modules:
  0.0 159.8 jit_solution(14538315696485053552)
XLA Ops:
  0.0 0.7 add_divide_fusion
  0.7 1.1 fusion.8
  1.8 3.1 %collective-permute-start = (bf16[128,512]{1,0:T(8,128)(2,1)S(1)}, bf16[128,512]{1,0:T(8,128)(2,1)S(1)}, u32[]{:S(2)}, u32[]{:S(2)}) collective-permute-start(bf16[128,512]{1,0:T(8,128)(2,1)S(1)} %bitcast.22), channel_id=1, source_target_pairs={{0,1},{1,0},{3,2},{2,3},{4,5},{5,4},{7,6},{6,7},{8,9},{9,8},{11,10... | collective-permute-start | bytes 393224 | tf_op jit(solution)/shard_map/ppermute | solution.py:127
  4.9 3.5 %collective-permute-done = bf16[128,512]{1,0:T(8,128)(2,1)S(1)} collective-permute-done((bf16[128,512]{1,0:T(8,128)(2,1)S(1)}, bf16[128,512]{1,0:T(8,128)(2,1)S(1)}, u32[]{:S(2)}, u32[]{:S(2)}) %collective-permute-start) | collective-permute-done | bytes 131104 | tf_op jit(solution)/shard_map/ppermute | solution.py:127
  8.6 3.3 %collective-permute-start.3 = (bf16[128,512]{1,0:T(8,128)(2,1)S(1)}, bf16[128,512]{1,0:T(8,128)(2,1)S(1)}, u32[]{:S(2)}, u32[]{:S(2)}) collective-permute-start(bf16[128,512]{1,0:T(8,128)(2,1)S(1)} %bitcast.20), channel_id=1, source_target_pairs={{0,1},{1,0},{3,2},{2,3},{4,5},{5,4},{7,6},{6,7},{8,9},{9,8},{11,10... | collective-permute-start | bytes 393224 | tf_op jit(solution)/shard_map/ppermute | solution.py:127
  11.9 0.8 collective-permute-start.9
  12.7 2.1 %collective-permute-done.3 = bf16[128,512]{1,0:T(8,128)(2,1)S(1)} collective-permute-done((bf16[128,512]{1,0:T(8,128)(2,1)S(1)}, bf16[128,512]{1,0:T(8,128)(2,1)S(1)}, u32[]{:S(2)}, u32[]{:S(2)}) %collective-permute-start.3) | collective-permute-done | bytes 131104 | tf_op jit(solution)/shard_map/ppermute | solution.py:127
  15.0 1.3 collective-permute-start.2
  16.3 0.3 collective-permute-done.4
  16.6 1.3 collective-permute-start.5
  17.9 8.3 %collective-permute-done.2 = bf16[128,1024]{1,0:T(8,128)(2,1)S(1)} collective-permute-done((bf16[128,1024]{1,0:T(8,128)(2,1)S(1)}, bf16[128,1024]{1,0:T(8,128)(2,1)S(1)}, u32[]{:S(2)}, u32[]{:S(2)}) %collective-permute-start.2) | collective-permute-done | bytes 262176 | tf_op jit(solution)/shard_map/ppermute | solution.py:127
  26.3 0.5 shard_map.55
  26.8 4.5 %collective-permute-done.5 = bf16[128,1024]{1,0:T(8,128)(2,1)S(1)} collective-permute-done((bf16[128,1024]{1,0:T(8,128)(2,1)S(1)}, bf16[128,1024]{1,0:T(8,128)(2,1)S(1)}, u32[]{:S(2)}, u32[]{:S(2)}) %collective-permute-start.5) | collective-permute-done | bytes 262176 | tf_op jit(solution)/shard_map/ppermute | solution.py:127
  31.3 0.5 shard_map.56
  31.9 7.7 %collective-permute-done.6 = bf16[256,512]{1,0:T(8,128)(2,1)S(1)} collective-permute-done((bf16[256,512]{1,0:T(8,128)(2,1)S(1)}, bf16[256,512]{1,0:T(8,128)(2,1)S(1)}, u32[]{:S(2)}, u32[]{:S(2)}) %collective-permute-start.6) | collective-permute-done | bytes 262176 | tf_op jit(solution)/shard_map/ppermute | solution.py:127
  39.6 3.2 %collective-permute-start.10 = (bf16[256,1024]{1,0:T(8,128)(2,1)S(1)}, bf16[256,1024]{1,0:T(8,128)(2,1)S(1)}, u32[]{:S(2)}, u32[]{:S(2)}) collective-permute-start(bf16[256,1024]{1,0:T(8,128)(2,1)S(1)} %pad_maximum_fusion), channel_id=1, source_target_pairs={{0,4},{1,5},{2,6},{3,7},{4,0},{5,1},{6,2},{7,3},{8,12},{9,13},{10,... | collective-permute-start | bytes 1572872 | tf_op jit(solution)/shard_map/ppermute | solution.py:127
  43.0 0.5 collective-permute-start.12
  43.4 0.9 collective-permute-done.10
  44.4 0.3 collective-permute-done.7.other_ref
  44.8 0.4 collective-permute-done.12.other_ref
  45.1 0.4 collective-permute-start.14
  45.5 1.2 copy-done
  46.7 11.9 %collective-permute-start.18 = (bf16[2048,512]{1,0:T(8,128)(2,1)S(1)}, bf16[2048,512]{1,0:T(8,128)(2,1)S(1)}, u32[]{:S(2)}, u32[]{:S(2)}) collective-permute-start(bf16[2048,512]{1,0:T(8,128)(2,1)S(1)} %bitcast.11), channel_id=1, source_target_pairs={{0,5},{3,6},{12,9},{15,10},{16,21},{19,22},{28,25},{31,26}} | collective-permute-start | bytes 6291464 | tf_op jit(solution)/shard_map/ppermute | solution.py:127
  58.7 0.5 collective-permute-start.13
  59.3 1.0 collective-permute-done.11.own_ref
  60.4 0.2 collective-permute-done.13.other_ref
  61.0 0.8 collective-permute-done.16.other_ref
  62.0 20.1 %collective-permute-done.18.refs_1_ = bf16[2048,512]{1,0:T(8,128)(2,1)S(1)} collective-permute-done((bf16[2048,512]{1,0:T(8,128)(2,1)S(1)}, bf16[2048,512]{1,0:T(8,128)(2,1)S(1)}, u32[]{:S(2)}, u32[]{:S(2)}) %collective-permute-start.18) | collective-permute-done | bytes 2097184 | tf_op jit(solution)/shard_map/ppermute | solution.py:127
  82.2 1.2 copy-done.1
  83.4 0.5 collective-permute-start.19
  83.9 0.5 collective-permute-start.23
  84.4 3.5 %collective-permute-done.19.own_ref = bf16[128,1024]{1,0:T(8,128)(2,1)S(1)} collective-permute-done((bf16[128,1024]{1,0:T(8,128)(2,1)S(1)}, bf16[128,1024]{1,0:T(8,128)(2,1)S(1)}, u32[]{:S(2)}, u32[]{:S(2)}) %collective-permute-start.19) | collective-permute-done | bytes 262176 | tf_op jit(solution)/shard_map/ppermute | solution.py:127
  87.9 0.4 collective-permute-done.21.other_ref
  88.7 0.4 collective-permute-done.24.other_ref
  89.3 5.4 %collective-permute-start.35 = (bf16[2048,512]{1,0:T(8,128)(2,1)}, bf16[2048,512]{1,0:T(8,128)(2,1)}, u32[]{:S(2)}, u32[]{:S(2)}) collective-permute-start(bf16[2048,512]{1,0:T(8,128)(2,1)} %bitcast.5.refs_0_), channel_id=1, source_target_pairs={{0,1},{3,2},{4,5},{7,6},{8,9},{11,10},{12,13},{15,14},{16,17},{19,... | collective-permute-start | bytes 6291464 | tf_op jit(solution)/shard_map/ppermute | solution.py:127
  94.8 0.5 collective-permute-start.28
  95.3 0.7 copy-done.4
  96.1 0.4 collective-permute-start.30
  96.7 0.7 shard_map.67
  97.5 0.4 collective-permute-done.30.other_ref
  97.9 0.7 shard_map.68
  98.8 0.4 collective-permute-start.31
  99.3 0.4 collective-permute-start.42
  99.7 0.9 collective-permute-done.32.other_ref
  100.5 1.6 copy-done.2
  102.1 0.9 copy-done.5
  103.1 1.7 %shard_map.70 = (bf16[128,1024]{1,0:T(8,128)(2,1)}, bf16[128,1024]{1,0:T(8,128)(2,1)S(1)}) custom-call(bf16[128,1024]{1,0:T(8,128)(2,1)} %get-tuple-element.84.own_ref, bf16[128,1024]{1,0:T(8,128)(2,1)} %collective-permute-done.32.other_ref, bf16[2048,512]{1,0:T(8,128)(2,1)S(1)} %collective-permute-done.8.refs_0_, bf16[2048,512]{1,0:T(8,128)(2,1)S(1)} %copy-done.2, ...), custom_call_target="tpu_custom_call" | custom-call | flops 536870912 | bytes 4194304 | tf_op jit(solution)/shard_map/pallas_call | solution.py:197
  104.8 1.7 %shard_map.69 = (bf16[128,1024]{1,0:T(8,128)(2,1)}, bf16[128,1024]{1,0:T(8,128)(2,1)S(1)}) custom-call(bf16[128,1024]{1,0:T(8,128)(2,1)} %get-tuple-element.85.own_ref, bf16[128,1024]{1,0:T(8,128)(2,1)} %collective-permute-done.31.other_ref, bf16[2048,512]{1,0:T(8,128)(2,1)S(1)} %collective-permute-done.8.refs_0_, bf16[2048,512]{1,0:T(8,128)(2,1)S(1)} %copy-done.2, ...), custom_call_target="tpu_custom_call" | custom-call | flops 536870912 | bytes 4194304 | tf_op jit(solution)/shard_map/pallas_call | solution.py:197
  106.7 1.1 convert_add_fusion.2
  107.8 0.4 collective-permute-start.37
  108.5 0.4 collective-permute-start.43
  109.2 0.5 collective-permute-done.40
  109.9 0.4 collective-permute-start.41
  110.3 28.5 %collective-permute-done.35.refs_1_ = bf16[2048,512]{1,0:T(8,128)(2,1)} collective-permute-done((bf16[2048,512]{1,0:T(8,128)(2,1)}, bf16[2048,512]{1,0:T(8,128)(2,1)}, u32[]{:S(2)}, u32[]{:S(2)}) %collective-permute-start.35) | collective-permute-done | bytes 2097184 | tf_op jit(solution)/shard_map/ppermute | solution.py:127
  138.8 2.2 %shard_map.71.refs_3_ = bf16[128,1024]{1,0:T(8,128)(2,1)S(1)} custom-call(bf16[128,1024]{1,0:T(8,128)(2,1)S(1)} %get-tuple-element.93.own_ref, bf16[128,1024]{1,0:T(8,128)(2,1)S(1)} %collective-permute-done.37.other_ref, bf16[2048,512]{1,0:T(8,128)(2,1)} %bitcast.5.refs_0_, bf16[2048,512]{1,0:T(8,128)(2,1)} %collective-permute-done.35.refs_1_, ...), custom_call_target="tpu_custom_call" | custom-call | flops 536870912 | bytes 4194304 | tf_op jit(solution)/shard_map/pallas_call | solution.py:197
  141.1 2.5 %collective-permute-start.39 = (bf16[128,512]{1,0:T(8,128)(2,1)S(1)}, bf16[128,512]{1,0:T(8,128)(2,1)}, u32[]{:S(2)}, u32[]{:S(2)}) collective-permute-start(bf16[128,512]{1,0:T(8,128)(2,1)S(1)} %slice.64), channel_id=1, source_target_pairs={{0,1},{1,0},{3,2},{2,3},{4,5},{5,4},{7,6},{6,7},{8,9},{9,8},{11,10... | collective-permute-start | bytes 393224 | tf_op jit(solution)/shard_map/ppermute | solution.py:127
  143.6 2.9 %shard_map.72 = (bf16[128,1024]{1,0:T(8,128)(2,1)}, bf16[128,1024]{1,0:T(8,128)(2,1)S(1)}) custom-call(bf16[128,1024]{1,0:T(8,128)(2,1)S(1)} %get-tuple-element.104.own_ref, bf16[128,1024]{1,0:T(8,128)(2,1)S(1)} %collective-permute-done.34.other_ref, bf16[2048,512]{1,0:T(8,128)(2,1)} %bitcast.5.refs_0_, bf16[2048,512]{1,0:T(8,128)(2,1)} %collective-permute-done.35.refs_1_, ...), custom_call_target="tpu_custom_call" | custom-call | flops 536870912 | bytes 4194304 | tf_op jit(solution)/shard_map/pallas_call | solution.py:197
  146.6 0.8 collective-permute-start.38
  147.4 2.3 %shard_map.73.refs_3_ = bf16[128,1024]{1,0:T(8,128)(2,1)S(1)} custom-call(bf16[128,1024]{1,0:T(8,128)(2,1)S(1)} %get-tuple-element.99.own_ref, bf16[128,1024]{1,0:T(8,128)(2,1)} %collective-permute-done.43.other_ref, bf16[2048,512]{1,0:T(8,128)(2,1)} %bitcast.5.refs_0_, bf16[2048,512]{1,0:T(8,128)(2,1)} %collective-permute-done.35.refs_1_, ...), custom_call_target="tpu_custom_call" | custom-call | flops 536870912 | bytes 4194304 | tf_op jit(solution)/shard_map/pallas_call | solution.py:197
  149.7 1.4 collective-permute-start.45
  151.1 2.9 %shard_map.74 = (bf16[128,1024]{1,0:T(8,128)(2,1)}, bf16[128,1024]{1,0:T(8,128)(2,1)S(1)}) custom-call(bf16[128,1024]{1,0:T(8,128)(2,1)S(1)} %get-tuple-element.108.own_ref, bf16[128,1024]{1,0:T(8,128)(2,1)S(1)} %collective-permute-done.41.other_ref, bf16[2048,512]{1,0:T(8,128)(2,1)} %bitcast.5.refs_0_, bf16[2048,512]{1,0:T(8,128)(2,1)} %collective-permute-done.35.refs_1_, ...), custom_call_target="tpu_custom_call" | custom-call | flops 536870912 | bytes 4194304 | tf_op jit(solution)/shard_map/pallas_call | solution.py:197
  154.0 1.5 collective-permute-start.44
  155.6 3.5 %collective-permute-done.44 = bf16[128,512]{1,0:T(8,128)(2,1)S(1)} collective-permute-done((bf16[128,512]{1,0:T(8,128)(2,1)S(1)}, bf16[128,512]{1,0:T(8,128)(2,1)S(1)}, u32[]{:S(2)}, u32[]{:S(2)}) %collective-permute-start.44) | collective-permute-done | bytes 131104 | tf_op jit(solution)/shard_map/ppermute | solution.py:127
  159.1 0.7 pad_maximum_fusion.4
  (82 shorter events, 3.9 us)
Async XLA Ops:
  1.8 6.6 %collective-permute-start = (bf16[128,512]{1,0:T(8,128)(2,1)S(1)}, bf16[128,512]{1,0:T(8,128)(2,1)S(1)}, u32[]{:S(2)}, u32[]{:S(2)}) collective-permute-start(bf16[128,512]{1,0:T(8,128)(2,1)S(1)} %bitcast.22), channel_id=1, source_target_pairs={{0,1},{1,0},{3,2},{2,3},{4,5},{5,4},{7,6},{6,7},{8,9},{9,8},{11,10... | collective-permute-start | bytes 393224 | tf_op jit(solution)/shard_map/ppermute | solution.py:127
  4.9 21.4 %copy-start.3 = (bf16[1,2048,512]{2,1,0:T(8,128)(2,1)S(1)}, bf16[1,2048,512]{2,1,0:T(8,128)(2,1)}, u32[]{:S(2)}) copy-start(bf16[1,2048,512]{2,1,0:T(8,128)(2,1)} %param.7) | copy-start | bytes 6291460
  8.5 6.5 %collective-permute-start.1 = (bf16[128,1024]{1,0:T(8,128)(2,1)S(1)}, bf16[128,1024]{1,0:T(8,128)(2,1)S(1)}, u32[]{:S(2)}, u32[]{:S(2)}) collective-permute-start(bf16[128,1024]{1,0:T(8,128)(2,1)S(1)} %get-tuple-element.113), channel_id=1, source_target_pairs={{0,4},{1,2},{2,1},{3,7},{4,0},{5,6},{6,5},{7,3},{8,12},{9,10},{10,... | collective-permute-start | bytes 786440 | tf_op jit(solution)/shard_map/ppermute | solution.py:127
  8.6 6.2 %collective-permute-start.3 = (bf16[128,512]{1,0:T(8,128)(2,1)S(1)}, bf16[128,512]{1,0:T(8,128)(2,1)S(1)}, u32[]{:S(2)}, u32[]{:S(2)}) collective-permute-start(bf16[128,512]{1,0:T(8,128)(2,1)S(1)} %bitcast.20), channel_id=1, source_target_pairs={{0,1},{1,0},{3,2},{2,3},{4,5},{5,4},{7,6},{6,7},{8,9},{9,8},{11,10... | collective-permute-start | bytes 393224 | tf_op jit(solution)/shard_map/ppermute | solution.py:127
  11.9 32.9 %collective-permute-start.8 = (bf16[2048,512]{1,0:T(8,128)(2,1)}, bf16[2048,512]{1,0:T(8,128)(2,1)S(1)}, u32[]{:S(2)}, u32[]{:S(2)}) collective-permute-start(bf16[2048,512]{1,0:T(8,128)(2,1)} %bitcast.9), channel_id=1, source_target_pairs={{0,4},{1,5},{2,6},{3,7},{4,0},{5,1},{6,2},{7,3},{8,12},{9,13},{10,... | collective-permute-start | bytes 6291464 | tf_op jit(solution)/shard_map/ppermute | solution.py:127
  11.9 32.9 %collective-permute-start.9 = (bf16[2048,512]{1,0:T(8,128)(2,1)}, bf16[2048,512]{1,0:T(8,128)(2,1)S(1)}, u32[]{:S(2)}, u32[]{:S(2)}) collective-permute-start(bf16[2048,512]{1,0:T(8,128)(2,1)} %bitcast.10), channel_id=1, source_target_pairs={{4,1},{7,2},{8,13},{11,14},{20,17},{23,18},{24,29},{27,30}} | collective-permute-start | bytes 6291464 | tf_op jit(solution)/shard_map/ppermute | solution.py:127
  14.9 1.7 %collective-permute-start.4 = (bf16[128,1024]{1,0:T(8,128)(2,1)S(1)}, bf16[128,1024]{1,0:T(8,128)(2,1)S(1)}, u32[]{:S(2)}, u32[]{:S(2)}) collective-permute-start(bf16[128,1024]{1,0:T(8,128)(2,1)S(1)} %get-tuple-element.117), channel_id=1, source_target_pairs={{0,4},{1,2},{2,1},{3,7},{4,0},{5,6},{6,5},{7,3},{8,12},{9,10},{10,... | collective-permute-start | bytes 786440 | tf_op jit(solution)/shard_map/ppermute | solution.py:127
  15.0 11.2 %collective-permute-start.2 = (bf16[128,1024]{1,0:T(8,128)(2,1)S(1)}, bf16[128,1024]{1,0:T(8,128)(2,1)S(1)}, u32[]{:S(2)}, u32[]{:S(2)}) collective-permute-start(bf16[128,1024]{1,0:T(8,128)(2,1)S(1)} %collective-permute-done.1), channel_id=1, source_target_pairs={{1,0},{2,3},{5,4},{6,7},{9,8},{10,11},{13,12},{14,15},{17,16},{18,... | collective-permute-start | bytes 786440 | tf_op jit(solution)/shard_map/ppermute | solution.py:127
  16.6 14.6 %collective-permute-start.5 = (bf16[128,1024]{1,0:T(8,128)(2,1)S(1)}, bf16[128,1024]{1,0:T(8,128)(2,1)S(1)}, u32[]{:S(2)}, u32[]{:S(2)}) collective-permute-start(bf16[128,1024]{1,0:T(8,128)(2,1)S(1)} %collective-permute-done.4), channel_id=1, source_target_pairs={{1,0},{2,3},{5,4},{6,7},{9,8},{10,11},{13,12},{14,15},{17,16},{18,... | collective-permute-start | bytes 786440 | tf_op jit(solution)/shard_map/ppermute | solution.py:127
  31.8 7.8 %collective-permute-start.6 = (bf16[256,512]{1,0:T(8,128)(2,1)S(1)}, bf16[256,512]{1,0:T(8,128)(2,1)S(1)}, u32[]{:S(2)}, u32[]{:S(2)}) collective-permute-start(bf16[256,512]{1,0:T(8,128)(2,1)S(1)} %pad_maximum_fusion.3), channel_id=1, source_target_pairs={{0,1},{1,0},{3,2},{2,3},{4,5},{5,4},{7,6},{6,7},{8,9},{9,8},{11,10... | collective-permute-start | bytes 786440 | tf_op jit(solution)/shard_map/ppermute | solution.py:127
  39.6 4.8 %collective-permute-start.10 = (bf16[256,1024]{1,0:T(8,128)(2,1)S(1)}, bf16[256,1024]{1,0:T(8,128)(2,1)S(1)}, u32[]{:S(2)}, u32[]{:S(2)}) collective-permute-start(bf16[256,1024]{1,0:T(8,128)(2,1)S(1)} %pad_maximum_fusion), channel_id=1, source_target_pairs={{0,4},{1,5},{2,6},{3,7},{4,0},{5,1},{6,2},{7,3},{8,12},{9,13},{10,... | collective-permute-start | bytes 1572872 | tf_op jit(solution)/shard_map/ppermute | solution.py:127
  42.9 1.9 %collective-permute-start.7 = (bf16[128,1024]{1,0:T(8,128)(2,1)S(1)}, bf16[128,1024]{1,0:T(8,128)(2,1)S(1)}, u32[]{:S(2)}, u32[]{:S(2)}) collective-permute-start(bf16[128,1024]{1,0:T(8,128)(2,1)S(1)} %get-tuple-element.111.refs_2_.refs_3_), channel_id=1, source_target_pairs={{0,4},{1,2},{2,1},{3,7},{4,0},{5,25},{6,26},{7,3},{8,12},{9,13},{1... | collective-permute-start | bytes 786440 | tf_op jit(solution)/shard_map/ppermute | solution.py:127
  43.0 2.2 %collective-permute-start.12 = (bf16[128,1024]{1,0:T(8,128)(2,1)S(1)}, bf16[128,1024]{1,0:T(8,128)(2,1)S(1)}, u32[]{:S(2)}, u32[]{:S(2)}) collective-permute-start(bf16[128,1024]{1,0:T(8,128)(2,1)S(1)} %get-tuple-element.54.own_ref.refs_2_.refs_3_), channel_id=1, source_target_pairs={{0,4},{1,2},{2,1},{3,7},{4,0},{5,25},{6,26},{7,3},{8,12},{9,13},{1... | collective-permute-start | bytes 786440 | tf_op jit(solution)/shard_map/ppermute | solution.py:127
  45.1 1.6 copy-start
  45.1 15.5 %collective-permute-start.14 = (bf16[2048,512]{1,0:T(8,128)(2,1)S(1)}, bf16[2048,512]{1,0:T(8,128)(2,1)S(1)}, u32[]{:S(2)}, u32[]{:S(2)}) collective-permute-start(bf16[2048,512]{1,0:T(8,128)(2,1)S(1)} %collective-permute-done.9.refs_1_), channel_id=1, source_target_pairs={{0,4},{1,5},{2,6},{3,7},{4,0},{5,1},{6,2},{7,3},{8,12},{9,13},{10,... | collective-permute-start | bytes 6291464 | tf_op jit(solution)/shard_map/ppermute | solution.py:127
  46.7 35.4 %collective-permute-start.18 = (bf16[2048,512]{1,0:T(8,128)(2,1)S(1)}, bf16[2048,512]{1,0:T(8,128)(2,1)S(1)}, u32[]{:S(2)}, u32[]{:S(2)}) collective-permute-start(bf16[2048,512]{1,0:T(8,128)(2,1)S(1)} %bitcast.11), channel_id=1, source_target_pairs={{0,5},{3,6},{12,9},{15,10},{16,21},{19,22},{28,25},{31,26}} | collective-permute-start | bytes 6291464 | tf_op jit(solution)/shard_map/ppermute | solution.py:127
  58.7 1.6 collective-permute-start.11
  58.7 1.9 %collective-permute-start.13 = (bf16[128,1024]{1,0:T(8,128)(2,1)S(1)}, bf16[128,1024]{1,0:T(8,128)(2,1)S(1)}, u32[]{:S(2)}, u32[]{:S(2)}) collective-permute-start(bf16[128,1024]{1,0:T(8,128)(2,1)S(1)} %shard_map.57.refs_3_), channel_id=1, source_target_pairs={{0,4},{1,10},{2,9},{3,7},{4,0},{5,1},{6,2},{7,3},{8,12},{9,13},{10... | collective-permute-start | bytes 786440 | tf_op jit(solution)/shard_map/ppermute | solution.py:127
  59.2 1.8 %collective-permute-start.15 = (bf16[128,1024]{1,0:T(8,128)(2,1)S(1)}, bf16[128,1024]{1,0:T(8,128)(2,1)S(1)}, u32[]{:S(2)}, u32[]{:S(2)}) collective-permute-start(bf16[128,1024]{1,0:T(8,128)(2,1)S(1)} %shard_map.58.refs_3_), channel_id=1, source_target_pairs={{0,4},{1,9},{2,10},{3,7},{4,0},{5,1},{6,2},{7,3},{8,12},{9,13},{10... | collective-permute-start | bytes 786440 | tf_op jit(solution)/shard_map/ppermute | solution.py:127
  60.3 1.5 collective-permute-start.16
  60.7 21.4 %collective-permute-start.17 = (bf16[128,1024]{1,0:T(8,128)(2,1)S(1)}, bf16[128,1024]{1,0:T(8,128)(2,1)S(1)}, u32[]{:S(2)}, u32[]{:S(2)}) collective-permute-start(bf16[128,1024]{1,0:T(8,128)(2,1)S(1)} %get-tuple-element.60.own_ref), channel_id=1, source_target_pairs={{0,4},{1,5},{2,6},{3,7},{4,0},{5,1},{6,2},{7,3},{8,12},{9,10},{10,... | collective-permute-start | bytes 786440 | tf_op jit(solution)/shard_map/ppermute | solution.py:127
  61.8 20.3 %collective-permute-start.20 = (bf16[128,1024]{1,0:T(8,128)(2,1)S(1)}, bf16[128,1024]{1,0:T(8,128)(2,1)S(1)}, u32[]{:S(2)}, u32[]{:S(2)}) collective-permute-start(bf16[128,1024]{1,0:T(8,128)(2,1)S(1)} %get-tuple-element.63.own_ref), channel_id=1, source_target_pairs={{0,4},{1,5},{2,6},{3,7},{4,0},{5,1},{6,2},{7,3},{8,12},{9,10},{10,... | collective-permute-start | bytes 786440 | tf_op jit(solution)/shard_map/ppermute | solution.py:127
  82.1 1.3 copy-start.1
  83.4 4.9 %collective-permute-start.22 = (bf16[2048,512]{1,0:T(8,128)(2,1)S(1)}, bf16[2048,512]{1,0:T(8,128)(2,1)S(1)}, u32[]{:S(2)}, u32[]{:S(2)}) collective-permute-start(bf16[2048,512]{1,0:T(8,128)(2,1)S(1)} %collective-permute-done.18.refs_1_), channel_id=1, source_target_pairs={{0,4},{1,5},{2,6},{3,7},{4,0},{5,1},{6,2},{7,3},{8,12},{9,13},{10,... | collective-permute-start | bytes 6291464 | tf_op jit(solution)/shard_map/ppermute | solution.py:127
  83.4 4.5 %collective-permute-start.19 = (bf16[128,1024]{1,0:T(8,128)(2,1)S(1)}, bf16[128,1024]{1,0:T(8,128)(2,1)S(1)}, u32[]{:S(2)}, u32[]{:S(2)}) collective-permute-start(bf16[128,1024]{1,0:T(8,128)(2,1)S(1)} %get-tuple-element.62), channel_id=1, source_target_pairs={{0,4},{1,5},{2,6},{3,7},{4,0},{5,1},{6,2},{7,3},{8,12},{9,17},{10,... | collective-permute-start | bytes 786440 | tf_op jit(solution)/shard_map/ppermute | solution.py:127
  83.9 4.4 %collective-permute-start.21 = (bf16[128,1024]{1,0:T(8,128)(2,1)S(1)}, bf16[128,1024]{1,0:T(8,128)(2,1)S(1)}, u32[]{:S(2)}, u32[]{:S(2)}) collective-permute-start(bf16[128,1024]{1,0:T(8,128)(2,1)S(1)} %get-tuple-element.62), channel_id=1, source_target_pairs={{0,4},{1,5},{2,6},{3,7},{4,0},{5,1},{6,2},{7,3},{8,12},{9,18},{10,... | collective-permute-start | bytes 786440 | tf_op jit(solution)/shard_map/ppermute | solution.py:127
  83.9 4.8 %collective-permute-start.23 = (bf16[128,1024]{1,0:T(8,128)(2,1)S(1)}, bf16[128,1024]{1,0:T(8,128)(2,1)S(1)}, u32[]{:S(2)}, u32[]{:S(2)}) collective-permute-start(bf16[128,1024]{1,0:T(8,128)(2,1)S(1)} %get-tuple-element.64), channel_id=1, source_target_pairs={{0,4},{1,5},{2,6},{3,7},{4,0},{5,1},{6,2},{7,3},{8,12},{9,17},{10,... | collective-permute-start | bytes 786440 | tf_op jit(solution)/shard_map/ppermute | solution.py:127
  84.4 4.6 %collective-permute-start.24 = (bf16[128,1024]{1,0:T(8,128)(2,1)S(1)}, bf16[128,1024]{1,0:T(8,128)(2,1)S(1)}, u32[]{:S(2)}, u32[]{:S(2)}) collective-permute-start(bf16[128,1024]{1,0:T(8,128)(2,1)S(1)} %get-tuple-element.64), channel_id=1, source_target_pairs={{0,4},{1,5},{2,6},{3,7},{4,0},{5,1},{6,2},{7,3},{8,12},{9,18},{10,... | collective-permute-start | bytes 786440 | tf_op jit(solution)/shard_map/ppermute | solution.py:127
  88.3 6.3 %collective-permute-start.25 = (bf16[128,1024]{1,0:T(8,128)(2,1)S(1)}, bf16[128,1024]{1,0:T(8,128)(2,1)S(1)}, u32[]{:S(2)}, u32[]{:S(2)}) collective-permute-start(bf16[128,1024]{1,0:T(8,128)(2,1)S(1)} %get-tuple-element.72.own_ref), channel_id=1, source_target_pairs={{0,4},{1,5},{2,6},{3,7},{4,0},{5,1},{6,2},{7,3},{8,12},{9,21},{10,... | collective-permute-start | bytes 786440 | tf_op jit(solution)/shard_map/ppermute | solution.py:127
  89.1 6.2 %collective-permute-start.27 = (bf16[128,1024]{1,0:T(8,128)(2,1)S(1)}, bf16[128,1024]{1,0:T(8,128)(2,1)S(1)}, u32[]{:S(2)}, u32[]{:S(2)}) collective-permute-start(bf16[128,1024]{1,0:T(8,128)(2,1)S(1)} %get-tuple-element.75.own_ref), channel_id=1, source_target_pairs={{0,4},{1,5},{2,6},{3,7},{4,0},{5,1},{6,2},{7,3},{8,12},{9,21},{10,... | collective-permute-start | bytes 786440 | tf_op jit(solution)/shard_map/ppermute | solution.py:127
  89.3 49.6 %collective-permute-start.35 = (bf16[2048,512]{1,0:T(8,128)(2,1)}, bf16[2048,512]{1,0:T(8,128)(2,1)}, u32[]{:S(2)}, u32[]{:S(2)}) collective-permute-start(bf16[2048,512]{1,0:T(8,128)(2,1)} %bitcast.5.refs_0_), channel_id=1, source_target_pairs={{0,1},{3,2},{4,5},{7,6},{8,9},{11,10},{12,13},{15,14},{16,17},{19,... | collective-permute-start | bytes 6291464 | tf_op jit(solution)/shard_map/ppermute | solution.py:127
  94.7 1.8 %collective-permute-start.26 = (bf16[128,1024]{1,0:T(8,128)(2,1)S(1)}, bf16[128,1024]{1,0:T(8,128)(2,1)S(1)}, u32[]{:S(2)}, u32[]{:S(2)}) collective-permute-start(bf16[128,1024]{1,0:T(8,128)(2,1)S(1)} %get-tuple-element.74), channel_id=1, source_target_pairs={{0,4},{1,9},{2,10},{3,7},{4,0},{5,1},{6,2},{7,3},{8,12},{9,13},{10... | collective-permute-start | bytes 786440 | tf_op jit(solution)/shard_map/ppermute | solution.py:127
  94.8 1.9 %collective-permute-start.28 = (bf16[128,1024]{1,0:T(8,128)(2,1)S(1)}, bf16[128,1024]{1,0:T(8,128)(2,1)S(1)}, u32[]{:S(2)}, u32[]{:S(2)}) collective-permute-start(bf16[128,1024]{1,0:T(8,128)(2,1)S(1)} %get-tuple-element.74), channel_id=1, source_target_pairs={{0,4},{1,9},{2,10},{3,7},{4,0},{5,1},{6,2},{7,3},{8,12},{9,13},{10... | collective-permute-start | bytes 786440 | tf_op jit(solution)/shard_map/ppermute | solution.py:127
  95.3 0.7 copy-start.4
  96.0 1.5 collective-permute-start.29
  96.1 1.8 %collective-permute-start.30 = (bf16[128,1024]{1,0:T(8,128)(2,1)S(1)}, bf16[128,1024]{1,0:T(8,128)(2,1)S(1)}, u32[]{:S(2)}, u32[]{:S(2)}) collective-permute-start(bf16[128,1024]{1,0:T(8,128)(2,1)S(1)} %get-tuple-element.77), channel_id=1, source_target_pairs={{0,4},{1,9},{2,10},{3,7},{4,0},{5,1},{6,2},{7,3},{8,12},{9,13},{10... | collective-permute-start | bytes 786440 | tf_op jit(solution)/shard_map/ppermute | solution.py:127
  98.6 1.9 %collective-permute-start.32 = (bf16[128,1024]{1,0:T(8,128)(2,1)}, bf16[128,1024]{1,0:T(8,128)(2,1)}, u32[]{:S(2)}, u32[]{:S(2)}) collective-permute-start(bf16[128,1024]{1,0:T(8,128)(2,1)} %get-tuple-element.84.own_ref), channel_id=1, source_target_pairs={{0,4},{1,29},{2,30},{3,7},{4,0},{5,6},{6,5},{7,3},{8,12},{9,13},{1... | collective-permute-start | bytes 786440 | tf_op jit(solution)/shard_map/ppermute | solution.py:127
  98.8 6.0 %collective-permute-start.31 = (bf16[128,1024]{1,0:T(8,128)(2,1)}, bf16[128,1024]{1,0:T(8,128)(2,1)}, u32[]{:S(2)}, u32[]{:S(2)}) collective-permute-start(bf16[128,1024]{1,0:T(8,128)(2,1)} %get-tuple-element.85.own_ref), channel_id=1, source_target_pairs={{0,4},{1,29},{2,30},{3,7},{4,0},{5,6},{6,5},{7,3},{8,12},{9,13},{1... | collective-permute-start | bytes 786440 | tf_op jit(solution)/shard_map/ppermute | solution.py:127
  99.2 7.5 %collective-permute-start.36 = (bf16[128,1024]{1,0:T(8,128)(2,1)S(1)}, bf16[128,1024]{1,0:T(8,128)(2,1)}, u32[]{:S(2)}, u32[]{:S(2)}) collective-permute-start(bf16[128,1024]{1,0:T(8,128)(2,1)S(1)} %get-tuple-element.86.refs_3_), channel_id=1, source_target_pairs={{0,4},{1,5},{2,6},{3,7},{4,0},{5,1},{6,2},{7,3},{8,12},{9,13},{10,... | collective-permute-start | bytes 786440 | tf_op jit(solution)/shard_map/ppermute | solution.py:127
  99.3 9.1 %collective-permute-start.42 = (bf16[128,1024]{1,0:T(8,128)(2,1)}, bf16[128,1024]{1,0:T(8,128)(2,1)S(1)}, u32[]{:S(2)}, u32[]{:S(2)}) collective-permute-start(bf16[128,1024]{1,0:T(8,128)(2,1)} %copy-done.4), channel_id=1, source_target_pairs={{0,4},{1,5},{2,6},{3,7},{4,0},{5,1},{6,2},{7,3},{8,12},{9,13},{10,... | collective-permute-start | bytes 786440 | tf_op jit(solution)/shard_map/ppermute | solution.py:127
  100.5 1.6 copy-start.2
  102.1 0.9 copy-start.5
  106.6 2.4 %collective-permute-start.33 = (bf16[128,1024]{1,0:T(8,128)(2,1)S(1)}, bf16[128,1024]{1,0:T(8,128)(2,1)S(1)}, u32[]{:S(2)}, u32[]{:S(2)}) collective-permute-start(bf16[128,1024]{1,0:T(8,128)(2,1)S(1)} %get-tuple-element.90), channel_id=1, source_target_pairs={{0,4},{1,5},{2,6},{3,7},{4,0},{5,1},{6,2},{7,3},{8,12},{9,13},{10,... | collective-permute-start | bytes 786440 | tf_op jit(solution)/shard_map/ppermute | solution.py:127
  107.8 31.1 %collective-permute-start.37 = (bf16[128,1024]{1,0:T(8,128)(2,1)S(1)}, bf16[128,1024]{1,0:T(8,128)(2,1)S(1)}, u32[]{:S(2)}, u32[]{:S(2)}) collective-permute-start(bf16[128,1024]{1,0:T(8,128)(2,1)S(1)} %get-tuple-element.93.own_ref), channel_id=1, source_target_pairs={{0,4},{1,29},{2,30},{3,7},{4,0},{5,6},{6,5},{7,3},{8,12},{9,10},{1... | collective-permute-start | bytes 786440 | tf_op jit(solution)/shard_map/ppermute | solution.py:127
  108.2 1.5 collective-permute-start.40
  108.5 38.9 %collective-permute-start.43 = (bf16[128,1024]{1,0:T(8,128)(2,1)S(1)}, bf16[128,1024]{1,0:T(8,128)(2,1)}, u32[]{:S(2)}, u32[]{:S(2)}) collective-permute-start(bf16[128,1024]{1,0:T(8,128)(2,1)S(1)} %get-tuple-element.99.own_ref), channel_id=1, source_target_pairs={{0,4},{1,29},{2,30},{3,7},{4,0},{5,6},{6,5},{7,3},{8,12},{9,10},{1... | collective-permute-start | bytes 786440 | tf_op jit(solution)/shard_map/ppermute | solution.py:127
  109.0 34.6 %collective-permute-start.34 = (bf16[128,1024]{1,0:T(8,128)(2,1)S(1)}, bf16[128,1024]{1,0:T(8,128)(2,1)S(1)}, u32[]{:S(2)}, u32[]{:S(2)}) collective-permute-start(bf16[128,1024]{1,0:T(8,128)(2,1)S(1)} %get-tuple-element.104.own_ref), channel_id=1, source_target_pairs={{0,4},{1,2},{2,1},{3,7},{4,0},{5,25},{6,26},{7,3},{8,12},{9,13},{1... | collective-permute-start | bytes 786440 | tf_op jit(solution)/shard_map/ppermute | solution.py:127
  109.9 41.2 %collective-permute-start.41 = (bf16[128,1024]{1,0:T(8,128)(2,1)S(1)}, bf16[128,1024]{1,0:T(8,128)(2,1)S(1)}, u32[]{:S(2)}, u32[]{:S(2)}) collective-permute-start(bf16[128,1024]{1,0:T(8,128)(2,1)S(1)} %get-tuple-element.108.own_ref), channel_id=1, source_target_pairs={{0,4},{1,2},{2,1},{3,7},{4,0},{5,25},{6,26},{7,3},{8,12},{9,13},{1... | collective-permute-start | bytes 786440 | tf_op jit(solution)/shard_map/ppermute | solution.py:127
  141.1 14.4 %collective-permute-start.39 = (bf16[128,512]{1,0:T(8,128)(2,1)S(1)}, bf16[128,512]{1,0:T(8,128)(2,1)}, u32[]{:S(2)}, u32[]{:S(2)}) collective-permute-start(bf16[128,512]{1,0:T(8,128)(2,1)S(1)} %slice.64), channel_id=1, source_target_pairs={{0,1},{1,0},{3,2},{2,3},{4,5},{5,4},{7,6},{6,7},{8,9},{9,8},{11,10... | collective-permute-start | bytes 393224 | tf_op jit(solution)/shard_map/ppermute | solution.py:127
  146.6 8.9 %collective-permute-start.38 = (bf16[128,512]{1,0:T(8,128)(2,1)S(1)}, bf16[128,512]{1,0:T(8,128)(2,1)S(1)}, u32[]{:S(2)}, u32[]{:S(2)}) collective-permute-start(bf16[128,512]{1,0:T(8,128)(2,1)S(1)} %slice.52), channel_id=1, source_target_pairs={{0,1},{1,0},{2,3},{3,2},{4,24},{5,25},{6,26},{7,27},{8,12},{9,13},... | collective-permute-start | bytes 393224 | tf_op jit(solution)/shard_map/ppermute | solution.py:127
  149.7 5.9 %collective-permute-start.45 = (bf16[128,512]{1,0:T(8,128)(2,1)S(1)}, bf16[128,512]{1,0:T(8,128)(2,1)S(1)}, u32[]{:S(2)}, u32[]{:S(2)}) collective-permute-start(bf16[128,512]{1,0:T(8,128)(2,1)S(1)} %slice.65), channel_id=1, source_target_pairs={{0,1},{1,0},{3,2},{2,3},{4,5},{5,4},{7,6},{6,7},{8,9},{9,8},{11,10... | collective-permute-start | bytes 393224 | tf_op jit(solution)/shard_map/ppermute | solution.py:127
  154.0 5.0 %collective-permute-start.44 = (bf16[128,512]{1,0:T(8,128)(2,1)S(1)}, bf16[128,512]{1,0:T(8,128)(2,1)S(1)}, u32[]{:S(2)}, u32[]{:S(2)}) collective-permute-start(bf16[128,512]{1,0:T(8,128)(2,1)S(1)} %slice.55), channel_id=1, source_target_pairs={{0,1},{1,0},{2,3},{3,2},{4,24},{5,25},{6,26},{7,27},{8,12},{9,13},... | collective-permute-start | bytes 393224 | tf_op jit(solution)/shard_map/ppermute | solution.py:127

commit v5 on v2

--- a/solution.py
+++ b/solution.py
@@ -118,7 +118,7 @@
     out_ref = rest.pop(0)
     kept_ref = rest.pop(0) if "kept" in extras else None
     work = functools.partial(
-        multiply, width, own_ref, other_ref, operators, named.get("addend"), out_ref, kept_ref, rest[:-1], rest[-1]
+        multiply, width, own_ref, other_ref, operators, named.get("addend"), out_ref, kept_ref, rest[:-1], rest[-1:]
     )
     if turn is None:
         work()
@@ -145,11 +145,21 @@
     down = [half - 1 - i for i in range(half)]
     up = [half + i for i in range(half)]
     blocks = [jnp.where(lower, x, y) for x, y in zip(down + up, up + down)]
+    if not tiles:
+        totals = [0.0] * pieces
+        for t, block in enumerate(blocks):
+            source = own_ref if t < half else other_ref
+            rows = source[:, (t % half) * depth:(t % half + 1) * depth]
+            deep = pl.ds(pl.multiple_of(block * depth, depth), depth)
+            for i, operator in enumerate(operators):
+                totals[i] += jnp.dot(rows, operator[deep, :], preferred_element_type=jnp.float32)
+        finish(totals, add_ref, out_ref, kept_ref)
+        return
     copies = []
     for t, block in enumerate(blocks):
         rows = pl.ds(pl.multiple_of(block * depth, depth), depth)
         group = [
-            pltpu.make_async_copy(operator.at[rows, :], tile.at[t], sems.at[i, t])
+            pltpu.make_async_copy(operator.at[rows, :], tile.at[t], sems[0].at[i, t])
             for i, (operator, tile) in enumerate(zip(operators, tiles))
         ]
         for copy in group:
@@ -162,6 +172,10 @@
         for i, copy in enumerate(group):
             copy.wait()
             totals[i] += jnp.dot(rows, tiles[i][t], preferred_element_type=jnp.float32)
+    finish(totals, add_ref, out_ref, kept_ref)
+
+
+def finish(totals, add_ref, out_ref, kept_ref):
     start = 0
     for total in totals:
         stop = start + total.shape[1]
@@ -174,7 +188,7 @@
         start = stop
 
 
-def applied(own, other, pieces, addend=None, kept=None, turn=None):
+def applied(own, other, pieces, addend=None, kept=None, turn=None, resident=False):
     width = lax.axis_size("trace")
     rows = own.shape[0]
     deep = pieces[0].shape[0]
@@ -183,24 +197,27 @@
     hbm = pl.BlockSpec(memory_space=pltpu.HBM)
     extras = {name: value for name, value in (("addend", addend), ("kept", kept)) if value is not None}
     outs = 1 if kept is None else 2
+    scratch = [] if resident else (
+        [pltpu.VMEM((width, deep // width, piece.shape[1]), piece.dtype) for piece in pieces]
+        + [pltpu.SemaphoreType.DMA((len(pieces), width))]
+    )
     return pl.pallas_call(
         functools.partial(apply_kernel, width, len(pieces), tuple(extras), turn),
         out_shape=[jax.ShapeDtypeStruct((rows, columns), jnp.bfloat16)] * outs,
-        in_specs=[vmem, vmem] + [hbm] * len(pieces) + [vmem] * len(extras),
+        in_specs=[vmem, vmem] + [vmem if resident else hbm] * len(pieces) + [vmem] * len(extras),
         out_specs=[vmem] * outs,
-        scratch_shapes=[pltpu.VMEM((width, deep // width, piece.shape[1]), piece.dtype) for piece in pieces]
-        + [pltpu.SemaphoreType.DMA((len(pieces), width))],
-        compiler_params=pltpu.CompilerParams(vmem_limit_bytes=16 * 1024 * 1024),
+        scratch_shapes=scratch,
+        compiler_params=pltpu.CompilerParams(vmem_limit_bytes=8 * 1024 * 1024),
         cost_estimate=pl.CostEstimate(
             flops=2 * rows * columns * deep, bytes_accessed=2 * columns * deep, transcendentals=0
         ),
     )(own, other, *pieces, *extras.values())
 
 
-def in_turn(rows, pieces, addends, last, kept, turn):
+def in_turn(rows, pieces, addends, last, kept, turn, resident):
     fresh = []
     for i, ((own, other), addend) in enumerate(zip(rows, addends)):
-        outs = applied(after(own, last), other, pieces, addend, kept[i] if kept else None, turn)
+        outs = applied(after(own, last), other, pieces, addend, kept[i] if kept else None, turn, resident)
         last = outs[0]
         fresh.append(outs)
     return [outs[0] for outs in fresh], [outs[-1] for outs in fresh]
@@ -243,7 +260,7 @@
         for hop, one_far, one_near in zip(hops, far_outward, near_outward):
             here = (z == places.ends(hop)[0][0]) | (z == places.ends(hop)[1][0])
             near, far = jnp.where(here, one_near, near), jnp.where(here, one_far, far)
-        driven_parts += applied(near, far, [response[0]])
+        driven_parts += applied(near, far, [response[0]], resident=True)
     driven_sent = jnp.concatenate(driven_parts, 0)
 
     transfer = transmission[0]
@@ -271,11 +288,11 @@
             for part in traces:
                 crossed = move(part, places.hop(stage, True))
                 arrived.append((move(part, places.hop(stage, False)), crossed))
-            traces, firsts = in_turn(arrived, first_pieces, first_parts, traces[-1], firsts, turn)
+            traces, firsts = in_turn(arrived, first_pieces, first_parts, traces[-1], firsts, turn, True)
         others = []
         for part in traces:
             others.append(move(part, places.swap(stage)))
-        traces, seconds = in_turn(list(zip(traces, others)), second_pieces, second_parts, traces[-1], seconds, turn)
+        traces, seconds = in_turn(list(zip(traces, others)), second_pieces, second_parts, traces[-1], seconds, turn, early)
         if stage == 0:
             first_early = [move(after(piece, traces[-1]), places.across_cores()) for piece in second_early]
         if stage == min(1, places.columns - 1):

time: 151 us -> 149 us (0.987)
  starting transfers between devices: 48.9 us -> 45.3 us
  waiting for transfers between devices: 91.7 us -> 93.3 us
    ppermute x40, starting transfers between devices: 48.9 us -> 45.3 us  [move(): return lax.ppermute(values, AXES, pairs)]
    ppermute x40, waiting for transfers between devices: 91.7 us -> 93.3 us  [move(): return lax.ppermute(values, AXES, pairs)]
  transfers between devices with their start and end apart: 40 -> 40, of which waited for: 24 -> 25; matrix products, arithmetic and copies ran while one was open for 1% -> 1% of each run, Pallas kernels for 3% -> 2%
where the time goes in v5:
time: 149 us; the launch traced here: 147 us
  waiting for transfers between devices  93.3 us (63%)
  starting transfers between devices  45.3 us (30%)
  other arithmetic  4.17 us (3%)
  Pallas kernels  3.03 us (2%)
    ppermute x40, waiting for transfers between devices, move(): return lax.ppermute(values, AXES, pairs)  93.3 us
    ppermute x40, starting transfers between devices, move(): return lax.ppermute(values, AXES, pairs)  45.3 us
    pallas_call x18, Pallas kernels, applied(): pl.pallas_call(functools.partial(apply_kernel, width, len(pieces), tuple(...  3.03 us
  transfers between devices with their start and end apart: 40, of which 25 were waited for; matrix products, arithmetic and copies ran while one was open for 1% of the time, Pallas kernels for 2%

profile of v5, /device:TPU:0, one launch (start us, length us, event | category | flops | bytes accessed | tf_op | source)
XLA Modules:
  0.0 147.4 jit_solution(7748316234932544987)
XLA Ops:
  0.0 0.8 add_divide_fusion
  0.8 1.1 fusion.4
  1.9 3.1 %collective-permute-start.3 = (bf16[128,512]{1,0:T(8,128)(2,1)S(1)}, bf16[128,512]{1,0:T(8,128)(2,1)S(1)}, u32[]{:S(2)}, u32[]{:S(2)}) collective-permute-start(bf16[128,512]{1,0:T(8,128)(2,1)S(1)} %bitcast.25), channel_id=1, source_target_pairs={{0,1},{1,0},{3,2},{2,3},{4,5},{5,4},{7,6},{6,7},{8,9},{9,8},{11,10... | collective-permute-start | bytes 393224 | tf_op jit(solution)/shard_map/ppermute | solution.py:104
  5.1 3.5 %collective-permute-done.3 = bf16[128,512]{1,0:T(8,128)(2,1)S(1)} collective-permute-done((bf16[128,512]{1,0:T(8,128)(2,1)S(1)}, bf16[128,512]{1,0:T(8,128)(2,1)S(1)}, u32[]{:S(2)}, u32[]{:S(2)}) %collective-permute-start.3) | collective-permute-done | bytes 131104 | tf_op jit(solution)/shard_map/ppermute | solution.py:104
  8.7 3.3 %collective-permute-start = (bf16[128,512]{1,0:T(8,128)(2,1)S(1)}, bf16[128,512]{1,0:T(8,128)(2,1)S(1)}, u32[]{:S(2)}, u32[]{:S(2)}) collective-permute-start(bf16[128,512]{1,0:T(8,128)(2,1)S(1)} %bitcast.23), channel_id=1, source_target_pairs={{0,1},{1,0},{3,2},{2,3},{4,5},{5,4},{7,6},{6,7},{8,9},{9,8},{11,10... | collective-permute-start | bytes 393224 | tf_op jit(solution)/shard_map/ppermute | solution.py:104
  12.0 0.8 collective-permute-start.9
  12.8 1.4 collective-permute-start.8
  14.3 0.7 collective-permute-done
  15.2 1.3 collective-permute-start.5
  16.5 2.2 %collective-permute-done.1 = bf16[128,1024]{1,0:T(8,128)(2,1)S(1)} collective-permute-done((bf16[128,1024]{1,0:T(8,128)(2,1)S(1)}, bf16[128,1024]{1,0:T(8,128)(2,1)S(1)}, u32[]{:S(2)}, u32[]{:S(2)}) %collective-permute-start.1) | collective-permute-done | bytes 262176 | tf_op jit(solution)/shard_map/ppermute | solution.py:104
  18.6 1.3 collective-permute-start.2
  19.9 6.5 %collective-permute-done.5 = bf16[128,1024]{1,0:T(8,128)(2,1)S(1)} collective-permute-done((bf16[128,1024]{1,0:T(8,128)(2,1)S(1)}, bf16[128,1024]{1,0:T(8,128)(2,1)S(1)}, u32[]{:S(2)}, u32[]{:S(2)}) %collective-permute-start.5) | collective-permute-done | bytes 262176 | tf_op jit(solution)/shard_map/ppermute | solution.py:104
  26.4 0.5 shard_map.56
  26.9 4.5 %collective-permute-done.2 = bf16[128,1024]{1,0:T(8,128)(2,1)S(1)} collective-permute-done((bf16[128,1024]{1,0:T(8,128)(2,1)S(1)}, bf16[128,1024]{1,0:T(8,128)(2,1)S(1)}, u32[]{:S(2)}, u32[]{:S(2)}) %collective-permute-start.2) | collective-permute-done | bytes 262176 | tf_op jit(solution)/shard_map/ppermute | solution.py:104
  31.4 0.5 shard_map.55
  32.0 7.7 %collective-permute-done.6 = bf16[256,512]{1,0:T(8,128)(2,1)S(1)} collective-permute-done((bf16[256,512]{1,0:T(8,128)(2,1)S(1)}, bf16[256,512]{1,0:T(8,128)(2,1)S(1)}, u32[]{:S(2)}, u32[]{:S(2)}) %collective-permute-start.6) | collective-permute-done | bytes 262176 | tf_op jit(solution)/shard_map/ppermute | solution.py:104
  39.8 3.2 %collective-permute-start.10 = (bf16[256,1024]{1,0:T(8,128)(2,1)S(1)}, bf16[256,1024]{1,0:T(8,128)(2,1)S(1)}, u32[]{:S(2)}, u32[]{:S(2)}) collective-permute-start(bf16[256,1024]{1,0:T(8,128)(2,1)S(1)} %pad_maximum_fusion), channel_id=1, source_target_pairs={{0,4},{1,5},{2,6},{3,7},{4,0},{5,1},{6,2},{7,3},{8,12},{9,13},{10,... | collective-permute-start | bytes 1572872 | tf_op jit(solution)/shard_map/ppermute | solution.py:104
  43.1 0.5 collective-permute-start.12
  43.6 0.9 collective-permute-done.10
  44.6 0.3 collective-permute-done.7.other_ref
  45.0 0.3 collective-permute-done.12.other_ref
  45.3 0.4 collective-permute-start.14
  45.8 1.1 copy-done
  46.9 11.4 %collective-permute-start.18 = (bf16[2048,512]{1,0:T(8,128)(2,1)S(1)}, bf16[2048,512]{1,0:T(8,128)(2,1)S(1)}, u32[]{:S(2)}, u32[]{:S(2)}) collective-permute-start(bf16[2048,512]{1,0:T(8,128)(2,1)S(1)} %bitcast.11), channel_id=1, source_target_pairs={{0,5},{3,6},{12,9},{15,10},{16,21},{19,22},{28,25},{31,26}} | collective-permute-start | bytes 6291464 | tf_op jit(solution)/shard_map/ppermute | solution.py:104
  58.3 0.5 collective-permute-start.13
  58.9 1.0 collective-permute-done.11.own_ref
  59.9 0.1 collective-permute-start.16
  60.0 0.2 collective-permute-done.13.other_ref
  60.3 0.2 collective-permute-start.17
  60.5 0.1 collective-permute-done.15.own_ref
  60.6 0.8 collective-permute-done.16.other_ref
  61.4 0.2 collective-permute-start.20
  61.6 20.1 %collective-permute-done.18.refs_1_ = bf16[2048,512]{1,0:T(8,128)(2,1)S(1)} collective-permute-done((bf16[2048,512]{1,0:T(8,128)(2,1)S(1)}, bf16[2048,512]{1,0:T(8,128)(2,1)S(1)}, u32[]{:S(2)}, u32[]{:S(2)}) %collective-permute-start.18) | collective-permute-done | bytes 2097184 | tf_op jit(solution)/shard_map/ppermute | solution.py:104
  81.8 0.5 collective-permute-start.19
  82.4 0.4 collective-permute-start.23
  82.9 3.4 %collective-permute-done.19.own_ref = bf16[128,1024]{1,0:T(8,128)(2,1)S(1)} collective-permute-done((bf16[128,1024]{1,0:T(8,128)(2,1)S(1)}, bf16[128,1024]{1,0:T(8,128)(2,1)S(1)}, u32[]{:S(2)}, u32[]{:S(2)}) %collective-permute-start.19) | collective-permute-done | bytes 262176 | tf_op jit(solution)/shard_map/ppermute | solution.py:104
  86.4 5.2 %collective-permute-start.34 = (bf16[2048,512]{1,0:T(8,128)(2,1)S(1)}, bf16[2048,512]{1,0:T(8,128)(2,1)}, u32[]{:S(2)}, u32[]{:S(2)}) collective-permute-start(bf16[2048,512]{1,0:T(8,128)(2,1)S(1)} %bitcast.20), channel_id=1, source_target_pairs={{0,1},{3,2},{4,5},{7,6},{8,9},{11,10},{12,13},{15,14},{16,17},{19,... | collective-permute-start | bytes 6291464 | tf_op jit(solution)/shard_map/ppermute | solution.py:104
  91.6 0.2 collective-permute-start.25
  91.8 0.5 collective-permute-start.27
  92.3 0.9 collective-permute-done.25.other_ref
  93.3 0.2 collective-permute-start.28
  93.5 0.4 collective-permute-start.26
  94.0 0.2 collective-permute-start.29
  94.1 0.4 collective-permute-start.30
  94.5 0.7 collective-permute-done.26.own_ref
  95.3 0.3 collective-permute-done.29.own_ref
  95.6 0.4 collective-permute-done.30.other_ref
  96.0 0.2 collective-permute-start.36
  96.2 0.4 collective-permute-start.31
  96.6 1.0 collective-permute-done.36.other_ref
  97.6 0.7 shard_map.71
  98.5 0.7 shard_map.69
  99.2 0.4 collective-permute-start.32
  99.6 0.3 collective-permute-done.37
  100.0 0.2 collective-permute-start.38
  100.2 0.7 collective-permute-done.32
  100.9 1.1 convert_add_fusion.1
  102.0 0.4 collective-permute-start.33
  102.4 33.2 %collective-permute-done.34.refs_1_ = bf16[2048,512]{1,0:T(8,128)(2,1)} collective-permute-done((bf16[2048,512]{1,0:T(8,128)(2,1)S(1)}, bf16[2048,512]{1,0:T(8,128)(2,1)}, u32[]{:S(2)}, u32[]{:S(2)}) %collective-permute-start.34) | collective-permute-done | bytes 2097184 | tf_op jit(solution)/shard_map/ppermute | solution.py:104
  135.7 4.9 %collective-permute-start.39 = (bf16[128,512]{1,0:T(8,128)(2,1)S(1)}, bf16[128,512]{1,0:T(8,128)(2,1)S(1)}, u32[]{:S(2)}, u32[]{:S(2)}) collective-permute-start(bf16[128,512]{1,0:T(8,128)(2,1)S(1)} %slice.58), channel_id=1, source_target_pairs={{0,1},{1,0},{3,2},{2,3},{4,5},{5,4},{7,6},{6,7},{8,9},{9,8},{11,10... | collective-permute-start | bytes 393224 | tf_op jit(solution)/shard_map/ppermute | solution.py:104
  140.7 2.4 %collective-permute-start.35 = (bf16[128,512]{1,0:T(8,128)(2,1)S(1)}, bf16[128,512]{1,0:T(8,128)(2,1)S(1)}, u32[]{:S(2)}, u32[]{:S(2)}) collective-permute-start(bf16[128,512]{1,0:T(8,128)(2,1)S(1)} %slice.56), channel_id=1, source_target_pairs={{0,1},{1,0},{3,2},{2,3},{4,5},{5,4},{7,6},{6,7},{8,9},{9,8},{11,10... | collective-permute-start | bytes 393224 | tf_op jit(solution)/shard_map/ppermute | solution.py:104
  143.1 1.1 collective-permute-done.39
  144.2 2.4 %collective-permute-done.35 = bf16[128,512]{1,0:T(8,128)(2,1)S(1)} collective-permute-done((bf16[128,512]{1,0:T(8,128)(2,1)S(1)}, bf16[128,512]{1,0:T(8,128)(2,1)S(1)}, u32[]{:S(2)}, u32[]{:S(2)}) %collective-permute-start.35) | collective-permute-done | bytes 131104 | tf_op jit(solution)/shard_map/ppermute | solution.py:104
  146.6 0.7 pad_maximum_fusion.4
  (58 shorter events, 2.0 us)
Async XLA Ops:
  0.0 26.4 %copy-start.1 = (bf16[1,2048,512]{2,1,0:T(8,128)(2,1)S(1)}, bf16[1,2048,512]{2,1,0:T(8,128)(2,1)}, u32[]{:S(2)}) copy-start(bf16[1,2048,512]{2,1,0:T(8,128)(2,1)} %param.7) | copy-start | bytes 6291460
  1.9 6.6 %collective-permute-start.3 = (bf16[128,512]{1,0:T(8,128)(2,1)S(1)}, bf16[128,512]{1,0:T(8,128)(2,1)S(1)}, u32[]{:S(2)}, u32[]{:S(2)}) collective-permute-start(bf16[128,512]{1,0:T(8,128)(2,1)S(1)} %bitcast.25), channel_id=1, source_target_pairs={{0,1},{1,0},{3,2},{2,3},{4,5},{5,4},{7,6},{6,7},{8,9},{9,8},{11,10... | collective-permute-start | bytes 393224 | tf_op jit(solution)/shard_map/ppermute | solution.py:104
  8.7 6.5 %collective-permute-start.4 = (bf16[128,1024]{1,0:T(8,128)(2,1)S(1)}, bf16[128,1024]{1,0:T(8,128)(2,1)S(1)}, u32[]{:S(2)}, u32[]{:S(2)}) collective-permute-start(bf16[128,1024]{1,0:T(8,128)(2,1)S(1)} %get-tuple-element.95), channel_id=1, source_target_pairs={{0,4},{1,2},{2,1},{3,7},{4,0},{5,6},{6,5},{7,3},{8,12},{9,10},{10,... | collective-permute-start | bytes 786440 | tf_op jit(solution)/shard_map/ppermute | solution.py:104
  8.7 6.2 %collective-permute-start = (bf16[128,512]{1,0:T(8,128)(2,1)S(1)}, bf16[128,512]{1,0:T(8,128)(2,1)S(1)}, u32[]{:S(2)}, u32[]{:S(2)}) collective-permute-start(bf16[128,512]{1,0:T(8,128)(2,1)S(1)} %bitcast.23), channel_id=1, source_target_pairs={{0,1},{1,0},{3,2},{2,3},{4,5},{5,4},{7,6},{6,7},{8,9},{9,8},{11,10... | collective-permute-start | bytes 393224 | tf_op jit(solution)/shard_map/ppermute | solution.py:104
  12.0 32.9 %collective-permute-start.9 = (bf16[2048,512]{1,0:T(8,128)(2,1)}, bf16[2048,512]{1,0:T(8,128)(2,1)S(1)}, u32[]{:S(2)}, u32[]{:S(2)}) collective-permute-start(bf16[2048,512]{1,0:T(8,128)(2,1)} %bitcast.9), channel_id=1, source_target_pairs={{4,1},{7,2},{8,13},{11,14},{20,17},{23,18},{24,29},{27,30}} | collective-permute-start | bytes 6291464 | tf_op jit(solution)/shard_map/ppermute | solution.py:104
  12.8 32.1 %collective-permute-start.8 = (bf16[2048,512]{1,0:T(8,128)(2,1)}, bf16[2048,512]{1,0:T(8,128)(2,1)S(1)}, u32[]{:S(2)}, u32[]{:S(2)}) collective-permute-start(bf16[2048,512]{1,0:T(8,128)(2,1)} %bitcast.10), channel_id=1, source_target_pairs={{0,4},{1,5},{2,6},{3,7},{4,0},{5,1},{6,2},{7,3},{8,12},{9,13},{10,... | collective-permute-start | bytes 6291464 | tf_op jit(solution)/shard_map/ppermute | solution.py:104
  15.1 3.5 %collective-permute-start.1 = (bf16[128,1024]{1,0:T(8,128)(2,1)S(1)}, bf16[128,1024]{1,0:T(8,128)(2,1)S(1)}, u32[]{:S(2)}, u32[]{:S(2)}) collective-permute-start(bf16[128,1024]{1,0:T(8,128)(2,1)S(1)} %get-tuple-element.91), channel_id=1, source_target_pairs={{0,4},{1,2},{2,1},{3,7},{4,0},{5,6},{6,5},{7,3},{8,12},{9,10},{10,... | collective-permute-start | bytes 786440 | tf_op jit(solution)/shard_map/ppermute | solution.py:104
  15.2 11.2 %collective-permute-start.5 = (bf16[128,1024]{1,0:T(8,128)(2,1)S(1)}, bf16[128,1024]{1,0:T(8,128)(2,1)S(1)}, u32[]{:S(2)}, u32[]{:S(2)}) collective-permute-start(bf16[128,1024]{1,0:T(8,128)(2,1)S(1)} %collective-permute-done.4), channel_id=1, source_target_pairs={{1,0},{2,3},{5,4},{6,7},{9,8},{10,11},{13,12},{14,15},{17,16},{18,... | collective-permute-start | bytes 786440 | tf_op jit(solution)/shard_map/ppermute | solution.py:104
  18.6 12.7 %collective-permute-start.2 = (bf16[128,1024]{1,0:T(8,128)(2,1)S(1)}, bf16[128,1024]{1,0:T(8,128)(2,1)S(1)}, u32[]{:S(2)}, u32[]{:S(2)}) collective-permute-start(bf16[128,1024]{1,0:T(8,128)(2,1)S(1)} %collective-permute-done.1), channel_id=1, source_target_pairs={{1,0},{2,3},{5,4},{6,7},{9,8},{10,11},{13,12},{14,15},{17,16},{18,... | collective-permute-start | bytes 786440 | tf_op jit(solution)/shard_map/ppermute | solution.py:104
  31.9 7.8 %collective-permute-start.6 = (bf16[256,512]{1,0:T(8,128)(2,1)S(1)}, bf16[256,512]{1,0:T(8,128)(2,1)S(1)}, u32[]{:S(2)}, u32[]{:S(2)}) collective-permute-start(bf16[256,512]{1,0:T(8,128)(2,1)S(1)} %pad_maximum_fusion.3), channel_id=1, source_target_pairs={{0,1},{1,0},{3,2},{2,3},{4,5},{5,4},{7,6},{6,7},{8,9},{9,8},{11,10... | collective-permute-start | bytes 786440 | tf_op jit(solution)/shard_map/ppermute | solution.py:104
  39.8 4.8 %collective-permute-start.10 = (bf16[256,1024]{1,0:T(8,128)(2,1)S(1)}, bf16[256,1024]{1,0:T(8,128)(2,1)S(1)}, u32[]{:S(2)}, u32[]{:S(2)}) collective-permute-start(bf16[256,1024]{1,0:T(8,128)(2,1)S(1)} %pad_maximum_fusion), channel_id=1, source_target_pairs={{0,4},{1,5},{2,6},{3,7},{4,0},{5,1},{6,2},{7,3},{8,12},{9,13},{10,... | collective-permute-start | bytes 1572872 | tf_op jit(solution)/shard_map/ppermute | solution.py:104
  43.0 1.9 %collective-permute-start.7 = (bf16[128,1024]{1,0:T(8,128)(2,1)S(1)}, bf16[128,1024]{1,0:T(8,128)(2,1)S(1)}, u32[]{:S(2)}, u32[]{:S(2)}) collective-permute-start(bf16[128,1024]{1,0:T(8,128)(2,1)S(1)} %get-tuple-element.89.refs_2_.refs_3_), channel_id=1, source_target_pairs={{0,4},{1,2},{2,1},{3,7},{4,0},{5,25},{6,26},{7,3},{8,12},{9,13},{1... | collective-permute-start | bytes 786440 | tf_op jit(solution)/shard_map/ppermute | solution.py:104
  43.1 2.2 %collective-permute-start.12 = (bf16[128,1024]{1,0:T(8,128)(2,1)S(1)}, bf16[128,1024]{1,0:T(8,128)(2,1)S(1)}, u32[]{:S(2)}, u32[]{:S(2)}) collective-permute-start(bf16[128,1024]{1,0:T(8,128)(2,1)S(1)} %get-tuple-element.45.own_ref.refs_2_.refs_3_), channel_id=1, source_target_pairs={{0,4},{1,2},{2,1},{3,7},{4,0},{5,25},{6,26},{7,3},{8,12},{9,13},{1... | collective-permute-start | bytes 786440 | tf_op jit(solution)/shard_map/ppermute | solution.py:104
  45.3 1.6 %copy-start = (bf16[1,2048,512]{2,1,0:T(8,128)(2,1)S(1)}, bf16[1,2048,512]{2,1,0:T(8,128)(2,1)}, u32[]{:S(2)}) copy-start(bf16[1,2048,512]{2,1,0:T(8,128)(2,1)} %param.5) | copy-start | bytes 6291460
  45.3 14.9 %collective-permute-start.14 = (bf16[2048,512]{1,0:T(8,128)(2,1)S(1)}, bf16[2048,512]{1,0:T(8,128)(2,1)S(1)}, u32[]{:S(2)}, u32[]{:S(2)}) collective-permute-start(bf16[2048,512]{1,0:T(8,128)(2,1)S(1)} %collective-permute-done.9.refs_1_), channel_id=1, source_target_pairs={{0,4},{1,5},{2,6},{3,7},{4,0},{5,1},{6,2},{7,3},{8,12},{9,13},{10,... | collective-permute-start | bytes 6291464 | tf_op jit(solution)/shard_map/ppermute | solution.py:104
  46.9 34.8 %collective-permute-start.18 = (bf16[2048,512]{1,0:T(8,128)(2,1)S(1)}, bf16[2048,512]{1,0:T(8,128)(2,1)S(1)}, u32[]{:S(2)}, u32[]{:S(2)}) collective-permute-start(bf16[2048,512]{1,0:T(8,128)(2,1)S(1)} %bitcast.11), channel_id=1, source_target_pairs={{0,5},{3,6},{12,9},{15,10},{16,21},{19,22},{28,25},{31,26}} | collective-permute-start | bytes 6291464 | tf_op jit(solution)/shard_map/ppermute | solution.py:104
  58.3 1.6 %collective-permute-start.11 = (bf16[128,1024]{1,0:T(8,128)(2,1)S(1)}, bf16[128,1024]{1,0:T(8,128)(2,1)S(1)}, u32[]{:S(2)}, u32[]{:S(2)}) collective-permute-start(bf16[128,1024]{1,0:T(8,128)(2,1)S(1)} %shard_map.57.refs_3_), channel_id=1, source_target_pairs={{0,4},{1,9},{2,10},{3,7},{4,0},{5,1},{6,2},{7,3},{8,12},{9,13},{10... | collective-permute-start | bytes 786440 | tf_op jit(solution)/shard_map/ppermute | solution.py:104
  58.3 1.9 %collective-permute-start.13 = (bf16[128,1024]{1,0:T(8,128)(2,1)S(1)}, bf16[128,1024]{1,0:T(8,128)(2,1)S(1)}, u32[]{:S(2)}, u32[]{:S(2)}) collective-permute-start(bf16[128,1024]{1,0:T(8,128)(2,1)S(1)} %shard_map.57.refs_3_), channel_id=1, source_target_pairs={{0,4},{1,10},{2,9},{3,7},{4,0},{5,1},{6,2},{7,3},{8,12},{9,13},{10... | collective-permute-start | bytes 786440 | tf_op jit(solution)/shard_map/ppermute | solution.py:104
  58.8 1.8 %collective-permute-start.15 = (bf16[128,1024]{1,0:T(8,128)(2,1)S(1)}, bf16[128,1024]{1,0:T(8,128)(2,1)S(1)}, u32[]{:S(2)}, u32[]{:S(2)}) collective-permute-start(bf16[128,1024]{1,0:T(8,128)(2,1)S(1)} %shard_map.58.refs_3_), channel_id=1, source_target_pairs={{0,4},{1,9},{2,10},{3,7},{4,0},{5,1},{6,2},{7,3},{8,12},{9,13},{10... | collective-permute-start | bytes 786440 | tf_op jit(solution)/shard_map/ppermute | solution.py:104
  59.9 1.5 %collective-permute-start.16 = (bf16[128,1024]{1,0:T(8,128)(2,1)S(1)}, bf16[128,1024]{1,0:T(8,128)(2,1)S(1)}, u32[]{:S(2)}, u32[]{:S(2)}) collective-permute-start(bf16[128,1024]{1,0:T(8,128)(2,1)S(1)} %shard_map.58.refs_3_), channel_id=1, source_target_pairs={{0,4},{1,10},{2,9},{3,7},{4,0},{5,1},{6,2},{7,3},{8,12},{9,13},{10... | collective-permute-start | bytes 786440 | tf_op jit(solution)/shard_map/ppermute | solution.py:104
  60.3 21.4 %collective-permute-start.17 = (bf16[128,1024]{1,0:T(8,128)(2,1)S(1)}, bf16[128,1024]{1,0:T(8,128)(2,1)S(1)}, u32[]{:S(2)}, u32[]{:S(2)}) collective-permute-start(bf16[128,1024]{1,0:T(8,128)(2,1)S(1)} %get-tuple-element.51.own_ref), channel_id=1, source_target_pairs={{0,4},{1,5},{2,6},{3,7},{4,0},{5,1},{6,2},{7,3},{8,12},{9,10},{10,... | collective-permute-start | bytes 786440 | tf_op jit(solution)/shard_map/ppermute | solution.py:104
  61.4 20.3 %collective-permute-start.20 = (bf16[128,1024]{1,0:T(8,128)(2,1)S(1)}, bf16[128,1024]{1,0:T(8,128)(2,1)S(1)}, u32[]{:S(2)}, u32[]{:S(2)}) collective-permute-start(bf16[128,1024]{1,0:T(8,128)(2,1)S(1)} %get-tuple-element.54.own_ref), channel_id=1, source_target_pairs={{0,4},{1,5},{2,6},{3,7},{4,0},{5,1},{6,2},{7,3},{8,12},{9,10},{10,... | collective-permute-start | bytes 786440 | tf_op jit(solution)/shard_map/ppermute | solution.py:104
  81.7 4.7 %copy-start.2 = (bf16[1,2048,512]{2,1,0:T(8,128)(2,1)S(1)}, bf16[1,2048,512]{2,1,0:T(8,128)(2,1)}, u32[]{:S(2)}) copy-start(bf16[1,2048,512]{2,1,0:T(8,128)(2,1)} %param.6) | copy-start | bytes 6291460
  81.8 9.8 %collective-permute-start.22 = (bf16[2048,512]{1,0:T(8,128)(2,1)S(1)}, bf16[2048,512]{1,0:T(8,128)(2,1)S(1)}, u32[]{:S(2)}, u32[]{:S(2)}) collective-permute-start(bf16[2048,512]{1,0:T(8,128)(2,1)S(1)} %collective-permute-done.18.refs_1_), channel_id=1, source_target_pairs={{0,4},{1,5},{2,6},{3,7},{4,0},{5,1},{6,2},{7,3},{8,12},{9,13},{10,... | collective-permute-start | bytes 6291464 | tf_op jit(solution)/shard_map/ppermute | solution.py:104
  81.8 4.5 %collective-permute-start.19 = (bf16[128,1024]{1,0:T(8,128)(2,1)S(1)}, bf16[128,1024]{1,0:T(8,128)(2,1)S(1)}, u32[]{:S(2)}, u32[]{:S(2)}) collective-permute-start(bf16[128,1024]{1,0:T(8,128)(2,1)S(1)} %get-tuple-element.53), channel_id=1, source_target_pairs={{0,4},{1,5},{2,6},{3,7},{4,0},{5,1},{6,2},{7,3},{8,12},{9,17},{10,... | collective-permute-start | bytes 786440 | tf_op jit(solution)/shard_map/ppermute | solution.py:104
  82.3 9.2 %collective-permute-start.21 = (bf16[128,1024]{1,0:T(8,128)(2,1)S(1)}, bf16[128,1024]{1,0:T(8,128)(2,1)S(1)}, u32[]{:S(2)}, u32[]{:S(2)}) collective-permute-start(bf16[128,1024]{1,0:T(8,128)(2,1)S(1)} %get-tuple-element.53), channel_id=1, source_target_pairs={{0,4},{1,5},{2,6},{3,7},{4,0},{5,1},{6,2},{7,3},{8,12},{9,18},{10,... | collective-permute-start | bytes 786440 | tf_op jit(solution)/shard_map/ppermute | solution.py:104
  82.4 9.3 %collective-permute-start.23 = (bf16[128,1024]{1,0:T(8,128)(2,1)S(1)}, bf16[128,1024]{1,0:T(8,128)(2,1)S(1)}, u32[]{:S(2)}, u32[]{:S(2)}) collective-permute-start(bf16[128,1024]{1,0:T(8,128)(2,1)S(1)} %get-tuple-element.55), channel_id=1, source_target_pairs={{0,4},{1,5},{2,6},{3,7},{4,0},{5,1},{6,2},{7,3},{8,12},{9,17},{10,... | collective-permute-start | bytes 786440 | tf_op jit(solution)/shard_map/ppermute | solution.py:104
  82.9 8.9 %collective-permute-start.24 = (bf16[128,1024]{1,0:T(8,128)(2,1)S(1)}, bf16[128,1024]{1,0:T(8,128)(2,1)S(1)}, u32[]{:S(2)}, u32[]{:S(2)}) collective-permute-start(bf16[128,1024]{1,0:T(8,128)(2,1)S(1)} %get-tuple-element.55), channel_id=1, source_target_pairs={{0,4},{1,5},{2,6},{3,7},{4,0},{5,1},{6,2},{7,3},{8,12},{9,18},{10,... | collective-permute-start | bytes 786440 | tf_op jit(solution)/shard_map/ppermute | solution.py:104
  86.4 49.2 %collective-permute-start.34 = (bf16[2048,512]{1,0:T(8,128)(2,1)S(1)}, bf16[2048,512]{1,0:T(8,128)(2,1)}, u32[]{:S(2)}, u32[]{:S(2)}) collective-permute-start(bf16[2048,512]{1,0:T(8,128)(2,1)S(1)} %bitcast.20), channel_id=1, source_target_pairs={{0,1},{3,2},{4,5},{7,6},{8,9},{11,10},{12,13},{15,14},{16,17},{19,... | collective-permute-start | bytes 6291464 | tf_op jit(solution)/shard_map/ppermute | solution.py:104
  91.6 1.6 %collective-permute-start.25 = (bf16[128,1024]{1,0:T(8,128)(2,1)S(1)}, bf16[128,1024]{1,0:T(8,128)(2,1)S(1)}, u32[]{:S(2)}, u32[]{:S(2)}) collective-permute-start(bf16[128,1024]{1,0:T(8,128)(2,1)S(1)} %get-tuple-element.63.own_ref), channel_id=1, source_target_pairs={{0,4},{1,5},{2,6},{3,7},{4,0},{5,1},{6,2},{7,3},{8,12},{9,21},{10,... | collective-permute-start | bytes 786440 | tf_op jit(solution)/shard_map/ppermute | solution.py:104
  91.8 2.1 %collective-permute-start.27 = (bf16[128,1024]{1,0:T(8,128)(2,1)S(1)}, bf16[128,1024]{1,0:T(8,128)(2,1)S(1)}, u32[]{:S(2)}, u32[]{:S(2)}) collective-permute-start(bf16[128,1024]{1,0:T(8,128)(2,1)S(1)} %get-tuple-element.66.own_ref), channel_id=1, source_target_pairs={{0,4},{1,5},{2,6},{3,7},{4,0},{5,1},{6,2},{7,3},{8,12},{9,21},{10,... | collective-permute-start | bytes 786440 | tf_op jit(solution)/shard_map/ppermute | solution.py:104
  93.3 2.0 %collective-permute-start.28 = (bf16[128,1024]{1,0:T(8,128)(2,1)S(1)}, bf16[128,1024]{1,0:T(8,128)(2,1)S(1)}, u32[]{:S(2)}, u32[]{:S(2)}) collective-permute-start(bf16[128,1024]{1,0:T(8,128)(2,1)S(1)} %get-tuple-element.65), channel_id=1, source_target_pairs={{0,4},{1,9},{2,10},{3,7},{4,0},{5,1},{6,2},{7,3},{8,12},{9,13},{10... | collective-permute-start | bytes 786440 | tf_op jit(solution)/shard_map/ppermute | solution.py:104
  93.5 1.8 %collective-permute-start.26 = (bf16[128,1024]{1,0:T(8,128)(2,1)S(1)}, bf16[128,1024]{1,0:T(8,128)(2,1)S(1)}, u32[]{:S(2)}, u32[]{:S(2)}) collective-permute-start(bf16[128,1024]{1,0:T(8,128)(2,1)S(1)} %get-tuple-element.65), channel_id=1, source_target_pairs={{0,4},{1,9},{2,10},{3,7},{4,0},{5,1},{6,2},{7,3},{8,12},{9,13},{10... | collective-permute-start | bytes 786440 | tf_op jit(solution)/shard_map/ppermute | solution.py:104
  94.0 1.7 %collective-permute-start.29 = (bf16[128,1024]{1,0:T(8,128)(2,1)S(1)}, bf16[128,1024]{1,0:T(8,128)(2,1)S(1)}, u32[]{:S(2)}, u32[]{:S(2)}) collective-permute-start(bf16[128,1024]{1,0:T(8,128)(2,1)S(1)} %get-tuple-element.68), channel_id=1, source_target_pairs={{0,4},{1,9},{2,10},{3,7},{4,0},{5,1},{6,2},{7,3},{8,12},{9,13},{10... | collective-permute-start | bytes 786440 | tf_op jit(solution)/shard_map/ppermute | solution.py:104
  94.1 1.9 %collective-permute-start.30 = (bf16[128,1024]{1,0:T(8,128)(2,1)S(1)}, bf16[128,1024]{1,0:T(8,128)(2,1)S(1)}, u32[]{:S(2)}, u32[]{:S(2)}) collective-permute-start(bf16[128,1024]{1,0:T(8,128)(2,1)S(1)} %get-tuple-element.68), channel_id=1, source_target_pairs={{0,4},{1,9},{2,10},{3,7},{4,0},{5,1},{6,2},{7,3},{8,12},{9,13},{10... | collective-permute-start | bytes 786440 | tf_op jit(solution)/shard_map/ppermute | solution.py:104
  96.0 1.6 %collective-permute-start.36 = (bf16[128,1024]{1,0:T(8,128)(2,1)S(1)}, bf16[128,1024]{1,0:T(8,128)(2,1)S(1)}, u32[]{:S(2)}, u32[]{:S(2)}) collective-permute-start(bf16[128,1024]{1,0:T(8,128)(2,1)S(1)} %get-tuple-element.75.own_ref), channel_id=1, source_target_pairs={{0,4},{1,29},{2,30},{3,7},{4,0},{5,6},{6,5},{7,3},{8,12},{9,13},{1... | collective-permute-start | bytes 786440 | tf_op jit(solution)/shard_map/ppermute | solution.py:104
  96.2 2.3 %collective-permute-start.31 = (bf16[128,1024]{1,0:T(8,128)(2,1)S(1)}, bf16[128,1024]{1,0:T(8,128)(2,1)S(1)}, u32[]{:S(2)}, u32[]{:S(2)}) collective-permute-start(bf16[128,1024]{1,0:T(8,128)(2,1)S(1)} %get-tuple-element.76.own_ref), channel_id=1, source_target_pairs={{0,4},{1,29},{2,30},{3,7},{4,0},{5,6},{6,5},{7,3},{8,12},{9,13},{1... | collective-permute-start | bytes 786440 | tf_op jit(solution)/shard_map/ppermute | solution.py:104
  98.4 1.5 %collective-permute-start.37 = (bf16[128,1024]{1,0:T(8,128)(2,1)S(1)}, bf16[128,1024]{1,0:T(8,128)(2,1)S(1)}, u32[]{:S(2)}, u32[]{:S(2)}) collective-permute-start(bf16[128,1024]{1,0:T(8,128)(2,1)S(1)} %get-tuple-element.82), channel_id=1, source_target_pairs={{0,4},{1,5},{2,6},{3,7},{4,0},{5,1},{6,2},{7,3},{8,12},{9,13},{10,... | collective-permute-start | bytes 786440 | tf_op jit(solution)/shard_map/ppermute | solution.py:104
  99.2 1.7 %collective-permute-start.32 = (bf16[128,1024]{1,0:T(8,128)(2,1)S(1)}, bf16[128,1024]{1,0:T(8,128)(2,1)}, u32[]{:S(2)}, u32[]{:S(2)}) collective-permute-start(bf16[128,1024]{1,0:T(8,128)(2,1)S(1)} %get-tuple-element.78), channel_id=1, source_target_pairs={{0,4},{1,5},{2,6},{3,7},{4,0},{5,1},{6,2},{7,3},{8,12},{9,13},{10,... | collective-permute-start | bytes 786440 | tf_op jit(solution)/shard_map/ppermute | solution.py:104
  100.0 35.6 %collective-permute-start.38 = (bf16[128,1024]{1,0:T(8,128)(2,1)S(1)}, bf16[128,1024]{1,0:T(8,128)(2,1)S(1)}, u32[]{:S(2)}, u32[]{:S(2)}) collective-permute-start(bf16[128,1024]{1,0:T(8,128)(2,1)S(1)} %get-tuple-element.86.own_ref), channel_id=1, source_target_pairs={{0,4},{1,2},{2,1},{3,7},{4,0},{5,6},{6,5},{7,3},{8,12},{9,10},{10,... | collective-permute-start | bytes 786440 | tf_op jit(solution)/shard_map/ppermute | solution.py:104
  102.0 38.7 %collective-permute-start.33 = (bf16[128,1024]{1,0:T(8,128)(2,1)S(1)}, bf16[128,1024]{1,0:T(8,128)(2,1)S(1)}, u32[]{:S(2)}, u32[]{:S(2)}) collective-permute-start(bf16[128,1024]{1,0:T(8,128)(2,1)S(1)} %get-tuple-element.84.own_ref), channel_id=1, source_target_pairs={{0,4},{1,2},{2,1},{3,7},{4,0},{5,6},{6,5},{7,3},{8,12},{9,10},{10,... | collective-permute-start | bytes 786440 | tf_op jit(solution)/shard_map/ppermute | solution.py:104
  135.7 8.4 %collective-permute-start.39 = (bf16[128,512]{1,0:T(8,128)(2,1)S(1)}, bf16[128,512]{1,0:T(8,128)(2,1)S(1)}, u32[]{:S(2)}, u32[]{:S(2)}) collective-permute-start(bf16[128,512]{1,0:T(8,128)(2,1)S(1)} %slice.58), channel_id=1, source_target_pairs={{0,1},{1,0},{3,2},{2,3},{4,5},{5,4},{7,6},{6,7},{8,9},{9,8},{11,10... | collective-permute-start | bytes 393224 | tf_op jit(solution)/shard_map/ppermute | solution.py:104
  140.7 5.9 %collective-permute-start.35 = (bf16[128,512]{1,0:T(8,128)(2,1)S(1)}, bf16[128,512]{1,0:T(8,128)(2,1)S(1)}, u32[]{:S(2)}, u32[]{:S(2)}) collective-permute-start(bf16[128,512]{1,0:T(8,128)(2,1)S(1)} %slice.56), channel_id=1, source_target_pairs={{0,1},{1,0},{3,2},{2,3},{4,5},{5,4},{7,6},{6,7},{8,9},{9,8},{11,10... | collective-permute-start | bytes 393224 | tf_op jit(solution)/shard_map/ppermute | solution.py:104

commit v6 on v5

--- a/solution.py
+++ b/solution.py
@@ -292,7 +292,9 @@
         others = []
         for part in traces:
             others.append(move(part, places.swap(stage)))
-        traces, seconds = in_turn(list(zip(traces, others)), second_pieces, second_parts, traces[-1], seconds, turn, early)
+        traces, seconds = in_turn(
+            list(zip(traces, others)), second_pieces, second_parts, traces[-1], seconds, turn, early
+        )
         if stage == 0:
             first_early = [move(after(piece, traces[-1]), places.across_cores()) for piece in second_early]
         if stage == min(1, places.columns - 1):
@@ -303,7 +305,8 @@
     outs = []
     for part in range(CHUNKS):
         mine = firsts[part].astype(jnp.float32)
-        opposite = move(seconds[part], places.across_cores()).astype(jnp.float32)
+        opposite = move(seconds[part], places.across_cores())
+        opposite = opposite.astype(jnp.float32)
         contrast = jnp.where(core == 0, mine - opposite, opposite - mine).astype(jnp.bfloat16)
         other = move(contrast, places.swap_all())
         combined, = applied(

time: 149 us -> 149 us (level)
  no operation moved by 1% of the time
where the time goes in v6:
time: 149 us; the launch traced here: 147 us
  waiting for transfers between devices  93.3 us (63%)
  starting transfers between devices  45.3 us (30%)
  other arithmetic  4.17 us (3%)
  Pallas kernels  3.03 us (2%)
    ppermute x40, waiting for transfers between devices, move(): return lax.ppermute(values, AXES, pairs)  93.3 us
    ppermute x40, starting transfers between devices, move(): return lax.ppermute(values, AXES, pairs)  45.3 us
    pallas_call x18, Pallas kernels, applied(): pl.pallas_call(functools.partial(apply_kernel, width, len(pieces), tuple(...  3.03 us
  transfers between devices with their start and end apart: 40, of which 25 were waited for; matrix products, arithmetic and copies ran while one was open for 1% of the time, Pallas kernels for 2%

profile of v6, /device:TPU:0, one launch (start us, length us, event | category | flops | bytes accessed | tf_op | source)
XLA Modules:
  0.0 147.4 jit_solution(7748316234932544987)
XLA Ops:
  0.0 0.8 add_divide_fusion
  0.8 1.1 fusion.4
  1.9 3.1 %collective-permute-start.3 = (bf16[128,512]{1,0:T(8,128)(2,1)S(1)}, bf16[128,512]{1,0:T(8,128)(2,1)S(1)}, u32[]{:S(2)}, u32[]{:S(2)}) collective-permute-start(bf16[128,512]{1,0:T(8,128)(2,1)S(1)} %bitcast.25), channel_id=1, source_target_pairs={{0,1},{1,0},{3,2},{2,3},{4,5},{5,4},{7,6},{6,7},{8,9},{9,8},{11,10... | collective-permute-start | bytes 393224 | tf_op jit(solution)/shard_map/ppermute | solution.py:104
  5.1 3.5 %collective-permute-done.3 = bf16[128,512]{1,0:T(8,128)(2,1)S(1)} collective-permute-done((bf16[128,512]{1,0:T(8,128)(2,1)S(1)}, bf16[128,512]{1,0:T(8,128)(2,1)S(1)}, u32[]{:S(2)}, u32[]{:S(2)}) %collective-permute-start.3) | collective-permute-done | bytes 131104 | tf_op jit(solution)/shard_map/ppermute | solution.py:104
  8.7 3.3 %collective-permute-start = (bf16[128,512]{1,0:T(8,128)(2,1)S(1)}, bf16[128,512]{1,0:T(8,128)(2,1)S(1)}, u32[]{:S(2)}, u32[]{:S(2)}) collective-permute-start(bf16[128,512]{1,0:T(8,128)(2,1)S(1)} %bitcast.23), channel_id=1, source_target_pairs={{0,1},{1,0},{3,2},{2,3},{4,5},{5,4},{7,6},{6,7},{8,9},{9,8},{11,10... | collective-permute-start | bytes 393224 | tf_op jit(solution)/shard_map/ppermute | solution.py:104
  12.0 0.8 collective-permute-start.9
  12.8 1.4 collective-permute-start.8
  14.3 0.7 collective-permute-done
  15.2 1.3 collective-permute-start.5
  16.5 2.2 %collective-permute-done.1 = bf16[128,1024]{1,0:T(8,128)(2,1)S(1)} collective-permute-done((bf16[128,1024]{1,0:T(8,128)(2,1)S(1)}, bf16[128,1024]{1,0:T(8,128)(2,1)S(1)}, u32[]{:S(2)}, u32[]{:S(2)}) %collective-permute-start.1) | collective-permute-done | bytes 262176 | tf_op jit(solution)/shard_map/ppermute | solution.py:104
  18.6 1.3 collective-permute-start.2
  19.9 6.5 %collective-permute-done.5 = bf16[128,1024]{1,0:T(8,128)(2,1)S(1)} collective-permute-done((bf16[128,1024]{1,0:T(8,128)(2,1)S(1)}, bf16[128,1024]{1,0:T(8,128)(2,1)S(1)}, u32[]{:S(2)}, u32[]{:S(2)}) %collective-permute-start.5) | collective-permute-done | bytes 262176 | tf_op jit(solution)/shard_map/ppermute | solution.py:104
  26.4 0.5 shard_map.56
  26.9 4.5 %collective-permute-done.2 = bf16[128,1024]{1,0:T(8,128)(2,1)S(1)} collective-permute-done((bf16[128,1024]{1,0:T(8,128)(2,1)S(1)}, bf16[128,1024]{1,0:T(8,128)(2,1)S(1)}, u32[]{:S(2)}, u32[]{:S(2)}) %collective-permute-start.2) | collective-permute-done | bytes 262176 | tf_op jit(solution)/shard_map/ppermute | solution.py:104
  31.4 0.5 shard_map.55
  32.0 7.7 %collective-permute-done.6 = bf16[256,512]{1,0:T(8,128)(2,1)S(1)} collective-permute-done((bf16[256,512]{1,0:T(8,128)(2,1)S(1)}, bf16[256,512]{1,0:T(8,128)(2,1)S(1)}, u32[]{:S(2)}, u32[]{:S(2)}) %collective-permute-start.6) | collective-permute-done | bytes 262176 | tf_op jit(solution)/shard_map/ppermute | solution.py:104
  39.8 3.2 %collective-permute-start.10 = (bf16[256,1024]{1,0:T(8,128)(2,1)S(1)}, bf16[256,1024]{1,0:T(8,128)(2,1)S(1)}, u32[]{:S(2)}, u32[]{:S(2)}) collective-permute-start(bf16[256,1024]{1,0:T(8,128)(2,1)S(1)} %pad_maximum_fusion), channel_id=1, source_target_pairs={{0,4},{1,5},{2,6},{3,7},{4,0},{5,1},{6,2},{7,3},{8,12},{9,13},{10,... | collective-permute-start | bytes 1572872 | tf_op jit(solution)/shard_map/ppermute | solution.py:104
  43.1 0.5 collective-permute-start.12
  43.6 0.9 collective-permute-done.10
  44.6 0.3 collective-permute-done.7.other_ref
  45.0 0.3 collective-permute-done.12.other_ref
  45.3 0.4 collective-permute-start.14
  45.8 1.1 copy-done
  46.9 11.4 %collective-permute-start.18 = (bf16[2048,512]{1,0:T(8,128)(2,1)S(1)}, bf16[2048,512]{1,0:T(8,128)(2,1)S(1)}, u32[]{:S(2)}, u32[]{:S(2)}) collective-permute-start(bf16[2048,512]{1,0:T(8,128)(2,1)S(1)} %bitcast.11), channel_id=1, source_target_pairs={{0,5},{3,6},{12,9},{15,10},{16,21},{19,22},{28,25},{31,26}} | collective-permute-start | bytes 6291464 | tf_op jit(solution)/shard_map/ppermute | solution.py:104
  58.3 0.5 collective-permute-start.13
  58.9 1.0 collective-permute-done.11.own_ref
  59.9 0.1 collective-permute-start.16
  60.0 0.2 collective-permute-done.13.other_ref
  60.3 0.2 collective-permute-start.17
  60.5 0.1 collective-permute-done.15.own_ref
  60.6 0.8 collective-permute-done.16.other_ref
  61.4 0.2 collective-permute-start.20
  61.6 20.1 %collective-permute-done.18.refs_1_ = bf16[2048,512]{1,0:T(8,128)(2,1)S(1)} collective-permute-done((bf16[2048,512]{1,0:T(8,128)(2,1)S(1)}, bf16[2048,512]{1,0:T(8,128)(2,1)S(1)}, u32[]{:S(2)}, u32[]{:S(2)}) %collective-permute-start.18) | collective-permute-done | bytes 2097184 | tf_op jit(solution)/shard_map/ppermute | solution.py:104
  81.8 0.5 collective-permute-start.19
  82.4 0.4 collective-permute-start.23
  82.9 3.4 %collective-permute-done.19.own_ref = bf16[128,1024]{1,0:T(8,128)(2,1)S(1)} collective-permute-done((bf16[128,1024]{1,0:T(8,128)(2,1)S(1)}, bf16[128,1024]{1,0:T(8,128)(2,1)S(1)}, u32[]{:S(2)}, u32[]{:S(2)}) %collective-permute-start.19) | collective-permute-done | bytes 262176 | tf_op jit(solution)/shard_map/ppermute | solution.py:104
  86.4 5.2 %collective-permute-start.34 = (bf16[2048,512]{1,0:T(8,128)(2,1)S(1)}, bf16[2048,512]{1,0:T(8,128)(2,1)}, u32[]{:S(2)}, u32[]{:S(2)}) collective-permute-start(bf16[2048,512]{1,0:T(8,128)(2,1)S(1)} %bitcast.20), channel_id=1, source_target_pairs={{0,1},{3,2},{4,5},{7,6},{8,9},{11,10},{12,13},{15,14},{16,17},{19,... | collective-permute-start | bytes 6291464 | tf_op jit(solution)/shard_map/ppermute | solution.py:104
  91.6 0.2 collective-permute-start.25
  91.8 0.5 collective-permute-start.27
  92.3 0.9 collective-permute-done.25.other_ref
  93.3 0.2 collective-permute-start.28
  93.5 0.4 collective-permute-start.26
  94.0 0.2 collective-permute-start.29
  94.1 0.4 collective-permute-start.30
  94.5 0.7 collective-permute-done.26.own_ref
  95.3 0.3 collective-permute-done.29.own_ref
  95.6 0.4 collective-permute-done.30.other_ref
  96.0 0.2 collective-permute-start.36
  96.2 0.4 collective-permute-start.31
  96.6 1.0 collective-permute-done.36.other_ref
  97.6 0.7 shard_map.71
  98.5 0.7 shard_map.69
  99.2 0.4 collective-permute-start.32
  99.6 0.3 collective-permute-done.37
  100.0 0.2 collective-permute-start.38
  100.2 0.7 collective-permute-done.32
  100.9 1.1 convert_add_fusion.1
  102.0 0.4 collective-permute-start.33
  102.4 33.2 %collective-permute-done.34.refs_1_ = bf16[2048,512]{1,0:T(8,128)(2,1)} collective-permute-done((bf16[2048,512]{1,0:T(8,128)(2,1)S(1)}, bf16[2048,512]{1,0:T(8,128)(2,1)}, u32[]{:S(2)}, u32[]{:S(2)}) %collective-permute-start.34) | collective-permute-done | bytes 2097184 | tf_op jit(solution)/shard_map/ppermute | solution.py:104
  135.7 4.9 %collective-permute-start.39 = (bf16[128,512]{1,0:T(8,128)(2,1)S(1)}, bf16[128,512]{1,0:T(8,128)(2,1)S(1)}, u32[]{:S(2)}, u32[]{:S(2)}) collective-permute-start(bf16[128,512]{1,0:T(8,128)(2,1)S(1)} %slice.58), channel_id=1, source_target_pairs={{0,1},{1,0},{3,2},{2,3},{4,5},{5,4},{7,6},{6,7},{8,9},{9,8},{11,10... | collective-permute-start | bytes 393224 | tf_op jit(solution)/shard_map/ppermute | solution.py:104
  140.7 2.4 %collective-permute-start.35 = (bf16[128,512]{1,0:T(8,128)(2,1)S(1)}, bf16[128,512]{1,0:T(8,128)(2,1)S(1)}, u32[]{:S(2)}, u32[]{:S(2)}) collective-permute-start(bf16[128,512]{1,0:T(8,128)(2,1)S(1)} %slice.56), channel_id=1, source_target_pairs={{0,1},{1,0},{3,2},{2,3},{4,5},{5,4},{7,6},{6,7},{8,9},{9,8},{11,10... | collective-permute-start | bytes 393224 | tf_op jit(solution)/shard_map/ppermute | solution.py:104
  143.1 1.1 collective-permute-done.39
  144.2 2.4 %collective-permute-done.35 = bf16[128,512]{1,0:T(8,128)(2,1)S(1)} collective-permute-done((bf16[128,512]{1,0:T(8,128)(2,1)S(1)}, bf16[128,512]{1,0:T(8,128)(2,1)S(1)}, u32[]{:S(2)}, u32[]{:S(2)}) %collective-permute-start.35) | collective-permute-done | bytes 131104 | tf_op jit(solution)/shard_map/ppermute | solution.py:104
  146.6 0.7 pad_maximum_fusion.4
  (58 shorter events, 2.0 us)
Async XLA Ops:
  0.0 26.4 %copy-start.1 = (bf16[1,2048,512]{2,1,0:T(8,128)(2,1)S(1)}, bf16[1,2048,512]{2,1,0:T(8,128)(2,1)}, u32[]{:S(2)}) copy-start(bf16[1,2048,512]{2,1,0:T(8,128)(2,1)} %param.7) | copy-start | bytes 6291460
  1.9 6.6 %collective-permute-start.3 = (bf16[128,512]{1,0:T(8,128)(2,1)S(1)}, bf16[128,512]{1,0:T(8,128)(2,1)S(1)}, u32[]{:S(2)}, u32[]{:S(2)}) collective-permute-start(bf16[128,512]{1,0:T(8,128)(2,1)S(1)} %bitcast.25), channel_id=1, source_target_pairs={{0,1},{1,0},{3,2},{2,3},{4,5},{5,4},{7,6},{6,7},{8,9},{9,8},{11,10... | collective-permute-start | bytes 393224 | tf_op jit(solution)/shard_map/ppermute | solution.py:104
  8.7 6.5 %collective-permute-start.4 = (bf16[128,1024]{1,0:T(8,128)(2,1)S(1)}, bf16[128,1024]{1,0:T(8,128)(2,1)S(1)}, u32[]{:S(2)}, u32[]{:S(2)}) collective-permute-start(bf16[128,1024]{1,0:T(8,128)(2,1)S(1)} %get-tuple-element.95), channel_id=1, source_target_pairs={{0,4},{1,2},{2,1},{3,7},{4,0},{5,6},{6,5},{7,3},{8,12},{9,10},{10,... | collective-permute-start | bytes 786440 | tf_op jit(solution)/shard_map/ppermute | solution.py:104
  8.7 6.2 %collective-permute-start = (bf16[128,512]{1,0:T(8,128)(2,1)S(1)}, bf16[128,512]{1,0:T(8,128)(2,1)S(1)}, u32[]{:S(2)}, u32[]{:S(2)}) collective-permute-start(bf16[128,512]{1,0:T(8,128)(2,1)S(1)} %bitcast.23), channel_id=1, source_target_pairs={{0,1},{1,0},{3,2},{2,3},{4,5},{5,4},{7,6},{6,7},{8,9},{9,8},{11,10... | collective-permute-start | bytes 393224 | tf_op jit(solution)/shard_map/ppermute | solution.py:104
  12.0 32.9 %collective-permute-start.9 = (bf16[2048,512]{1,0:T(8,128)(2,1)}, bf16[2048,512]{1,0:T(8,128)(2,1)S(1)}, u32[]{:S(2)}, u32[]{:S(2)}) collective-permute-start(bf16[2048,512]{1,0:T(8,128)(2,1)} %bitcast.9), channel_id=1, source_target_pairs={{4,1},{7,2},{8,13},{11,14},{20,17},{23,18},{24,29},{27,30}} | collective-permute-start | bytes 6291464 | tf_op jit(solution)/shard_map/ppermute | solution.py:104
  12.8 32.1 %collective-permute-start.8 = (bf16[2048,512]{1,0:T(8,128)(2,1)}, bf16[2048,512]{1,0:T(8,128)(2,1)S(1)}, u32[]{:S(2)}, u32[]{:S(2)}) collective-permute-start(bf16[2048,512]{1,0:T(8,128)(2,1)} %bitcast.10), channel_id=1, source_target_pairs={{0,4},{1,5},{2,6},{3,7},{4,0},{5,1},{6,2},{7,3},{8,12},{9,13},{10,... | collective-permute-start | bytes 6291464 | tf_op jit(solution)/shard_map/ppermute | solution.py:104
  15.1 3.5 %collective-permute-start.1 = (bf16[128,1024]{1,0:T(8,128)(2,1)S(1)}, bf16[128,1024]{1,0:T(8,128)(2,1)S(1)}, u32[]{:S(2)}, u32[]{:S(2)}) collective-permute-start(bf16[128,1024]{1,0:T(8,128)(2,1)S(1)} %get-tuple-element.91), channel_id=1, source_target_pairs={{0,4},{1,2},{2,1},{3,7},{4,0},{5,6},{6,5},{7,3},{8,12},{9,10},{10,... | collective-permute-start | bytes 786440 | tf_op jit(solution)/shard_map/ppermute | solution.py:104
  15.2 11.2 %collective-permute-start.5 = (bf16[128,1024]{1,0:T(8,128)(2,1)S(1)}, bf16[128,1024]{1,0:T(8,128)(2,1)S(1)}, u32[]{:S(2)}, u32[]{:S(2)}) collective-permute-start(bf16[128,1024]{1,0:T(8,128)(2,1)S(1)} %collective-permute-done.4), channel_id=1, source_target_pairs={{1,0},{2,3},{5,4},{6,7},{9,8},{10,11},{13,12},{14,15},{17,16},{18,... | collective-permute-start | bytes 786440 | tf_op jit(solution)/shard_map/ppermute | solution.py:104
  18.6 12.7 %collective-permute-start.2 = (bf16[128,1024]{1,0:T(8,128)(2,1)S(1)}, bf16[128,1024]{1,0:T(8,128)(2,1)S(1)}, u32[]{:S(2)}, u32[]{:S(2)}) collective-permute-start(bf16[128,1024]{1,0:T(8,128)(2,1)S(1)} %collective-permute-done.1), channel_id=1, source_target_pairs={{1,0},{2,3},{5,4},{6,7},{9,8},{10,11},{13,12},{14,15},{17,16},{18,... | collective-permute-start | bytes 786440 | tf_op jit(solution)/shard_map/ppermute | solution.py:104
  31.9 7.8 %collective-permute-start.6 = (bf16[256,512]{1,0:T(8,128)(2,1)S(1)}, bf16[256,512]{1,0:T(8,128)(2,1)S(1)}, u32[]{:S(2)}, u32[]{:S(2)}) collective-permute-start(bf16[256,512]{1,0:T(8,128)(2,1)S(1)} %pad_maximum_fusion.3), channel_id=1, source_target_pairs={{0,1},{1,0},{3,2},{2,3},{4,5},{5,4},{7,6},{6,7},{8,9},{9,8},{11,10... | collective-permute-start | bytes 786440 | tf_op jit(solution)/shard_map/ppermute | solution.py:104
  39.8 4.8 %collective-permute-start.10 = (bf16[256,1024]{1,0:T(8,128)(2,1)S(1)}, bf16[256,1024]{1,0:T(8,128)(2,1)S(1)}, u32[]{:S(2)}, u32[]{:S(2)}) collective-permute-start(bf16[256,1024]{1,0:T(8,128)(2,1)S(1)} %pad_maximum_fusion), channel_id=1, source_target_pairs={{0,4},{1,5},{2,6},{3,7},{4,0},{5,1},{6,2},{7,3},{8,12},{9,13},{10,... | collective-permute-start | bytes 1572872 | tf_op jit(solution)/shard_map/ppermute | solution.py:104
  43.0 1.9 %collective-permute-start.7 = (bf16[128,1024]{1,0:T(8,128)(2,1)S(1)}, bf16[128,1024]{1,0:T(8,128)(2,1)S(1)}, u32[]{:S(2)}, u32[]{:S(2)}) collective-permute-start(bf16[128,1024]{1,0:T(8,128)(2,1)S(1)} %get-tuple-element.89.refs_2_.refs_3_), channel_id=1, source_target_pairs={{0,4},{1,2},{2,1},{3,7},{4,0},{5,25},{6,26},{7,3},{8,12},{9,13},{1... | collective-permute-start | bytes 786440 | tf_op jit(solution)/shard_map/ppermute | solution.py:104
  43.1 2.2 %collective-permute-start.12 = (bf16[128,1024]{1,0:T(8,128)(2,1)S(1)}, bf16[128,1024]{1,0:T(8,128)(2,1)S(1)}, u32[]{:S(2)}, u32[]{:S(2)}) collective-permute-start(bf16[128,1024]{1,0:T(8,128)(2,1)S(1)} %get-tuple-element.45.own_ref.refs_2_.refs_3_), channel_id=1, source_target_pairs={{0,4},{1,2},{2,1},{3,7},{4,0},{5,25},{6,26},{7,3},{8,12},{9,13},{1... | collective-permute-start | bytes 786440 | tf_op jit(solution)/shard_map/ppermute | solution.py:104
  45.3 1.6 %copy-start = (bf16[1,2048,512]{2,1,0:T(8,128)(2,1)S(1)}, bf16[1,2048,512]{2,1,0:T(8,128)(2,1)}, u32[]{:S(2)}) copy-start(bf16[1,2048,512]{2,1,0:T(8,128)(2,1)} %param.5) | copy-start | bytes 6291460
  45.3 14.9 %collective-permute-start.14 = (bf16[2048,512]{1,0:T(8,128)(2,1)S(1)}, bf16[2048,512]{1,0:T(8,128)(2,1)S(1)}, u32[]{:S(2)}, u32[]{:S(2)}) collective-permute-start(bf16[2048,512]{1,0:T(8,128)(2,1)S(1)} %collective-permute-done.9.refs_1_), channel_id=1, source_target_pairs={{0,4},{1,5},{2,6},{3,7},{4,0},{5,1},{6,2},{7,3},{8,12},{9,13},{10,... | collective-permute-start | bytes 6291464 | tf_op jit(solution)/shard_map/ppermute | solution.py:104
  46.9 34.8 %collective-permute-start.18 = (bf16[2048,512]{1,0:T(8,128)(2,1)S(1)}, bf16[2048,512]{1,0:T(8,128)(2,1)S(1)}, u32[]{:S(2)}, u32[]{:S(2)}) collective-permute-start(bf16[2048,512]{1,0:T(8,128)(2,1)S(1)} %bitcast.11), channel_id=1, source_target_pairs={{0,5},{3,6},{12,9},{15,10},{16,21},{19,22},{28,25},{31,26}} | collective-permute-start | bytes 6291464 | tf_op jit(solution)/shard_map/ppermute | solution.py:104
  58.3 1.6 %collective-permute-start.11 = (bf16[128,1024]{1,0:T(8,128)(2,1)S(1)}, bf16[128,1024]{1,0:T(8,128)(2,1)S(1)}, u32[]{:S(2)}, u32[]{:S(2)}) collective-permute-start(bf16[128,1024]{1,0:T(8,128)(2,1)S(1)} %shard_map.57.refs_3_), channel_id=1, source_target_pairs={{0,4},{1,9},{2,10},{3,7},{4,0},{5,1},{6,2},{7,3},{8,12},{9,13},{10... | collective-permute-start | bytes 786440 | tf_op jit(solution)/shard_map/ppermute | solution.py:104
  58.3 1.9 %collective-permute-start.13 = (bf16[128,1024]{1,0:T(8,128)(2,1)S(1)}, bf16[128,1024]{1,0:T(8,128)(2,1)S(1)}, u32[]{:S(2)}, u32[]{:S(2)}) collective-permute-start(bf16[128,1024]{1,0:T(8,128)(2,1)S(1)} %shard_map.57.refs_3_), channel_id=1, source_target_pairs={{0,4},{1,10},{2,9},{3,7},{4,0},{5,1},{6,2},{7,3},{8,12},{9,13},{10... | collective-permute-start | bytes 786440 | tf_op jit(solution)/shard_map/ppermute | solution.py:104
  58.8 1.8 %collective-permute-start.15 = (bf16[128,1024]{1,0:T(8,128)(2,1)S(1)}, bf16[128,1024]{1,0:T(8,128)(2,1)S(1)}, u32[]{:S(2)}, u32[]{:S(2)}) collective-permute-start(bf16[128,1024]{1,0:T(8,128)(2,1)S(1)} %shard_map.58.refs_3_), channel_id=1, source_target_pairs={{0,4},{1,9},{2,10},{3,7},{4,0},{5,1},{6,2},{7,3},{8,12},{9,13},{10... | collective-permute-start | bytes 786440 | tf_op jit(solution)/shard_map/ppermute | solution.py:104
  59.9 1.5 %collective-permute-start.16 = (bf16[128,1024]{1,0:T(8,128)(2,1)S(1)}, bf16[128,1024]{1,0:T(8,128)(2,1)S(1)}, u32[]{:S(2)}, u32[]{:S(2)}) collective-permute-start(bf16[128,1024]{1,0:T(8,128)(2,1)S(1)} %shard_map.58.refs_3_), channel_id=1, source_target_pairs={{0,4},{1,10},{2,9},{3,7},{4,0},{5,1},{6,2},{7,3},{8,12},{9,13},{10... | collective-permute-start | bytes 786440 | tf_op jit(solution)/shard_map/ppermute | solution.py:104
  60.3 21.4 %collective-permute-start.17 = (bf16[128,1024]{1,0:T(8,128)(2,1)S(1)}, bf16[128,1024]{1,0:T(8,128)(2,1)S(1)}, u32[]{:S(2)}, u32[]{:S(2)}) collective-permute-start(bf16[128,1024]{1,0:T(8,128)(2,1)S(1)} %get-tuple-element.51.own_ref), channel_id=1, source_target_pairs={{0,4},{1,5},{2,6},{3,7},{4,0},{5,1},{6,2},{7,3},{8,12},{9,10},{10,... | collective-permute-start | bytes 786440 | tf_op jit(solution)/shard_map/ppermute | solution.py:104
  61.4 20.3 %collective-permute-start.20 = (bf16[128,1024]{1,0:T(8,128)(2,1)S(1)}, bf16[128,1024]{1,0:T(8,128)(2,1)S(1)}, u32[]{:S(2)}, u32[]{:S(2)}) collective-permute-start(bf16[128,1024]{1,0:T(8,128)(2,1)S(1)} %get-tuple-element.54.own_ref), channel_id=1, source_target_pairs={{0,4},{1,5},{2,6},{3,7},{4,0},{5,1},{6,2},{7,3},{8,12},{9,10},{10,... | collective-permute-start | bytes 786440 | tf_op jit(solution)/shard_map/ppermute | solution.py:104
  81.7 4.7 %copy-start.2 = (bf16[1,2048,512]{2,1,0:T(8,128)(2,1)S(1)}, bf16[1,2048,512]{2,1,0:T(8,128)(2,1)}, u32[]{:S(2)}) copy-start(bf16[1,2048,512]{2,1,0:T(8,128)(2,1)} %param.6) | copy-start | bytes 6291460
  81.8 9.8 %collective-permute-start.22 = (bf16[2048,512]{1,0:T(8,128)(2,1)S(1)}, bf16[2048,512]{1,0:T(8,128)(2,1)S(1)}, u32[]{:S(2)}, u32[]{:S(2)}) collective-permute-start(bf16[2048,512]{1,0:T(8,128)(2,1)S(1)} %collective-permute-done.18.refs_1_), channel_id=1, source_target_pairs={{0,4},{1,5},{2,6},{3,7},{4,0},{5,1},{6,2},{7,3},{8,12},{9,13},{10,... | collective-permute-start | bytes 6291464 | tf_op jit(solution)/shard_map/ppermute | solution.py:104
  81.8 4.5 %collective-permute-start.19 = (bf16[128,1024]{1,0:T(8,128)(2,1)S(1)}, bf16[128,1024]{1,0:T(8,128)(2,1)S(1)}, u32[]{:S(2)}, u32[]{:S(2)}) collective-permute-start(bf16[128,1024]{1,0:T(8,128)(2,1)S(1)} %get-tuple-element.53), channel_id=1, source_target_pairs={{0,4},{1,5},{2,6},{3,7},{4,0},{5,1},{6,2},{7,3},{8,12},{9,17},{10,... | collective-permute-start | bytes 786440 | tf_op jit(solution)/shard_map/ppermute | solution.py:104
  82.3 9.2 %collective-permute-start.21 = (bf16[128,1024]{1,0:T(8,128)(2,1)S(1)}, bf16[128,1024]{1,0:T(8,128)(2,1)S(1)}, u32[]{:S(2)}, u32[]{:S(2)}) collective-permute-start(bf16[128,1024]{1,0:T(8,128)(2,1)S(1)} %get-tuple-element.53), channel_id=1, source_target_pairs={{0,4},{1,5},{2,6},{3,7},{4,0},{5,1},{6,2},{7,3},{8,12},{9,18},{10,... | collective-permute-start | bytes 786440 | tf_op jit(solution)/shard_map/ppermute | solution.py:104
  82.4 9.3 %collective-permute-start.23 = (bf16[128,1024]{1,0:T(8,128)(2,1)S(1)}, bf16[128,1024]{1,0:T(8,128)(2,1)S(1)}, u32[]{:S(2)}, u32[]{:S(2)}) collective-permute-start(bf16[128,1024]{1,0:T(8,128)(2,1)S(1)} %get-tuple-element.55), channel_id=1, source_target_pairs={{0,4},{1,5},{2,6},{3,7},{4,0},{5,1},{6,2},{7,3},{8,12},{9,17},{10,... | collective-permute-start | bytes 786440 | tf_op jit(solution)/shard_map/ppermute | solution.py:104
  82.9 8.9 %collective-permute-start.24 = (bf16[128,1024]{1,0:T(8,128)(2,1)S(1)}, bf16[128,1024]{1,0:T(8,128)(2,1)S(1)}, u32[]{:S(2)}, u32[]{:S(2)}) collective-permute-start(bf16[128,1024]{1,0:T(8,128)(2,1)S(1)} %get-tuple-element.55), channel_id=1, source_target_pairs={{0,4},{1,5},{2,6},{3,7},{4,0},{5,1},{6,2},{7,3},{8,12},{9,18},{10,... | collective-permute-start | bytes 786440 | tf_op jit(solution)/shard_map/ppermute | solution.py:104
  86.4 49.2 %collective-permute-start.34 = (bf16[2048,512]{1,0:T(8,128)(2,1)S(1)}, bf16[2048,512]{1,0:T(8,128)(2,1)}, u32[]{:S(2)}, u32[]{:S(2)}) collective-permute-start(bf16[2048,512]{1,0:T(8,128)(2,1)S(1)} %bitcast.20), channel_id=1, source_target_pairs={{0,1},{3,2},{4,5},{7,6},{8,9},{11,10},{12,13},{15,14},{16,17},{19,... | collective-permute-start | bytes 6291464 | tf_op jit(solution)/shard_map/ppermute | solution.py:104
  91.6 1.6 %collective-permute-start.25 = (bf16[128,1024]{1,0:T(8,128)(2,1)S(1)}, bf16[128,1024]{1,0:T(8,128)(2,1)S(1)}, u32[]{:S(2)}, u32[]{:S(2)}) collective-permute-start(bf16[128,1024]{1,0:T(8,128)(2,1)S(1)} %get-tuple-element.63.own_ref), channel_id=1, source_target_pairs={{0,4},{1,5},{2,6},{3,7},{4,0},{5,1},{6,2},{7,3},{8,12},{9,21},{10,... | collective-permute-start | bytes 786440 | tf_op jit(solution)/shard_map/ppermute | solution.py:104
  91.8 2.1 %collective-permute-start.27 = (bf16[128,1024]{1,0:T(8,128)(2,1)S(1)}, bf16[128,1024]{1,0:T(8,128)(2,1)S(1)}, u32[]{:S(2)}, u32[]{:S(2)}) collective-permute-start(bf16[128,1024]{1,0:T(8,128)(2,1)S(1)} %get-tuple-element.66.own_ref), channel_id=1, source_target_pairs={{0,4},{1,5},{2,6},{3,7},{4,0},{5,1},{6,2},{7,3},{8,12},{9,21},{10,... | collective-permute-start | bytes 786440 | tf_op jit(solution)/shard_map/ppermute | solution.py:104
  93.3 2.0 %collective-permute-start.28 = (bf16[128,1024]{1,0:T(8,128)(2,1)S(1)}, bf16[128,1024]{1,0:T(8,128)(2,1)S(1)}, u32[]{:S(2)}, u32[]{:S(2)}) collective-permute-start(bf16[128,1024]{1,0:T(8,128)(2,1)S(1)} %get-tuple-element.65), channel_id=1, source_target_pairs={{0,4},{1,9},{2,10},{3,7},{4,0},{5,1},{6,2},{7,3},{8,12},{9,13},{10... | collective-permute-start | bytes 786440 | tf_op jit(solution)/shard_map/ppermute | solution.py:104
  93.5 1.8 %collective-permute-start.26 = (bf16[128,1024]{1,0:T(8,128)(2,1)S(1)}, bf16[128,1024]{1,0:T(8,128)(2,1)S(1)}, u32[]{:S(2)}, u32[]{:S(2)}) collective-permute-start(bf16[128,1024]{1,0:T(8,128)(2,1)S(1)} %get-tuple-element.65), channel_id=1, source_target_pairs={{0,4},{1,9},{2,10},{3,7},{4,0},{5,1},{6,2},{7,3},{8,12},{9,13},{10... | collective-permute-start | bytes 786440 | tf_op jit(solution)/shard_map/ppermute | solution.py:104
  94.0 1.7 %collective-permute-start.29 = (bf16[128,1024]{1,0:T(8,128)(2,1)S(1)}, bf16[128,1024]{1,0:T(8,128)(2,1)S(1)}, u32[]{:S(2)}, u32[]{:S(2)}) collective-permute-start(bf16[128,1024]{1,0:T(8,128)(2,1)S(1)} %get-tuple-element.68), channel_id=1, source_target_pairs={{0,4},{1,9},{2,10},{3,7},{4,0},{5,1},{6,2},{7,3},{8,12},{9,13},{10... | collective-permute-start | bytes 786440 | tf_op jit(solution)/shard_map/ppermute | solution.py:104
  94.1 1.9 %collective-permute-start.30 = (bf16[128,1024]{1,0:T(8,128)(2,1)S(1)}, bf16[128,1024]{1,0:T(8,128)(2,1)S(1)}, u32[]{:S(2)}, u32[]{:S(2)}) collective-permute-start(bf16[128,1024]{1,0:T(8,128)(2,1)S(1)} %get-tuple-element.68), channel_id=1, source_target_pairs={{0,4},{1,9},{2,10},{3,7},{4,0},{5,1},{6,2},{7,3},{8,12},{9,13},{10... | collective-permute-start | bytes 786440 | tf_op jit(solution)/shard_map/ppermute | solution.py:104
  96.0 1.6 %collective-permute-start.36 = (bf16[128,1024]{1,0:T(8,128)(2,1)S(1)}, bf16[128,1024]{1,0:T(8,128)(2,1)S(1)}, u32[]{:S(2)}, u32[]{:S(2)}) collective-permute-start(bf16[128,1024]{1,0:T(8,128)(2,1)S(1)} %get-tuple-element.75.own_ref), channel_id=1, source_target_pairs={{0,4},{1,29},{2,30},{3,7},{4,0},{5,6},{6,5},{7,3},{8,12},{9,13},{1... | collective-permute-start | bytes 786440 | tf_op jit(solution)/shard_map/ppermute | solution.py:104
  96.2 2.3 %collective-permute-start.31 = (bf16[128,1024]{1,0:T(8,128)(2,1)S(1)}, bf16[128,1024]{1,0:T(8,128)(2,1)S(1)}, u32[]{:S(2)}, u32[]{:S(2)}) collective-permute-start(bf16[128,1024]{1,0:T(8,128)(2,1)S(1)} %get-tuple-element.76.own_ref), channel_id=1, source_target_pairs={{0,4},{1,29},{2,30},{3,7},{4,0},{5,6},{6,5},{7,3},{8,12},{9,13},{1... | collective-permute-start | bytes 786440 | tf_op jit(solution)/shard_map/ppermute | solution.py:104
  98.4 1.5 %collective-permute-start.37 = (bf16[128,1024]{1,0:T(8,128)(2,1)S(1)}, bf16[128,1024]{1,0:T(8,128)(2,1)S(1)}, u32[]{:S(2)}, u32[]{:S(2)}) collective-permute-start(bf16[128,1024]{1,0:T(8,128)(2,1)S(1)} %get-tuple-element.82), channel_id=1, source_target_pairs={{0,4},{1,5},{2,6},{3,7},{4,0},{5,1},{6,2},{7,3},{8,12},{9,13},{10,... | collective-permute-start | bytes 786440 | tf_op jit(solution)/shard_map/ppermute | solution.py:104
  99.2 1.7 %collective-permute-start.32 = (bf16[128,1024]{1,0:T(8,128)(2,1)S(1)}, bf16[128,1024]{1,0:T(8,128)(2,1)}, u32[]{:S(2)}, u32[]{:S(2)}) collective-permute-start(bf16[128,1024]{1,0:T(8,128)(2,1)S(1)} %get-tuple-element.78), channel_id=1, source_target_pairs={{0,4},{1,5},{2,6},{3,7},{4,0},{5,1},{6,2},{7,3},{8,12},{9,13},{10,... | collective-permute-start | bytes 786440 | tf_op jit(solution)/shard_map/ppermute | solution.py:104
  100.0 35.6 %collective-permute-start.38 = (bf16[128,1024]{1,0:T(8,128)(2,1)S(1)}, bf16[128,1024]{1,0:T(8,128)(2,1)S(1)}, u32[]{:S(2)}, u32[]{:S(2)}) collective-permute-start(bf16[128,1024]{1,0:T(8,128)(2,1)S(1)} %get-tuple-element.86.own_ref), channel_id=1, source_target_pairs={{0,4},{1,2},{2,1},{3,7},{4,0},{5,6},{6,5},{7,3},{8,12},{9,10},{10,... | collective-permute-start | bytes 786440 | tf_op jit(solution)/shard_map/ppermute | solution.py:104
  102.0 38.7 %collective-permute-start.33 = (bf16[128,1024]{1,0:T(8,128)(2,1)S(1)}, bf16[128,1024]{1,0:T(8,128)(2,1)S(1)}, u32[]{:S(2)}, u32[]{:S(2)}) collective-permute-start(bf16[128,1024]{1,0:T(8,128)(2,1)S(1)} %get-tuple-element.84.own_ref), channel_id=1, source_target_pairs={{0,4},{1,2},{2,1},{3,7},{4,0},{5,6},{6,5},{7,3},{8,12},{9,10},{10,... | collective-permute-start | bytes 786440 | tf_op jit(solution)/shard_map/ppermute | solution.py:104
  135.7 8.4 %collective-permute-start.39 = (bf16[128,512]{1,0:T(8,128)(2,1)S(1)}, bf16[128,512]{1,0:T(8,128)(2,1)S(1)}, u32[]{:S(2)}, u32[]{:S(2)}) collective-permute-start(bf16[128,512]{1,0:T(8,128)(2,1)S(1)} %slice.58), channel_id=1, source_target_pairs={{0,1},{1,0},{3,2},{2,3},{4,5},{5,4},{7,6},{6,7},{8,9},{9,8},{11,10... | collective-permute-start | bytes 393224 | tf_op jit(solution)/shard_map/ppermute | solution.py:104
  140.7 5.9 %collective-permute-start.35 = (bf16[128,512]{1,0:T(8,128)(2,1)S(1)}, bf16[128,512]{1,0:T(8,128)(2,1)S(1)}, u32[]{:S(2)}, u32[]{:S(2)}) collective-permute-start(bf16[128,512]{1,0:T(8,128)(2,1)S(1)} %slice.56), channel_id=1, source_target_pairs={{0,1},{1,0},{3,2},{2,3},{4,5},{5,4},{7,6},{6,7},{8,9},{9,8},{11,10... | collective-permute-start | bytes 393224 | tf_op jit(solution)/shard_map/ppermute | solution.py:104
